TPU v7x, 128 devices: a whole 4x4x4 slice. The times are simulated.
128 devices in a mesh: blk: 16 (over y_lo, x, core), group: 8 (over z, y_hi).
Axes of the slice: x: 4, y: 4 (y_hi: 2, y_lo: 2; y = y_hi * 2 + y_lo), z: 4, core: 2. Of those that a mesh axis runs over, the one named last changes fastest.
Arguments:
- image_embed: bfloat16 [8192, 1152], P(('blk', 'group')), may hold values from -6 to 6
- caption_vectors: bfloat16 [65536, 1152], P(('blk', 'group')), may hold values from -6 to 6
- caption_counts: int32 [8192], replicated, may hold values from 1 to 8, as said below
- natural_log_multiplier: float32 [1], replicated, may hold values from 1.5 to 2.5
- match_odds_offset: float32 [1], replicated, may hold values from -6 to -4
Outputs:
- image_grad: float32 [8192, 1152], P(('blk', 'group'))
- caption_grad: float32 [65536, 1152], P(('blk', 'group'))
Inputs may be any that keep to these rules, and one draw needn't show every extreme that they name: Images are numbered as in caption_counts, 64 to a device, devices in the order of blk then group. Local image k of the device with blk index b < 8 and group index g and local image k of the device with blk index b + 8 and group index g have counts that sum to 9. On at least one device all 64 images have 8 captions.
All inputs are finite; a program needn't handle non-finite values.
Results may differ from a plain program's by a relative error of at most 0.0028.
Values may be sent and summed in bfloat16 or wider, within the bound.
No kernel may reach another device: no remote copies, remote signals or barrier semaphores. Data moves between devices by JAX's collectives and lax.ppermute only.
A program may use at most 64 MiB of HBM per device.

v0:
```python
import functools

import jax
import jax.numpy as jnp
from jax import lax
from jax.experimental import pallas as pl
from jax.experimental.pallas import tpu as pltpu
from jax.sharding import Mesh, PartitionSpec as P


EPSILON = 1e-06
LOG2E = 1.4426950408889634
AXES = ("y_lo", "x", "core", "z", "y_hi")
SIZES = (2, 4, 2, 4, 2)
F32 = jnp.float32
BF16 = jnp.bfloat16
VMEM = pl.BlockSpec(memory_space=pltpu.VMEM)
ANY = pl.BlockSpec(memory_space=pl.ANY)
SMEM = pl.BlockSpec(memory_space=pltpu.SMEM)
MIB = 2**20


def coordinates(device):
    out = []
    for size in reversed(SIZES):
        out.append(device % size)
        device //= size
    return out[::-1]


def flat(coords):
    device = 0
    for size, c in zip(SIZES, coords):
        device = device * size + c
    return device


def route(move):
    pairs = []
    for device in range(128):
        c = coordinates(device)
        move(c)
        pairs.append((device, flat(c)))
    return pairs


def ring_route(stage, distance):
    def move(c):
        axis = 1 if c[2] == stage else 3
        c[axis] = (c[axis] + distance) % 4

    return route(move)


def flip_route(axis):
    def move(c):
        c[axis] = 1 - c[axis]

    return route(move)


def send(value, pairs):
    return lax.ppermute(value, AXES, pairs)


def unit_rows(raw):
    values = raw.astype(F32)
    inverse = lax.rsqrt(jnp.sum(values * values, axis=1, keepdims=True) + EPSILON)
    return values * inverse, inverse


def near_kernel(own_ref, far_ref, near_ref):
    count = own_ref.shape[0]
    near_ref[:count] = unit_rows(own_ref[...])[0].astype(BF16)
    near_ref[count:] = unit_rows(far_ref[...])[0].astype(BF16)


def join_kernel(*refs):
    rows = refs[0].shape[0]
    refs[-2][:rows] = refs[0][...]
    refs[-2][rows:] = refs[1][...]
    refs[-1][:rows] = refs[2][...]
    refs[-1][rows:] = refs[3][...]


def plain(kernel, out_shape, args, flops=10**6, smem=0, limit=16, after=()):
    return pl.pallas_call(
        lambda *refs: kernel(*refs[: len(args)], *refs[len(args) + len(after) :]),
        out_shape=out_shape,
        in_specs=[SMEM] * smem + [VMEM] * (len(args) - smem) + [ANY] * len(after),
        out_specs=(VMEM,) * len(out_shape) if isinstance(out_shape, tuple) else VMEM,
        compiler_params=pltpu.CompilerParams(vmem_limit_bytes=limit * MIB),
        cost_estimate=pl.CostEstimate(flops=flops, bytes_accessed=MIB, transcendentals=0),
    )(*args, *after)


def prep_kernel(total_ref, own_ref, early_ref, late_ref):
    slots = own_ref.shape[0]
    early = early_ref.shape[0]
    low = unit_rows(own_ref[...])[0]
    slot = lax.broadcasted_iota(jnp.int32, low.shape, 0)
    low = jnp.where(slot < total_ref[0], low, 0.0).astype(BF16)
    early_ref[...] = low[:early]
    late_ref[: slots - early] = low[early:]
    late_ref[slots - early :] = jnp.zeros((late_ref.shape[0] - slots + early, low.shape[1]), BF16)


def picked(rows, columns, offset, values):
    row = lax.broadcasted_iota(jnp.int32, (rows, columns), 0)
    column = lax.broadcasted_iota(jnp.int32, (rows, columns), 1)
    pick = jnp.where(column == row + offset, 1.0, 0.0).astype(BF16)
    return jnp.dot(pick, values, preferred_element_type=F32)


def merge_kernel(start, parts, total_ref, own_ref, *refs):
    out_ref = refs[-1]
    rows = out_ref.shape[0]
    merged = own_ref[...].astype(F32)
    for number in range(parts):
        raw = refs[number][...]
        low = unit_rows(raw)[0].astype(BF16)
        offset = start - number * raw.shape[0] - total_ref[0]
        merged = merged + picked(rows, raw.shape[0], offset, low)
    out_ref[...] = merged.astype(BF16)


def stack(own_ref, other_ref, out_ref):
    rows = own_ref.shape[0]
    out_ref[:256] = own_ref[:256]
    out_ref[256:512] = other_ref[:256]
    if rows > 256:
        out_ref[512 : rows + 256] = own_ref[256:]
        out_ref[rows + 256 :] = other_ref[256:]


def weigh(local, start, scalar_ref, spans_ref, images, captions, weight_ref):
    scale = scalar_ref[0]
    bias = scalar_ref[1]
    scores = lax.dot_general(
        images, captions, (((1,), (1,)), ((), ())), preferred_element_type=F32
    )
    steep = scores * (scale * -LOG2E) + (bias * -LOG2E)
    weight_ref[...] = (scale / (1.0 + jnp.exp2(steep))).astype(BF16)
    if local:
        count = spans_ref.shape[0]
        head = steep[:count]
        column = lax.broadcasted_iota(jnp.int32, head.shape, 1)
        rest = (column >= 512) & (column < 576)
        position = jnp.where(column < 256, column, jnp.where(rest, column - 256, -1 - start)) + start
        match = (position >= spans_ref[:, 0:1]) & (position < spans_ref[:, 1:2])
        value = scale / (1.0 + jnp.exp2(jnp.where(match, -head, head)))
        weight_ref[:count] = jnp.where(match, -value, value).astype(BF16)


def early_kernel(
    local, scalar_ref, spans_ref, head_ref, tail_ref, own_ref, other_ref, *refs
):
    weight_ref, images_ref, sums_ref, captions_ref = refs[-4:]
    rows = head_ref.shape[0]
    images_ref[:rows] = head_ref[...]
    images_ref[rows:] = tail_ref[...]
    stack(own_ref, other_ref, captions_ref)
    weigh(local, 0, scalar_ref, spans_ref, images_ref[...], captions_ref[...], weight_ref)
    sums_ref[...] = jnp.dot(weight_ref[...], captions_ref[...], preferred_element_type=F32)


def late_kernel(
    local, start, scalar_ref, spans_ref, images_ref, sums_ref, own_ref, other_ref, *refs
):
    weight_ref, head_out, tail_out, captions_ref = refs[-4:]
    rows = head_out.shape[0]
    stack(own_ref, other_ref, captions_ref)
    weigh(local, start, scalar_ref, spans_ref, images_ref[...], captions_ref[...], weight_ref)
    sums = sums_ref[...] + jnp.dot(
        weight_ref[...], captions_ref[...], preferred_element_type=F32
    )
    head_out[...] = sums[:rows].astype(head_out.dtype)
    tail_out[...] = sums[rows:].astype(tail_out.dtype)


def early_terms(local, scalars, spans, head, tail, own, other, after=()):
    rows, width = head.shape
    slots = 2 * own.shape[0]
    return pl.pallas_call(
        lambda *refs: early_kernel(local, *refs),
        out_shape=(
            jax.ShapeDtypeStruct((2 * rows, slots), BF16),
            jax.ShapeDtypeStruct((2 * rows, width), BF16),
            jax.ShapeDtypeStruct((2 * rows, width), F32),
        ),
        in_specs=[SMEM, VMEM, VMEM, VMEM, VMEM, VMEM] + [ANY] * len(after),
        out_specs=(VMEM,) * 3,
        scratch_shapes=[pltpu.VMEM((slots, width), BF16)],
        compiler_params=pltpu.CompilerParams(vmem_limit_bytes=20 * MIB),
        cost_estimate=pl.CostEstimate(
            flops=8 * rows * slots * width, bytes_accessed=8 * MIB, transcendentals=2 * rows * slots
        ),
        name="early_local" if local else "early_remote",
    )(scalars, spans, head, tail, own, other, *after)


def late_terms(local, start, scalars, spans, images, sums, own, other, types, after=()):
    rows, width = images.shape
    slots = 2 * own.shape[0]
    return pl.pallas_call(
        lambda *refs: late_kernel(local, start, *refs),
        out_shape=(
            jax.ShapeDtypeStruct((rows, slots), BF16),
            jax.ShapeDtypeStruct((rows // 2, width), types[0]),
            jax.ShapeDtypeStruct((rows // 2, width), types[1]),
        ),
        in_specs=[SMEM, VMEM, VMEM, VMEM, VMEM, VMEM] + [ANY] * len(after),
        out_specs=(VMEM,) * 3,
        scratch_shapes=[pltpu.VMEM((slots, width), BF16)],
        compiler_params=pltpu.CompilerParams(vmem_limit_bytes=20 * MIB),
        cost_estimate=pl.CostEstimate(
            flops=4 * rows * slots * width, bytes_accessed=8 * MIB, transcendentals=rows * slots
        ),
        name="late_local" if local else "late_remote",
    )(scalars, spans, images, sums, own, other, *after)


def caption_kernel(blocks, *refs):
    own_ref, cross_ref = refs[-2:]
    rows = own_ref.shape[0]
    total = None
    for weight_ref, images_ref in zip(refs[:blocks], refs[blocks : 2 * blocks]):
        part = lax.dot_general(
            weight_ref[...], images_ref[...], (((0,), (0,)), ((), ())), preferred_element_type=F32
        )
        total = part if total is None else total + part
    own_ref[:256] = total[:256]
    cross_ref[:256] = total[256:512].astype(BF16)
    if rows > 256:
        own_ref[256:] = total[512 : rows + 256]
        cross_ref[256:] = total[rows + 256 :].astype(BF16)


def caption_terms(weights, images, after=()):
    slots = weights[0].shape[1]
    width = images[0].shape[1]
    rows = sum(i.shape[0] for i in images)
    return pl.pallas_call(
        lambda *refs: caption_kernel(len(weights), *refs),
        out_shape=(
            jax.ShapeDtypeStruct((slots // 2, width), F32),
            jax.ShapeDtypeStruct((slots // 2, width), BF16),
        ),
        in_specs=[VMEM] * (2 * len(weights)) + [ANY] * len(after),
        out_specs=(VMEM, VMEM),
        compiler_params=pltpu.CompilerParams(vmem_limit_bytes=24 * MIB),
        cost_estimate=pl.CostEstimate(
            flops=2 * rows * slots * width, bytes_accessed=8 * MIB, transcendentals=0
        ),
        name="caption_terms",
    )(*weights, *images, *after)


def pair_kernel(skip, own_ref, cross_ref, pair_ref, back_ref):
    pair = own_ref[...] + cross_ref[...].astype(F32)
    pair_ref[...] = pair
    back_ref[...] = pair[skip:].astype(BF16)


def home_kernel(total_ref, early_ref, late_ref, back_ref, out_ref):
    slots = out_ref.shape[0]
    early = early_ref.shape[0]
    back = picked(slots, back_ref.shape[0], slots // 2 - total_ref[0], back_ref[...])
    out_ref[:early] = back[:early] + early_ref[...]
    out_ref[early:] = back[early:] + late_ref[: slots - early]


def grad_kernel(total_ref, raw_ref, own_ref, back_ref, out_ref):
    rows = out_ref.shape[0]
    start = pl.program_id(0) * rows
    unit, inverse = unit_rows(raw_ref[...])
    offset = start + pl.num_programs(0) * rows - total_ref[0]
    sums = own_ref[...] + picked(rows, back_ref.shape[0], offset, back_ref[...])
    grads = (sums - unit * jnp.sum(unit * sums, axis=1, keepdims=True)) * inverse
    slot = start + lax.broadcasted_iota(jnp.int32, grads.shape, 0)
    out_ref[...] = jnp.where(slot < total_ref[0], grads, 0.0)


def caption_grads(total, raw, own_rows, back):
    slots, width = raw.shape
    steps = 4
    some = pl.BlockSpec((slots // steps, width), lambda i: (i, 0))
    return pl.pallas_call(
        grad_kernel,
        grid=(steps,),
        out_shape=jax.ShapeDtypeStruct((slots, width), F32),
        in_specs=[SMEM, some, some, pl.BlockSpec(back.shape, lambda i: (0, 0))],
        out_specs=some,
        compiler_params=pltpu.CompilerParams(vmem_limit_bytes=16 * MIB),
        cost_estimate=pl.CostEstimate(
            flops=8 * slots * width, bytes_accessed=4 * MIB, transcendentals=0
        ),
        name="caption_grad",
    )(total, raw, own_rows, back)


def program(image_embed, caption_vectors, caption_counts, natural_log_multiplier, match_odds_offset):
    count, width = image_embed.shape
    slots = caption_vectors.shape[0]
    pair_rows = 9 * count
    index = {a: lax.axis_index(a) for a in AXES}
    home = flat([index[a] for a in AXES])
    scale = jnp.exp(natural_log_multiplier[0])
    scalars = jnp.stack([scale, match_odds_offset[0]])

    far_raw = send(image_embed, flip_route(4))
    half_slots = slots // 2
    partner_a = send(caption_vectors[:half_slots], flip_route(0))
    partner_b = send(caption_vectors[half_slots:], flip_route(0))

    counts = lax.dynamic_slice_in_dim(caption_counts, home * count, count)
    earlier = lax.iota(jnp.int32, count)[None, :] <= lax.iota(jnp.int32, count)[:, None]
    ends = jnp.sum(jnp.where(earlier, counts[None, :], 0), axis=1, keepdims=True)
    spans = jnp.concatenate([ends - counts[:, None], ends], axis=1)
    total = jnp.sum(counts).reshape(1)

    half = jax.ShapeDtypeStruct((4 * count, width), BF16)
    near = plain(
        near_kernel, jax.ShapeDtypeStruct((2 * count, width), BF16), (image_embed, far_raw)
    )
    first = {}
    for k in (2, 1, 3):
        first[k] = send(near, ring_route(0, k))
    head, tail = plain(join_kernel, (half, half), (near, first[1], first[3], first[2]))
    up_head = send(head, ring_route(1, 1))
    down_tail = send(tail, ring_route(1, 3))
    up_tail = send(tail, ring_route(1, 1))
    down_head = send(head, ring_route(1, 3))
    two_head = send(up_head, ring_route(1, 1))
    two_tail = send(down_tail, ring_route(1, 3))

    late_rows = half_slots
    early_rows = pair_rows - late_rows
    early_shape = jax.ShapeDtypeStruct((early_rows, width), BF16)
    late_shape = jax.ShapeDtypeStruct((late_rows, width), BF16)
    own_early, own_late = plain(
        prep_kernel, (early_shape, late_shape), (total, caption_vectors), smem=1
    )
    merge_flops = 2 * early_rows * half_slots * width
    early_own = plain(
        functools.partial(merge_kernel, 0, 1),
        early_shape,
        (total, own_early, partner_a),
        merge_flops,
        1,
        after=(head,),
    )
    early_other = send(early_own, flip_route(2))
    late_own = plain(
        functools.partial(merge_kernel, early_rows, 2),
        late_shape,
        (total, own_late, partner_a, partner_b),
        2 * merge_flops,
        1,
        after=(up_head, down_tail),
    )
    late_other = send(late_own, flip_route(2))

    def early(head, tail, local=False, after=()):
        return early_terms(local, scalars, spans, head, tail, early_own, early_other, after)

    def late(images, sums, types, local=False, after=()):
        return late_terms(
            local, early_rows, scalars, spans, images, sums, late_own, late_other, types, after
        )

    we_local, i_local, s_local = early(head, tail, True)
    we_up, i_up, s_up = early(up_head, up_tail)
    we_down, i_down, s_down = early(down_head, down_tail)
    wl_up, up_a, up_b = late(i_up, s_up, (BF16, F32), after=(we_down,))
    from_above = send(up_a, ring_route(1, 3)).astype(F32)
    wl_down, down_a, down_b = late(i_down, s_down, (F32, BF16))
    from_below = send(down_b, ring_route(1, 1)).astype(F32)
    we_two, i_two, s_two = early(two_head, two_tail, after=(wl_up, wl_down))
    wl_two, two_a, two_b = late(i_two, s_two, (BF16, BF16))
    over_head = send(two_a, ring_route(1, 1)).astype(F32)
    over_tail = send(two_b, ring_route(1, 3)).astype(F32)
    wl_local, local_a, local_b = late(i_local, s_local, (F32, F32), True, after=(wl_two,))
    images = [i_up, i_down, i_two, i_local]
    late_part, late_cross = caption_terms([wl_up, wl_down, wl_two, wl_local], images)
    late_crossed = send(late_cross, flip_route(2))
    early_part, early_cross = caption_terms(
        [we_up, we_down, we_two, we_local], images, after=(late_part,)
    )
    early_crossed = send(early_cross, flip_route(2))
    head_below = send((down_a + over_head).astype(BF16), ring_route(1, 1)).astype(F32)
    tail_above = send((up_b + over_tail).astype(BF16), ring_route(1, 3)).astype(F32)
    back_shape = jax.ShapeDtypeStruct((half_slots, width), BF16)
    late_pair, late_back = plain(
        functools.partial(pair_kernel, 0),
        (jax.ShapeDtypeStruct((late_rows, width), F32), back_shape),
        (late_part, late_crossed),
    )
    returned_late = send(late_back, flip_route(0))
    early_pair, early_back = plain(
        functools.partial(pair_kernel, early_rows - half_slots),
        (jax.ShapeDtypeStruct((early_rows, width), F32), back_shape),
        (early_part, early_crossed),
    )
    returned_early = send(early_back, flip_route(0))
    head_sum = local_a + from_above + head_below
    tail_sum = local_b + from_below + tail_above

    near_rows = 2 * count
    pieces = {1: head_sum[near_rows:], 3: tail_sum[:near_rows], 2: tail_sum[near_rows:]}
    near_sum = head_sum[:near_rows]
    for k in (2, 1, 3):
        near_sum = near_sum + send(pieces[k].astype(BF16), ring_route(0, -k)).astype(F32)
    far_sum = send(near_sum[count:].astype(BF16), flip_route(4)).astype(F32)
    own_sum = near_sum[:count] + far_sum
    image_unit, image_inverse = unit_rows(image_embed)
    image_grad = (
        own_sum - image_unit * jnp.sum(image_unit * own_sum, axis=1, keepdims=True)
    ) * image_inverse

    own_rows = plain(
        home_kernel,
        jax.ShapeDtypeStruct((slots, width), F32),
        (total, early_pair, late_pair, returned_late),
        2 * slots * half_slots * width,
        1,
    )
    caption_grad = caption_grads(total, caption_vectors, own_rows, returned_early)
    return image_grad, caption_grad


def solution(mesh):
    fine = Mesh(mesh.devices.reshape(SIZES), AXES)
    placed = (P(AXES, None), P(AXES, None), P(), P(), P())
    return jax.shard_map(
        program,
        mesh=fine,
        in_specs=placed,
        out_specs=(P(AXES, None), P(AXES, None)),
        check_vma=False,
    )
```

profile of v0, /device:TPU:6, one launch (start us, length us, event | category | flops | bytes accessed | tf_op | source)
XLA Modules:
  0.0 147.0 jit_solution(15220072668862072612)
XLA Ops:
  0.6 3.3 %collective-permute-start = (bf16[64,1152]{1,0:T(8,128)(2,1)}, bf16[64,1152]{1,0:T(8,128)(2,1)S(1)}, u32[]{:S(2)}, u32[]{:S(2)}) collective-permute-start(bf16[64,1152]{1,0:T(8,128)(2,1)} %refs_0_.1), channel_id=1, source_target_pairs={{0,1},{1,0},{2,3},{3,2},{4,5},{5,4},{6,7},{7,6},{8,9},{9,8},{10,11... | collective-permute-start | bytes 442376 | tf_op jit(solution)/shard_map/ppermute | solution.py:63
  3.9 4.1 %collective-permute-done.refs_1_ = bf16[64,1152]{1,0:T(8,128)(2,1)S(1)} collective-permute-done((bf16[64,1152]{1,0:T(8,128)(2,1)}, bf16[64,1152]{1,0:T(8,128)(2,1)S(1)}, u32[]{:S(2)}, u32[]{:S(2)}) %collective-permute-start) | collective-permute-done | bytes 147488 | tf_op jit(solution)/shard_map/ppermute | solution.py:63
  10.6 3.2 %collective-permute-start.1 = (bf16[128,1152]{1,0:T(8,128)(2,1)S(1)}, bf16[128,1152]{1,0:T(8,128)(2,1)S(1)}, u32[]{:S(2)}, u32[]{:S(2)}) collective-permute-start(bf16[128,1152]{1,0:T(8,128)(2,1)S(1)} %shard_map.68.refs_0_), channel_id=1, source_target_pairs={{0,16},{1,17},{2,18},{3,19},{4,20},{5,21},{6,22},{7,23},{8,10},{9,... | collective-permute-start | bytes 884744 | tf_op jit(solution)/shard_map/ppermute | solution.py:63
  13.8 2.1 %fusion.9 = (bf16[256,1152]{1,0:T(8,128)(2,1)}, bf16[256,1152]{1,0:T(8,128)(2,1)S(1)}) fusion(bf16[512,1152]{1,0:T(8,128)(2,1)} %raw_ref.1), kind=kLoop, calls=%fused_computation.25 | loop fusion | bytes 2359296 | tf_op jit(solution)/shard_map/slice | solution.py:314
  18.0 2.6 %collective-permute-done.2.refs_2_ = bf16[128,1152]{1,0:T(8,128)(2,1)S(1)} collective-permute-done((bf16[128,1152]{1,0:T(8,128)(2,1)S(1)}, bf16[128,1152]{1,0:T(8,128)(2,1)S(1)}, u32[]{:S(2)}, u32[]{:S(2)}) %collective-permute-start.2) | collective-permute-done | bytes 294944 | tf_op jit(solution)/shard_map/ppermute | solution.py:63
  21.6 4.0 %collective-permute-start.8 = (bf16[256,1152]{1,0:T(8,128)(2,1)}, bf16[256,1152]{1,0:T(8,128)(2,1)S(1)}, u32[]{:S(2)}, u32[]{:S(2)}) collective-permute-start(bf16[256,1152]{1,0:T(8,128)(2,1)} %get-tuple-element.39.refs_3_), channel_id=1, source_target_pairs={{0,6},{1,7},{2,0},{3,1},{4,2},{5,3},{6,4},{7,5},{8,56},{9,57},{10,... | collective-permute-start | bytes 1769480 | tf_op jit(solution)/shard_map/ppermute | solution.py:63
  28.2 3.9 %collective-permute-done.4.refs_2_ = bf16[256,1152]{1,0:T(8,128)(2,1)S(1)} collective-permute-done((bf16[256,1152]{1,0:T(8,128)(2,1)S(1)}, bf16[256,1152]{1,0:T(8,128)(2,1)S(1)}, u32[]{:S(2)}, u32[]{:S(2)}) %collective-permute-start.4) | collective-permute-done | bytes 589856 | tf_op jit(solution)/shard_map/ppermute | solution.py:63
  33.4 4.1 %collective-permute-start.13 = (bf16[256,1152]{1,0:T(8,128)(2,1)}, bf16[256,1152]{1,0:T(8,128)(2,1)}, u32[]{:S(2)}, u32[]{:S(2)}) collective-permute-start(bf16[256,1152]{1,0:T(8,128)(2,1)} %get-tuple-element.38.refs_3_.refs_2_), channel_id=1, source_target_pairs={{0,6},{1,7},{2,0},{3,1},{4,2},{5,3},{6,4},{7,5},{8,56},{9,57},{10,... | collective-permute-start | bytes 1769480 | tf_op jit(solution)/shard_map/ppermute | solution.py:63
  37.7 5.7 %collective-permute-done.6.refs_3_ = bf16[256,1152]{1,0:T(8,128)(2,1)} collective-permute-done((bf16[256,1152]{1,0:T(8,128)(2,1)}, bf16[256,1152]{1,0:T(8,128)(2,1)}, u32[]{:S(2)}, u32[]{:S(2)}) %collective-permute-start.6) | collective-permute-done | bytes 589856 | tf_op jit(solution)/shard_map/ppermute | solution.py:63
  46.2 2.5 %shard_map.72.refs_4_ = bf16[256,1152]{1,0:T(8,128)(2,1)S(1)} custom-call(s32[1]{0:T(128)} %bitcast.2.refs_0_.total_ref, bf16[256,1152]{1,0:T(8,128)(2,1)S(1)} %get-tuple-element.43.refs_1_, bf16[256,1152]{1,0:T(8,128)(2,1)S(1)} %collective-permute-done.4.refs_2_, bf16[256,1152]{1,0:T(8,128)(2,1)} %collective-permute-done.6.refs_3_, ...), custom_call_target="tpu_custom_call" | custom-call | flops 377487360 | bytes 1048576 | tf_op jit(solution)/shard_map/pallas_call | solution.py:87
  50.2 2.2 %collective-permute-start.11 = (bf16[256,1152]{1,0:T(8,128)(2,1)}, bf16[256,1152]{1,0:T(8,128)(2,1)S(1)}, u32[]{:S(2)}, u32[]{:S(2)}) collective-permute-start(bf16[256,1152]{1,0:T(8,128)(2,1)} %copy-done.3), channel_id=1, source_target_pairs={{0,6},{1,7},{2,0},{3,1},{4,2},{5,3},{6,4},{7,5},{8,56},{9,57},{10,... | collective-permute-start | bytes 1769480 | tf_op jit(solution)/shard_map/ppermute | solution.py:63
  53.6 3.8 %early_remote.4 = (bf16[512,640]{1,0:T(8,128)(2,1)S(1)}, bf16[512,1152]{1,0:T(8,128)(2,1)S(1)}, f32[512,1152]{1,0:T(8,128)S(1)}) custom-call(f32[2]{0:T(128)S(1)} %pad_maximum_fusion.refs_0_, s32[64,2]{1,0:T(8,128)S(1)} %copy.24.refs_1_, bf16[256,1152]{1,0:T(8,128)(2,1)} %collective-permute-done.13.refs_2_, bf16[256,1152]{1,0:T(8,128)(2,1)S(1)} %copy-done.5, ...), custom_call_target="tpu_custom_call" | custom-call | flops 1509949440 | bytes 8388608 | tf_op jit(solution)/shard_map/early_remote/pallas_call | solution.py:184
  57.5 4.0 %early_remote.3 = (bf16[512,640]{1,0:T(8,128)(2,1)S(1)}, bf16[512,1152]{1,0:T(8,128)(2,1)S(1)}, f32[512,1152]{1,0:T(8,128)S(1)}) custom-call(f32[2]{0:T(128)S(1)} %pad_maximum_fusion.refs_0_, s32[64,2]{1,0:T(8,128)S(1)} %copy.24.refs_1_, bf16[256,1152]{1,0:T(8,128)(2,1)} %collective-permute-done.7.refs_4_.refs_2_, ...), custom_call_target="tpu_custom_call" | custom-call | flops 1509949440 | bytes 8388608 | tf_op jit(solution)/shard_map/early_remote/pallas_call | solution.py:184
  61.5 2.2 %late_remote.4 = (bf16[512,512]{1,0:T(8,128)(2,1)S(1)}, f32[256,1152]{1,0:T(8,128)S(1)}, bf16[256,1152]{1,0:T(8,128)(2,1)S(1)}) custom-call(f32[2]{0:T(128)S(1)} %pad_maximum_fusion.refs_0_, s32[64,2]{1,0:T(8,128)S(1)} %copy.24.refs_1_, bf16[512,1152]{1,0:T(8,128)(2,1)S(1)} %get-tuple-element.48.refs_2_.refs_5_, f32[512,1152]{1,0:T(8,128)S(1)} %get-tuple-element.49.refs_3_, ...), custom_call_target="tpu_custom_call" | custom-call | flops 1207959552 | bytes 8388608 | tf_op jit(solution)/shard_map/late_remote/pallas_call | solution.py:205
  63.8 2.3 %late_remote.3 = (bf16[512,512]{1,0:T(8,128)(2,1)S(1)}, bf16[256,1152]{1,0:T(8,128)(2,1)S(1)}, f32[256,1152]{1,0:T(8,128)S(1)}) custom-call(f32[2]{0:T(128)S(1)} %pad_maximum_fusion.refs_0_, s32[64,2]{1,0:T(8,128)S(1)} %copy.24.refs_1_, bf16[512,1152]{1,0:T(8,128)(2,1)S(1)} %get-tuple-element.44.refs_2_.refs_4_, f32[512,1152]{1,0:T(8,128)S(1)} %get-tuple-element.45.refs_3_, ...), custom_call_target="tpu_custom_call" | custom-call | flops 1207959552 | bytes 8388608 | tf_op jit(solution)/shard_map/late_remote/pallas_call | solution.py:205
  66.0 3.7 %early_remote.5 = (bf16[512,640]{1,0:T(8,128)(2,1)S(1)}, bf16[512,1152]{1,0:T(8,128)(2,1)S(1)}, f32[512,1152]{1,0:T(8,128)S(1)}) custom-call(f32[2]{0:T(128)S(1)} %pad_maximum_fusion.refs_0_, s32[64,2]{1,0:T(8,128)S(1)} %copy.24.refs_1_, bf16[256,1152]{1,0:T(8,128)(2,1)S(1)} %collective-permute-done.10.refs_2_, ...), custom_call_target="tpu_custom_call" | custom-call | flops 1509949440 | bytes 8388608 | tf_op jit(solution)/shard_map/early_remote/pallas_call | solution.py:184
  69.7 2.3 %late_remote.5 = (bf16[512,512]{1,0:T(8,128)(2,1)S(1)}, bf16[256,1152]{1,0:T(8,128)(2,1)S(1)}, bf16[256,1152]{1,0:T(8,128)(2,1)S(1)}) custom-call(f32[2]{0:T(128)S(1)} %pad_maximum_fusion.refs_0_, s32[64,2]{1,0:T(8,128)S(1)} %copy.24.refs_1_, bf16[512,1152]{1,0:T(8,128)(2,1)S(1)} %get-tuple-element.51.refs_2_.refs_6_, ...), custom_call_target="tpu_custom_call" | custom-call | flops 1207959552 | bytes 8388608 | tf_op jit(solution)/shard_map/late_remote/pallas_call | solution.py:205
  72.6 4.0 %early_local.1 = (bf16[512,640]{1,0:T(8,128)(2,1)S(1)}, bf16[512,1152]{1,0:T(8,128)(2,1)S(1)}, f32[512,1152]{1,0:T(8,128)S(1)}) custom-call(f32[2]{0:T(128)S(1)} %pad_maximum_fusion.refs_0_, s32[64,2]{1,0:T(8,128)S(1)} %copy.24.refs_1_, bf16[256,1152]{1,0:T(8,128)(2,1)} %get-tuple-element.38.refs_3_.refs_2_, bf16[256,1152]{1,0:T(8,128)(2,1)} %get-tuple-element.39.refs_3_, ...), custom_call_target="tpu_custom_call" | custom-call | flops 1509949440 | bytes 8388608 | tf_op jit(solution)/shard_map/early_local/pallas_call | solution.py:184
  76.6 1.8 %collective-permute-start.17 = (bf16[256,1152]{1,0:T(8,128)(2,1)S(1)}, bf16[256,1152]{1,0:T(8,128)(2,1)S(1)}, u32[]{:S(2)}, u32[]{:S(2)}) collective-permute-start(bf16[256,1152]{1,0:T(8,128)(2,1)S(1)} %get-tuple-element.59), channel_id=1, source_target_pairs={{0,2},{1,3},{2,4},{3,5},{4,6},{5,7},{6,0},{7,1},{8,24},{9,25},{10,... | collective-permute-start | bytes 1769480 | tf_op jit(solution)/shard_map/ppermute | solution.py:63
  80.0 1.7 %collective-permute-start.18 = (bf16[256,1152]{1,0:T(8,128)(2,1)S(1)}, bf16[256,1152]{1,0:T(8,128)(2,1)S(1)}, u32[]{:S(2)}, u32[]{:S(2)}) collective-permute-start(bf16[256,1152]{1,0:T(8,128)(2,1)S(1)} %get-tuple-element.61), channel_id=1, source_target_pairs={{0,6},{1,7},{2,0},{3,1},{4,2},{5,3},{6,4},{7,5},{8,56},{9,57},{10,... | collective-permute-start | bytes 1769480 | tf_op jit(solution)/shard_map/ppermute | solution.py:63
  81.7 2.3 %late_local.1 = (bf16[512,512]{1,0:T(8,128)(2,1)S(1)}, f32[256,1152]{1,0:T(8,128)S(1)}, f32[256,1152]{1,0:T(8,128)S(1)}) custom-call(f32[2]{0:T(128)S(1)} %pad_maximum_fusion.refs_0_, s32[64,2]{1,0:T(8,128)S(1)} %copy.24.refs_1_, bf16[512,1152]{1,0:T(8,128)(2,1)S(1)} %get-tuple-element.41.refs_2_.refs_7_, f32[512,1152]{1,0:T(8,128)S(1)} %get-tuple-element.42.refs_3_, ...), custom_call_target="tpu_custom_call" | custom-call | flops 1207959552 | bytes 8388608 | tf_op jit(solution)/shard_map/late_local/pallas_call | solution.py:205
  84.0 2.9 %caption_terms.2 = (f32[256,1152]{1,0:T(8,128)S(1)}, bf16[256,1152]{1,0:T(8,128)(2,1)S(1)}) custom-call(bf16[512,512]{1,0:T(8,128)(2,1)S(1)} %get-tuple-element.47.refs_6_.refs_0_, bf16[512,512]{1,0:T(8,128)(2,1)S(1)} %get-tuple-element.50.refs_7_.refs_1_, bf16[512,512]{1,0:T(8,128)(2,1)S(1)} %get-tuple-element.53.refs_6_.refs_2_, ...), custom_call_target="tpu_custom_call" | custom-call | flops 2415919104 | bytes 8388608 | tf_op jit(solution)/shard_map/caption_terms/pallas_call | solution.py:243
  87.5 3.6 %caption_terms.3 = (f32[320,1152]{1,0:T(8,128)S(1)}, bf16[320,1152]{1,0:T(8,128)(2,1)S(1)}) custom-call(bf16[512,640]{1,0:T(8,128)(2,1)S(1)} %get-tuple-element.62.refs_0_, bf16[512,640]{1,0:T(8,128)(2,1)S(1)} %get-tuple-element.46.refs_6_.refs_1_, bf16[512,640]{1,0:T(8,128)(2,1)S(1)} %get-tuple-element.63.refs_2_, ...), custom_call_target="tpu_custom_call" | custom-call | flops 3019898880 | bytes 8388608 | tf_op jit(solution)/shard_map/caption_terms/pallas_call | solution.py:243
  91.1 4.1 %collective-permute-done.18 = bf16[256,1152]{1,0:T(8,128)(2,1)S(1)} collective-permute-done((bf16[256,1152]{1,0:T(8,128)(2,1)S(1)}, bf16[256,1152]{1,0:T(8,128)(2,1)S(1)}, u32[]{:S(2)}, u32[]{:S(2)}) %collective-permute-start.18) | collective-permute-done | bytes 589856 | tf_op jit(solution)/shard_map/ppermute | solution.py:63
  95.3 2.3 %collective-permute-start.19 = (bf16[256,1152]{1,0:T(8,128)(2,1)S(1)}, bf16[256,1152]{1,0:T(8,128)(2,1)S(1)}, u32[]{:S(2)}, u32[]{:S(2)}) collective-permute-start(bf16[256,1152]{1,0:T(8,128)(2,1)S(1)} %add_convert_fusion.1), channel_id=1, source_target_pairs={{0,6},{1,7},{2,0},{3,1},{4,2},{5,3},{6,4},{7,5},{8,56},{9,57},{10,... | collective-permute-start | bytes 1769480 | tf_op jit(solution)/shard_map/ppermute | solution.py:63
  99.1 9.3 %collective-permute-done.19 = bf16[256,1152]{1,0:T(8,128)(2,1)S(1)} collective-permute-done((bf16[256,1152]{1,0:T(8,128)(2,1)S(1)}, bf16[256,1152]{1,0:T(8,128)(2,1)S(1)}, u32[]{:S(2)}, u32[]{:S(2)}) %collective-permute-start.19) | collective-permute-done | bytes 589856 | tf_op jit(solution)/shard_map/ppermute | solution.py:63
  110.1 1.8 %collective-permute-start.22 = (bf16[128,1152]{1,0:T(8,128)(2,1)S(1)}, bf16[128,1152]{1,0:T(8,128)(2,1)S(1)}, u32[]{:S(2)}, u32[]{:S(2)}) collective-permute-start(bf16[128,1152]{1,0:T(8,128)(2,1)S(1)} %get-tuple-element.79), channel_id=1, source_target_pairs={{0,16},{1,17},{2,18},{3,19},{4,20},{5,21},{6,22},{7,23},{8,10},{9,... | collective-permute-start | bytes 884744 | tf_op jit(solution)/shard_map/ppermute | solution.py:63
  114.6 2.3 %collective-permute-done.20 = bf16[128,1152]{1,0:T(8,128)(2,1)S(1)} collective-permute-done((bf16[128,1152]{1,0:T(8,128)(2,1)S(1)}, bf16[128,1152]{1,0:T(8,128)(2,1)S(1)}, u32[]{:S(2)}, u32[]{:S(2)}) %collective-permute-start.20) | collective-permute-done | bytes 294944 | tf_op jit(solution)/shard_map/ppermute | solution.py:63
  118.1 3.3 %collective-permute-start.23 = (bf16[64,1152]{1,0:T(8,128)(2,1)S(1)}, bf16[64,1152]{1,0:T(8,128)(2,1)S(1)}, u32[]{:S(2)}, u32[]{:S(2)}) collective-permute-start(bf16[64,1152]{1,0:T(8,128)(2,1)S(1)} %slice.55), channel_id=1, source_target_pairs={{0,1},{1,0},{2,3},{3,2},{4,5},{5,4},{6,7},{7,6},{8,9},{9,8},{10,11... | collective-permute-start | bytes 442376 | tf_op jit(solution)/shard_map/ppermute | solution.py:63
  121.4 7.2 %collective-permute-done.26.refs_3_ = bf16[256,1152]{1,0:T(8,128)(2,1)S(1)} collective-permute-done((bf16[256,1152]{1,0:T(8,128)(2,1)S(1)}, bf16[256,1152]{1,0:T(8,128)(2,1)S(1)}, u32[]{:S(2)}, u32[]{:S(2)}) %collective-permute-start.26) | collective-permute-done | bytes 589856 | tf_op jit(solution)/shard_map/ppermute | solution.py:63
  129.7 11.5 %collective-permute-done.27.back_ref = bf16[256,1152]{1,0:T(8,128)(2,1)S(1)} collective-permute-done((bf16[256,1152]{1,0:T(8,128)(2,1)S(1)}, bf16[256,1152]{1,0:T(8,128)(2,1)S(1)}, u32[]{:S(2)}, u32[]{:S(2)}) %collective-permute-start.27) | collective-permute-done | bytes 589856 | tf_op jit(solution)/shard_map/ppermute | solution.py:63
  141.2 3.6 %caption_grad.1 = f32[512,1152]{1,0:T(8,128)} custom-call(s32[1]{0:T(128)} %bitcast.2.refs_0_.total_ref, bf16[512,1152]{1,0:T(8,128)(2,1)S(1)} %copy-done, f32[512,1152]{1,0:T(8,128)S(1)} %shard_map.75.own_ref, bf16[256,1152]{1,0:T(8,128)(2,1)S(1)} %collective-permute-done.27.back_ref), custom_call_target="tpu_custom_call" | custom-call | flops 4718592 | bytes 4194304 | tf_op jit(solution)/shard_map/caption_grad/pallas_call | solution.py:288
  (74 shorter events, 27.1 us)
Async XLA Ops:
  0.6 7.4 %collective-permute-start = (bf16[64,1152]{1,0:T(8,128)(2,1)}, bf16[64,1152]{1,0:T(8,128)(2,1)S(1)}, u32[]{:S(2)}, u32[]{:S(2)}) collective-permute-start(bf16[64,1152]{1,0:T(8,128)(2,1)} %refs_0_.1), channel_id=1, source_target_pairs={{0,1},{1,0},{2,3},{3,2},{4,5},{5,4},{6,7},{7,6},{8,9},{9,8},{10,11... | collective-permute-start | bytes 442376 | tf_op jit(solution)/shard_map/ppermute | solution.py:63
  9.1 8.9 %collective-permute-start.3 = (bf16[128,1152]{1,0:T(8,128)(2,1)S(1)}, bf16[128,1152]{1,0:T(8,128)(2,1)S(1)}, u32[]{:S(2)}, u32[]{:S(2)}) collective-permute-start(bf16[128,1152]{1,0:T(8,128)(2,1)S(1)} %shard_map.68.refs_0_), channel_id=1, source_target_pairs={{0,32},{1,33},{2,34},{3,35},{4,36},{5,37},{6,38},{7,39},{8,12},{9,... | collective-permute-start | bytes 884744 | tf_op jit(solution)/shard_map/ppermute | solution.py:63
  10.6 10.0 %collective-permute-start.2 = (bf16[128,1152]{1,0:T(8,128)(2,1)S(1)}, bf16[128,1152]{1,0:T(8,128)(2,1)S(1)}, u32[]{:S(2)}, u32[]{:S(2)}) collective-permute-start(bf16[128,1152]{1,0:T(8,128)(2,1)S(1)} %shard_map.68.refs_0_), channel_id=1, source_target_pairs={{0,48},{1,49},{2,50},{3,51},{4,52},{5,53},{6,54},{7,55},{8,14},{9,... | collective-permute-start | bytes 884744 | tf_op jit(solution)/shard_map/ppermute | solution.py:63
  10.6 10.0 %collective-permute-start.1 = (bf16[128,1152]{1,0:T(8,128)(2,1)S(1)}, bf16[128,1152]{1,0:T(8,128)(2,1)S(1)}, u32[]{:S(2)}, u32[]{:S(2)}) collective-permute-start(bf16[128,1152]{1,0:T(8,128)(2,1)S(1)} %shard_map.68.refs_0_), channel_id=1, source_target_pairs={{0,16},{1,17},{2,18},{3,19},{4,20},{5,21},{6,22},{7,23},{8,10},{9,... | collective-permute-start | bytes 884744 | tf_op jit(solution)/shard_map/ppermute | solution.py:63
  15.9 11.1 %copy-start = (bf16[512,1152]{1,0:T(8,128)(2,1)S(1)}, bf16[512,1152]{1,0:T(8,128)(2,1)}, u32[]{:S(2)}) copy-start(bf16[512,1152]{1,0:T(8,128)(2,1)} %raw_ref.1) | copy-start | bytes 3538948
  15.9 16.2 %collective-permute-start.4 = (bf16[256,1152]{1,0:T(8,128)(2,1)S(1)}, bf16[256,1152]{1,0:T(8,128)(2,1)S(1)}, u32[]{:S(2)}, u32[]{:S(2)}) collective-permute-start(bf16[256,1152]{1,0:T(8,128)(2,1)S(1)} %get-tuple-element.77), channel_id=1, source_target_pairs={{0,64},{1,65},{2,66},{3,67},{4,68},{5,69},{6,70},{7,71},{8,72},{9,... | collective-permute-start | bytes 1769480 | tf_op jit(solution)/shard_map/ppermute | solution.py:63
  17.5 25.8 %collective-permute-start.6 = (bf16[256,1152]{1,0:T(8,128)(2,1)}, bf16[256,1152]{1,0:T(8,128)(2,1)}, u32[]{:S(2)}, u32[]{:S(2)}) collective-permute-start(bf16[256,1152]{1,0:T(8,128)(2,1)} %get-tuple-element.76), channel_id=1, source_target_pairs={{0,64},{1,65},{2,66},{3,67},{4,68},{5,69},{6,70},{7,71},{8,72},{9,... | collective-permute-start | bytes 1769480 | tf_op jit(solution)/shard_map/ppermute | solution.py:63
  21.6 22.7 %collective-permute-start.8 = (bf16[256,1152]{1,0:T(8,128)(2,1)}, bf16[256,1152]{1,0:T(8,128)(2,1)S(1)}, u32[]{:S(2)}, u32[]{:S(2)}) collective-permute-start(bf16[256,1152]{1,0:T(8,128)(2,1)} %get-tuple-element.39.refs_3_), channel_id=1, source_target_pairs={{0,6},{1,7},{2,0},{3,1},{4,2},{5,3},{6,4},{7,5},{8,56},{9,57},{10,... | collective-permute-start | bytes 1769480 | tf_op jit(solution)/shard_map/ppermute | solution.py:63
  25.7 19.5 %collective-permute-start.7 = (bf16[256,1152]{1,0:T(8,128)(2,1)}, bf16[256,1152]{1,0:T(8,128)(2,1)}, u32[]{:S(2)}, u32[]{:S(2)}) collective-permute-start(bf16[256,1152]{1,0:T(8,128)(2,1)} %get-tuple-element.38.refs_3_.refs_2_), channel_id=1, source_target_pairs={{0,2},{1,3},{2,4},{3,5},{4,6},{5,7},{6,0},{7,1},{8,24},{9,25},{10,... | collective-permute-start | bytes 1769480 | tf_op jit(solution)/shard_map/ppermute | solution.py:63
  33.3 19.2 %collective-permute-start.5 = (bf16[320,1152]{1,0:T(8,128)(2,1)S(1)}, bf16[320,1152]{1,0:T(8,128)(2,1)}, u32[]{:S(2)}, u32[]{:S(2)}) collective-permute-start(bf16[320,1152]{1,0:T(8,128)(2,1)S(1)} %shard_map.71.refs_4_), channel_id=1, source_target_pairs={{0,8},{1,9},{2,10},{3,11},{4,12},{5,13},{6,14},{7,15},{8,0},{9,1},... | collective-permute-start | bytes 2211848 | tf_op jit(solution)/shard_map/ppermute | solution.py:63
  33.4 19.0 %collective-permute-start.13 = (bf16[256,1152]{1,0:T(8,128)(2,1)}, bf16[256,1152]{1,0:T(8,128)(2,1)}, u32[]{:S(2)}, u32[]{:S(2)}) collective-permute-start(bf16[256,1152]{1,0:T(8,128)(2,1)} %get-tuple-element.38.refs_3_.refs_2_), channel_id=1, source_target_pairs={{0,6},{1,7},{2,0},{3,1},{4,2},{5,3},{6,4},{7,5},{8,56},{9,57},{10,... | collective-permute-start | bytes 1769480 | tf_op jit(solution)/shard_map/ppermute | solution.py:63
  43.3 14.2 %collective-permute-start.12 = (bf16[256,1152]{1,0:T(8,128)(2,1)}, bf16[256,1152]{1,0:T(8,128)(2,1)}, u32[]{:S(2)}, u32[]{:S(2)}) collective-permute-start(bf16[256,1152]{1,0:T(8,128)(2,1)} %get-tuple-element.39.refs_3_), channel_id=1, source_target_pairs={{0,2},{1,3},{2,4},{3,5},{4,6},{5,7},{6,0},{7,1},{8,24},{9,25},{10,... | collective-permute-start | bytes 1769480 | tf_op jit(solution)/shard_map/ppermute | solution.py:63
  45.2 1.1 copy-start.4
  48.7 12.8 %collective-permute-start.9 = (bf16[256,1152]{1,0:T(8,128)(2,1)S(1)}, bf16[256,1152]{1,0:T(8,128)(2,1)S(1)}, u32[]{:S(2)}, u32[]{:S(2)}) collective-permute-start(bf16[256,1152]{1,0:T(8,128)(2,1)S(1)} %shard_map.72.refs_4_), channel_id=1, source_target_pairs={{0,8},{1,9},{2,10},{3,11},{4,12},{5,13},{6,14},{7,15},{8,0},{9,1},... | collective-permute-start | bytes 1769480 | tf_op jit(solution)/shard_map/ppermute | solution.py:63
  50.2 15.8 %collective-permute-start.11 = (bf16[256,1152]{1,0:T(8,128)(2,1)}, bf16[256,1152]{1,0:T(8,128)(2,1)S(1)}, u32[]{:S(2)}, u32[]{:S(2)}) collective-permute-start(bf16[256,1152]{1,0:T(8,128)(2,1)} %copy-done.3), channel_id=1, source_target_pairs={{0,6},{1,7},{2,0},{3,1},{4,2},{5,3},{6,4},{7,5},{8,56},{9,57},{10,... | collective-permute-start | bytes 1769480 | tf_op jit(solution)/shard_map/ppermute | solution.py:63
  52.5 13.6 %collective-permute-start.10 = (bf16[256,1152]{1,0:T(8,128)(2,1)}, bf16[256,1152]{1,0:T(8,128)(2,1)S(1)}, u32[]{:S(2)}, u32[]{:S(2)}) collective-permute-start(bf16[256,1152]{1,0:T(8,128)(2,1)} %collective-permute-done.7.refs_4_.refs_2_), channel_id=1, source_target_pairs={{0,2},{1,3},{2,4},{3,5},{4,6},{5,7},{6,0},{7,1},{8,24},{9,25},{10,... | collective-permute-start | bytes 1769480 | tf_op jit(solution)/shard_map/ppermute | solution.py:63
  52.6 1.1 copy-start.5
  72.0 15.0 %collective-permute-start.15 = (bf16[256,1152]{1,0:T(8,128)(2,1)S(1)}, bf16[256,1152]{1,0:T(8,128)(2,1)S(1)}, u32[]{:S(2)}, u32[]{:S(2)}) collective-permute-start(bf16[256,1152]{1,0:T(8,128)(2,1)S(1)} %get-tuple-element.57), channel_id=1, source_target_pairs={{0,2},{1,3},{2,4},{3,5},{4,6},{5,7},{6,0},{7,1},{8,24},{9,25},{10,... | collective-permute-start | bytes 1769480 | tf_op jit(solution)/shard_map/ppermute | solution.py:63
  76.6 22.5 %collective-permute-start.17 = (bf16[256,1152]{1,0:T(8,128)(2,1)S(1)}, bf16[256,1152]{1,0:T(8,128)(2,1)S(1)}, u32[]{:S(2)}, u32[]{:S(2)}) collective-permute-start(bf16[256,1152]{1,0:T(8,128)(2,1)S(1)} %get-tuple-element.59), channel_id=1, source_target_pairs={{0,2},{1,3},{2,4},{3,5},{4,6},{5,7},{6,0},{7,1},{8,24},{9,25},{10,... | collective-permute-start | bytes 1769480 | tf_op jit(solution)/shard_map/ppermute | solution.py:63
  78.5 16.8 %collective-permute-start.14 = (bf16[256,1152]{1,0:T(8,128)(2,1)S(1)}, bf16[256,1152]{1,0:T(8,128)(2,1)S(1)}, u32[]{:S(2)}, u32[]{:S(2)}) collective-permute-start(bf16[256,1152]{1,0:T(8,128)(2,1)S(1)} %get-tuple-element.55), channel_id=1, source_target_pairs={{0,6},{1,7},{2,0},{3,1},{4,2},{5,3},{6,4},{7,5},{8,56},{9,57},{10,... | collective-permute-start | bytes 1769480 | tf_op jit(solution)/shard_map/ppermute | solution.py:63
  80.0 15.2 %collective-permute-start.18 = (bf16[256,1152]{1,0:T(8,128)(2,1)S(1)}, bf16[256,1152]{1,0:T(8,128)(2,1)S(1)}, u32[]{:S(2)}, u32[]{:S(2)}) collective-permute-start(bf16[256,1152]{1,0:T(8,128)(2,1)S(1)} %get-tuple-element.61), channel_id=1, source_target_pairs={{0,6},{1,7},{2,0},{3,1},{4,2},{5,3},{6,4},{7,5},{8,56},{9,57},{10,... | collective-permute-start | bytes 1769480 | tf_op jit(solution)/shard_map/ppermute | solution.py:63
  86.9 25.2 %collective-permute-start.25 = (bf16[256,1152]{1,0:T(8,128)(2,1)S(1)}, bf16[256,1152]{1,0:T(8,128)(2,1)S(1)}, u32[]{:S(2)}, u32[]{:S(2)}) collective-permute-start(bf16[256,1152]{1,0:T(8,128)(2,1)S(1)} %get-tuple-element.70), channel_id=1, source_target_pairs={{0,8},{1,9},{2,10},{3,11},{4,12},{5,13},{6,14},{7,15},{8,0},{9,1},... | collective-permute-start | bytes 1769480 | tf_op jit(solution)/shard_map/ppermute | solution.py:63
  87.1 11.2 %collective-permute-start.16 = (bf16[256,1152]{1,0:T(8,128)(2,1)S(1)}, bf16[256,1152]{1,0:T(8,128)(2,1)S(1)}, u32[]{:S(2)}, u32[]{:S(2)}) collective-permute-start(bf16[256,1152]{1,0:T(8,128)(2,1)S(1)} %add_convert_fusion.2), channel_id=1, source_target_pairs={{0,2},{1,3},{2,4},{3,5},{4,6},{5,7},{6,0},{7,1},{8,24},{9,25},{10,... | collective-permute-start | bytes 1769480 | tf_op jit(solution)/shard_map/ppermute | solution.py:63
  95.2 18.7 %collective-permute-start.24 = (bf16[320,1152]{1,0:T(8,128)(2,1)S(1)}, bf16[320,1152]{1,0:T(8,128)(2,1)S(1)}, u32[]{:S(2)}, u32[]{:S(2)}) collective-permute-start(bf16[320,1152]{1,0:T(8,128)(2,1)S(1)} %get-tuple-element.68), channel_id=1, source_target_pairs={{0,8},{1,9},{2,10},{3,11},{4,12},{5,13},{6,14},{7,15},{8,0},{9,1},... | collective-permute-start | bytes 2211848 | tf_op jit(solution)/shard_map/ppermute | solution.py:63
  95.3 13.1 %collective-permute-start.19 = (bf16[256,1152]{1,0:T(8,128)(2,1)S(1)}, bf16[256,1152]{1,0:T(8,128)(2,1)S(1)}, u32[]{:S(2)}, u32[]{:S(2)}) collective-permute-start(bf16[256,1152]{1,0:T(8,128)(2,1)S(1)} %add_convert_fusion.1), channel_id=1, source_target_pairs={{0,6},{1,7},{2,0},{3,1},{4,2},{5,3},{6,4},{7,5},{8,56},{9,57},{10,... | collective-permute-start | bytes 1769480 | tf_op jit(solution)/shard_map/ppermute | solution.py:63
  98.5 16.1 %collective-permute-start.21 = (bf16[128,1152]{1,0:T(8,128)(2,1)S(1)}, bf16[128,1152]{1,0:T(8,128)(2,1)S(1)}, u32[]{:S(2)}, u32[]{:S(2)}) collective-permute-start(bf16[128,1152]{1,0:T(8,128)(2,1)S(1)} %slice.54), channel_id=1, source_target_pairs={{0,48},{1,49},{2,50},{3,51},{4,52},{5,53},{6,54},{7,55},{8,14},{9,... | collective-permute-start | bytes 884744 | tf_op jit(solution)/shard_map/ppermute | solution.py:63
  108.6 3.4 %copy-start.2 = (bf16[64,1152]{1,0:T(8,128)(2,1)S(1)}, bf16[64,1152]{1,0:T(8,128)(2,1)}, u32[]{:S(2)}) copy-start(bf16[64,1152]{1,0:T(8,128)(2,1)} %refs_0_.1) | copy-start | bytes 442372
  108.7 8.3 %collective-permute-start.20 = (bf16[128,1152]{1,0:T(8,128)(2,1)S(1)}, bf16[128,1152]{1,0:T(8,128)(2,1)S(1)}, u32[]{:S(2)}, u32[]{:S(2)}) collective-permute-start(bf16[128,1152]{1,0:T(8,128)(2,1)S(1)} %get-tuple-element.78), channel_id=1, source_target_pairs={{0,32},{1,33},{2,34},{3,35},{4,36},{5,37},{6,38},{7,39},{8,12},{9,... | collective-permute-start | bytes 884744 | tf_op jit(solution)/shard_map/ppermute | solution.py:63
  110.1 7.8 %collective-permute-start.22 = (bf16[128,1152]{1,0:T(8,128)(2,1)S(1)}, bf16[128,1152]{1,0:T(8,128)(2,1)S(1)}, u32[]{:S(2)}, u32[]{:S(2)}) collective-permute-start(bf16[128,1152]{1,0:T(8,128)(2,1)S(1)} %get-tuple-element.79), channel_id=1, source_target_pairs={{0,16},{1,17},{2,18},{3,19},{4,20},{5,21},{6,22},{7,23},{8,10},{9,... | collective-permute-start | bytes 884744 | tf_op jit(solution)/shard_map/ppermute | solution.py:63
  112.2 16.3 %collective-permute-start.26 = (bf16[256,1152]{1,0:T(8,128)(2,1)S(1)}, bf16[256,1152]{1,0:T(8,128)(2,1)S(1)}, u32[]{:S(2)}, u32[]{:S(2)}) collective-permute-start(bf16[256,1152]{1,0:T(8,128)(2,1)S(1)} %get-tuple-element.72), channel_id=1, source_target_pairs={{0,64},{1,65},{2,66},{3,67},{4,68},{5,69},{6,70},{7,71},{8,72},{9,... | collective-permute-start | bytes 1769480 | tf_op jit(solution)/shard_map/ppermute | solution.py:63
  114.1 27.1 %collective-permute-start.27 = (bf16[256,1152]{1,0:T(8,128)(2,1)S(1)}, bf16[256,1152]{1,0:T(8,128)(2,1)S(1)}, u32[]{:S(2)}, u32[]{:S(2)}) collective-permute-start(bf16[256,1152]{1,0:T(8,128)(2,1)S(1)} %get-tuple-element.73), channel_id=1, source_target_pairs={{0,64},{1,65},{2,66},{3,67},{4,68},{5,69},{6,70},{7,71},{8,72},{9,... | collective-permute-start | bytes 1769480 | tf_op jit(solution)/shard_map/ppermute | solution.py:63
  118.1 27.9 %collective-permute-start.23 = (bf16[64,1152]{1,0:T(8,128)(2,1)S(1)}, bf16[64,1152]{1,0:T(8,128)(2,1)S(1)}, u32[]{:S(2)}, u32[]{:S(2)}) collective-permute-start(bf16[64,1152]{1,0:T(8,128)(2,1)S(1)} %slice.55), channel_id=1, source_target_pairs={{0,1},{1,0},{2,3},{3,2},{4,5},{5,4},{6,7},{7,6},{8,9},{9,8},{10,11... | collective-permute-start | bytes 442376 | tf_op jit(solution)/shard_map/ppermute | solution.py:63
  (2 other events, 1.7 us)
where the time goes:
time: 148 us; the launch traced here: 147 us
  waiting for transfers between devices  53.6 us (36%)
  Pallas kernels  42.1 us (28%)
  starting transfers between devices  39.4 us (27%)
  local copies, waits for them, and re-layouts  6.2 us (4%)
  other arithmetic  3.43 us (2%)
  between operations  2.24 us (2%)
    ppermute x28, waiting for transfers between devices, send(): return lax.ppermute(value, AXES, pairs)  53.6 us
    ppermute x28, starting transfers between devices, send(): return lax.ppermute(value, AXES, pairs)  39.4 us
    pallas_call x4, Pallas kernels, early_terms(): pl.pallas_call(lambda *refs: early_kernel(local, *refs), out_shape=(jax.S...  15.5 us
    pallas_call x4, Pallas kernels, late_terms(): pl.pallas_call(lambda *refs: late_kernel(local, start, *refs), out_shape=...  9.04 us
    pallas_call x8, Pallas kernels, plain(): pl.pallas_call(lambda *refs: kernel(*refs[:len(args)], *refs[len(args) +...  7.51 us
    pallas_call x2, Pallas kernels, caption_terms(): pl.pallas_call(lambda *refs: caption_kernel(len(weights), *refs), out_sha...  6.51 us
    unnamed x12, local copies, waits for them, and re-layouts  3.86 us
    pallas_call x1, Pallas kernels, caption_grads(): pl.pallas_call(grad_kernel, grid=(steps,), out_shape=jax.ShapeDtypeStruct...  3.56 us
  transfers between devices with their start and end apart: 28, of which 12 were waited for; matrix products, arithmetic and copies ran while one was open for 3% of the time, Pallas kernels for 25%

commit v1 on v0

v1 whole, which is shorter than its diff:
```python
import functools

import jax
import jax.numpy as jnp
from jax import lax
from jax.experimental import pallas as pl
from jax.experimental.pallas import tpu as pltpu
from jax.sharding import Mesh, PartitionSpec as P


EPSILON = 1e-06
LOG2E = 1.4426950408889634
AXES = ("y_lo", "x", "core", "z", "y_hi")
SIZES = (2, 4, 2, 4, 2)
F32 = jnp.float32
BF16 = jnp.bfloat16
VMEM = pl.BlockSpec(memory_space=pltpu.VMEM)
ANY = pl.BlockSpec(memory_space=pl.ANY)
SMEM = pl.BlockSpec(memory_space=pltpu.SMEM)
MIB = 2**20


def coordinates(device):
    out = []
    for size in reversed(SIZES):
        out.append(device % size)
        device //= size
    return out[::-1]


def flat(coords):
    device = 0
    for size, c in zip(SIZES, coords):
        device = device * size + c
    return device


def route(move):
    pairs = []
    for device in range(128):
        c = coordinates(device)
        move(c)
        pairs.append((device, flat(c)))
    return pairs


def ring_route(stage, distance):
    def move(c):
        axis = 1 if c[2] == stage else 3
        c[axis] = (c[axis] + distance) % 4

    return route(move)


def flip_route(axis):
    def move(c):
        c[axis] = 1 - c[axis]

    return route(move)


def send(value, pairs):
    return lax.ppermute(value, AXES, pairs)


def unit_rows(raw):
    values = raw.astype(F32)
    inverse = lax.rsqrt(jnp.sum(values * values, axis=1, keepdims=True) + EPSILON)
    return values * inverse, inverse


def near_kernel(own_ref, far_ref, near_ref):
    count = own_ref.shape[0]
    near_ref[:count] = unit_rows(own_ref[...])[0].astype(BF16)
    near_ref[count:] = unit_rows(far_ref[...])[0].astype(BF16)


def join_kernel(*refs):
    rows = refs[0].shape[0]
    refs[-2][:rows] = refs[0][...]
    refs[-2][rows:] = refs[1][...]
    refs[-1][:rows] = refs[2][...]
    refs[-1][rows:] = refs[3][...]


def plain(kernel, out_shape, args, flops=10**6, smem=0, limit=16, after=()):
    return pl.pallas_call(
        lambda *refs: kernel(*refs[: len(args)], *refs[len(args) + len(after) :]),
        out_shape=out_shape,
        in_specs=[SMEM] * smem + [VMEM] * (len(args) - smem) + [ANY] * len(after),
        out_specs=(VMEM,) * len(out_shape) if isinstance(out_shape, tuple) else VMEM,
        compiler_params=pltpu.CompilerParams(vmem_limit_bytes=limit * MIB),
        cost_estimate=pl.CostEstimate(flops=flops, bytes_accessed=MIB, transcendentals=0),
    )(*args, *after)


def prep_kernel(total_ref, own_ref, out_ref):
    slots = own_ref.shape[0]
    low = unit_rows(own_ref[...])[0]
    slot = lax.broadcasted_iota(jnp.int32, low.shape, 0)
    out_ref[:slots] = jnp.where(slot < total_ref[0], low, 0.0).astype(BF16)
    out_ref[slots:] = jnp.zeros((out_ref.shape[0] - slots, low.shape[1]), BF16)


def picked(rows, columns, offset, values):
    row = lax.broadcasted_iota(jnp.int32, (rows, columns), 0)
    column = lax.broadcasted_iota(jnp.int32, (rows, columns), 1)
    pick = jnp.where(column == row + offset, 1.0, 0.0).astype(BF16)
    return jnp.dot(pick, values, preferred_element_type=F32)


def merge_kernel(total_ref, own_ref, raw_ref, out_ref):
    low = unit_rows(raw_ref[...])[0].astype(BF16)
    other = picked(out_ref.shape[0], low.shape[0], -total_ref[0], low)
    out_ref[...] = (own_ref[...].astype(F32) + other).astype(BF16)


def stack_kernel(own_ref, other_ref, out_ref):
    rows = own_ref.shape[0]
    out_ref[:512] = own_ref[:512]
    out_ref[512:1024] = other_ref[:512]
    out_ref[1024 : rows + 512] = own_ref[512:]
    out_ref[rows + 512 :] = other_ref[512:]


def weigh(local, scalar_ref, spans_ref, images, captions, weight_ref):
    scale = scalar_ref[0]
    bias = scalar_ref[1]
    scores = lax.dot_general(
        images, captions, (((1,), (1,)), ((), ())), preferred_element_type=F32
    )
    steep = scores * (scale * -LOG2E) + (bias * -LOG2E)
    weight_ref[...] = (scale / (1.0 + jnp.exp2(steep))).astype(BF16)
    if local:
        count = spans_ref.shape[0]
        head = steep[:count, :512]
        slot = lax.broadcasted_iota(jnp.int32, head.shape, 1)
        match = (slot >= spans_ref[:, 0:1]) & (slot < spans_ref[:, 1:2])
        value = scale / (1.0 + jnp.exp2(jnp.where(match, -head, head)))
        weight_ref[:count, :512] = jnp.where(match, -value, value).astype(BF16)


def weight_kernel(
    local, sums, scalar_ref, spans_ref, head_ref, tail_ref, captions_ref, weight_ref, images_ref,
    *outs,
):
    rows = head_ref.shape[0]
    images_ref[:rows] = head_ref[...]
    images_ref[rows:] = tail_ref[...]
    weigh(local, scalar_ref, spans_ref, images_ref[...], captions_ref[...], weight_ref)
    if sums:
        total = jnp.dot(weight_ref[...], captions_ref[...], preferred_element_type=F32)
        outs[0][...] = total[:rows].astype(outs[0].dtype)
        outs[1][...] = total[rows:].astype(outs[1].dtype)


def weight_terms(local, types, scalars, spans, head, tail, captions, after=()):
    rows, width = head.shape
    slots = captions.shape[0]
    arity = 5
    return pl.pallas_call(
        lambda *refs: weight_kernel(
            local, bool(types), *refs[:arity], *refs[arity + len(after) :]
        ),
        out_shape=(
            jax.ShapeDtypeStruct((2 * rows, slots), BF16),
            jax.ShapeDtypeStruct((2 * rows, width), BF16),
            *[jax.ShapeDtypeStruct((rows, width), t) for t in types],
        ),
        in_specs=[SMEM] + [VMEM] * (arity - 1) + [ANY] * len(after),
        out_specs=(VMEM,) * (2 + len(types)),
        compiler_params=pltpu.CompilerParams(vmem_limit_bytes=20 * MIB),
        cost_estimate=pl.CostEstimate(
            flops=(8 if types else 4) * rows * slots * width,
            bytes_accessed=8 * MIB,
            transcendentals=2 * rows * slots,
        ),
        name="block_local" if local else "block_remote",
    )(scalars, spans, head, tail, captions, *after)


def local_sums_kernel(weight_ref, captions_ref, head_out, tail_out):
    rows = head_out.shape[0]
    total = jnp.dot(weight_ref[...], captions_ref[...], preferred_element_type=F32)
    head_out[...] = total[:rows]
    tail_out[...] = total[rows:]


def caption_sum(refs, blocks, columns):
    total = None
    for weight_ref, images_ref in zip(refs[:blocks], refs[blocks : 2 * blocks]):
        part = lax.dot_general(
            weight_ref[:, columns], images_ref[...], (((0,), (0,)), ((), ())),
            preferred_element_type=F32,
        )
        total = part if total is None else total + part
    return total


def cross_kernel(blocks, *refs):
    cross_ref, tail_ref = refs[-2:]
    rest = tail_ref.shape[0]
    total = caption_sum(refs, blocks, slice(512, refs[0].shape[1]))
    cross_ref[:512] = total[:512].astype(BF16)
    tail_ref[...] = total[512 : 512 + rest]
    cross_ref[512:] = total[512 + rest :].astype(BF16)


def own_kernel(blocks, *refs):
    refs[-1][...] = caption_sum(refs, blocks, slice(0, 512))


def combine_kernel(down_a, down_b, over_head, up_a, up_b, over_tail, plus_ref, minus_ref):
    rows = down_a.shape[0]
    plus_ref[:rows] = (down_a[...] + over_head[...].astype(F32)).astype(BF16)
    plus_ref[rows:] = down_b[...]
    minus_ref[:rows] = up_a[...]
    minus_ref[rows:] = (up_b[...] + over_tail[...].astype(F32)).astype(BF16)


def back_kernel(total_ref, own_ref, tail_ref, cross_ref, pair_ref, back_ref):
    slots, rest = own_ref.shape[0], tail_ref.shape[0]
    pair = own_ref[...] + cross_ref[:slots].astype(F32)
    tail = tail_ref[...] + cross_ref[slots:].astype(F32)
    pair_ref[...] = pair
    offset = total_ref[0]
    back_ref[...] = (
        picked(slots, slots, offset, pair.astype(BF16))
        + picked(slots, rest, offset - slots, tail.astype(BF16))
    ).astype(BF16)


def grad_kernel(total_ref, raw_ref, own_ref, back_ref, out_ref):
    rows = out_ref.shape[0]
    unit, inverse = unit_rows(raw_ref[...])
    sums = own_ref[...] + back_ref[...].astype(F32)
    grads = (sums - unit * jnp.sum(unit * sums, axis=1, keepdims=True)) * inverse
    slot = pl.program_id(0) * rows + lax.broadcasted_iota(jnp.int32, grads.shape, 0)
    out_ref[...] = jnp.where(slot < total_ref[0], grads, 0.0)


def caption_grads(total, raw, own_rows, back):
    slots, width = raw.shape
    steps = 4
    some = pl.BlockSpec((slots // steps, width), lambda i: (i, 0))
    return pl.pallas_call(
        grad_kernel,
        grid=(steps,),
        out_shape=jax.ShapeDtypeStruct((slots, width), F32),
        in_specs=[SMEM, some, some, some],
        out_specs=some,
        compiler_params=pltpu.CompilerParams(vmem_limit_bytes=16 * MIB),
        cost_estimate=pl.CostEstimate(
            flops=8 * slots * width, bytes_accessed=4 * MIB, transcendentals=0
        ),
        name="caption_grad",
    )(total, raw, own_rows, back)


def program(image_embed, caption_vectors, caption_counts, natural_log_multiplier, match_odds_offset):
    count, width = image_embed.shape
    slots = caption_vectors.shape[0]
    pair_rows = 9 * count
    index = {a: lax.axis_index(a) for a in AXES}
    home = flat([index[a] for a in AXES])
    scale = jnp.exp(natural_log_multiplier[0])
    scalars = jnp.stack([scale, match_odds_offset[0]])

    far_raw = send(image_embed, flip_route(4))
    partner_raw = send(caption_vectors, flip_route(0))

    counts = lax.dynamic_slice_in_dim(caption_counts, home * count, count)
    earlier = lax.iota(jnp.int32, count)[None, :] <= lax.iota(jnp.int32, count)[:, None]
    ends = jnp.sum(jnp.where(earlier, counts[None, :], 0), axis=1, keepdims=True)
    spans = jnp.concatenate([ends - counts[:, None], ends], axis=1)
    total = jnp.sum(counts).reshape(1)

    half = jax.ShapeDtypeStruct((4 * count, width), BF16)
    near = plain(
        near_kernel, jax.ShapeDtypeStruct((2 * count, width), BF16), (image_embed, far_raw)
    )
    first = {}
    for k in (2, 1, 3):
        first[k] = send(near, ring_route(0, k))
    own_pad = plain(
        prep_kernel,
        jax.ShapeDtypeStruct((pair_rows, width), BF16),
        (total, caption_vectors),
        smem=1,
    )
    head, tail = plain(
        join_kernel, (half, half), (near, first[1], first[3], first[2]), after=(own_pad,)
    )
    up_head = send(head, ring_route(1, 1))
    down_tail = send(tail, ring_route(1, 3))
    up_tail = send(tail, ring_route(1, 1))
    down_head = send(head, ring_route(1, 3))
    two_head = send(up_head, ring_route(1, 1))
    two_tail = send(down_tail, ring_route(1, 3))

    own_pair = plain(
        merge_kernel,
        jax.ShapeDtypeStruct((pair_rows, width), BF16),
        (total, own_pad, partner_raw),
        2 * pair_rows * slots * width,
        1,
        after=(head,),
    )
    other_pair = send(own_pair, flip_route(2))
    captions = plain(
        stack_kernel, jax.ShapeDtypeStruct((2 * pair_rows, width), BF16), (own_pair, other_pair)
    )

    def terms(head, tail, types, local=False, after=()):
        return weight_terms(local, types, scalars, spans, head, tail, captions, after)

    w_local, i_local = terms(head, tail, (), True)
    w_down, i_down, down_a, down_b = terms(down_head, down_tail, (F32, BF16), after=(w_local,))
    w_two, i_two, two_a, two_b = terms(two_head, two_tail, (BF16, BF16), after=(down_b,))
    over_head = send(two_a, ring_route(1, 1))
    over_tail = send(two_b, ring_route(1, 3))
    w_up, i_up, up_a, up_b = terms(up_head, up_tail, (BF16, F32), after=(two_a,))
    block_shape = jax.ShapeDtypeStruct((8 * count, width), BF16)
    plus, minus = plain(
        combine_kernel,
        (block_shape, block_shape),
        (down_a, down_b, over_head, up_a, up_b, over_tail),
    )
    below = send(plus, ring_route(1, 1)).astype(F32)
    above = send(minus, ring_route(1, 3)).astype(F32)
    operands = [w_local, w_two, w_down, w_up, i_local, i_two, i_down, i_up]
    sum_flops = 2 * 32 * count * pair_rows * width
    cross, own_tail = plain(
        functools.partial(cross_kernel, 4),
        (
            jax.ShapeDtypeStruct((pair_rows, width), BF16),
            jax.ShapeDtypeStruct((pair_rows - slots, width), F32),
        ),
        operands,
        sum_flops,
        limit=24,
        after=(minus,),
    )
    crossed = send(cross, flip_route(2))
    own_part = plain(
        functools.partial(own_kernel, 4),
        jax.ShapeDtypeStruct((slots, width), F32),
        operands,
        sum_flops,
        limit=24,
        after=(cross,),
    )
    own_rows, back = plain(
        back_kernel,
        (
            jax.ShapeDtypeStruct((slots, width), F32),
            jax.ShapeDtypeStruct((slots, width), BF16),
        ),
        (total, own_part, own_tail, crossed),
        2 * pair_rows * slots * width,
        1,
        24,
    )
    returned = send(back, flip_route(0))
    half_sum = jax.ShapeDtypeStruct((4 * count, width), F32)
    local_a, local_b = plain(
        local_sums_kernel,
        (half_sum, half_sum),
        (w_local, captions),
        16 * count * 2 * pair_rows * width,
        after=(back,),
    )
    rows = 4 * count
    head_sum = local_a + below[:rows] + above[:rows]
    tail_sum = local_b + below[rows:] + above[rows:]

    near_rows = 2 * count
    pieces = {1: head_sum[near_rows:], 3: tail_sum[:near_rows], 2: tail_sum[near_rows:]}
    near_sum = head_sum[:near_rows]
    for k in (2, 1, 3):
        near_sum = near_sum + send(pieces[k].astype(BF16), ring_route(0, -k)).astype(F32)
    far_sum = send(near_sum[count:].astype(BF16), flip_route(4)).astype(F32)
    own_sum = near_sum[:count] + far_sum
    image_unit, image_inverse = unit_rows(image_embed)
    image_grad = (
        own_sum - image_unit * jnp.sum(image_unit * own_sum, axis=1, keepdims=True)
    ) * image_inverse

    caption_grad = caption_grads(total, caption_vectors, own_rows, returned)
    return image_grad, caption_grad


def solution(mesh):
    fine = Mesh(mesh.devices.reshape(SIZES), AXES)
    placed = (P(AXES, None), P(AXES, None), P(), P(), P())
    return jax.shard_map(
        program,
        mesh=fine,
        in_specs=placed,
        out_specs=(P(AXES, None), P(AXES, None)),
        check_vma=False,
    )
```

time: 148 us -> 157 us (1.061)
  the two profiles are of different devices: /device:TPU:6 before, /device:TPU:1 now
where the time goes in v1:
time: 157 us
  waiting for transfers between devices  81.9 us (52%)
  Pallas kernels  34.3 us (22%)
  starting transfers between devices  32 us (20%)
  other arithmetic  3.62 us (2%)
  local copies, waits for them, and re-layouts  3.04 us (2%)
  between operations  2.23 us (1%)
    ppermute x22, waiting for transfers between devices, send(): return lax.ppermute(value, AXES, pairs)  81.9 us
    ppermute x22, starting transfers between devices, send(): return lax.ppermute(value, AXES, pairs)  32 us
    pallas_call x4, Pallas kernels, weight_terms(): pl.pallas_call(lambda *refs: weight_kernel(local, bool(types), *refs[:ari...  17.1 us
    pallas_call x10, Pallas kernels, plain(): pl.pallas_call(lambda *refs: kernel(*refs[:len(args)], *refs[len(args) +...  14 us
    pallas_call x1, Pallas kernels, caption_grads(): pl.pallas_call(grad_kernel, grid=(steps,), out_shape=jax.ShapeDtypeStruct...  3.15 us
  transfers between devices with their start and end apart: 22, of which 10 were waited for; matrix products, arithmetic and copies ran while one was open for 2% of the time, Pallas kernels for 14%

profile of v1, /device:TPU:1, one launch (start us, length us, event | category | flops | bytes accessed | tf_op | source)
XLA Modules:
  0.0 157.1 jit_solution(6739767807249448406)
XLA Ops:
  0.6 2.2 %collective-permute-start.4 = (bf16[512,1152]{1,0:T(8,128)(2,1)}, bf16[512,1152]{1,0:T(8,128)(2,1)S(1)}, u32[]{:S(2)}, u32[]{:S(2)}) collective-permute-start(bf16[512,1152]{1,0:T(8,128)(2,1)} %raw_ref.1), channel_id=1, source_target_pairs={{0,64},{1,65},{2,66},{3,67},{4,68},{5,69},{6,70},{7,71},{8,72},{9,... | collective-permute-start | bytes 3538952 | tf_op jit(solution)/shard_map/ppermute | solution.py:63
  2.8 2.6 %collective-permute-start = (bf16[64,1152]{1,0:T(8,128)(2,1)}, bf16[64,1152]{1,0:T(8,128)(2,1)S(1)}, u32[]{:S(2)}, u32[]{:S(2)}) collective-permute-start(bf16[64,1152]{1,0:T(8,128)(2,1)} %refs_0_.1), channel_id=1, source_target_pairs={{0,1},{1,0},{2,3},{3,2},{4,5},{5,4},{6,7},{7,6},{8,9},{9,8},{10,11... | collective-permute-start | bytes 442376 | tf_op jit(solution)/shard_map/ppermute | solution.py:63
  5.4 28.8 %collective-permute-done.refs_1_ = bf16[64,1152]{1,0:T(8,128)(2,1)S(1)} collective-permute-done((bf16[64,1152]{1,0:T(8,128)(2,1)}, bf16[64,1152]{1,0:T(8,128)(2,1)S(1)}, u32[]{:S(2)}, u32[]{:S(2)}) %collective-permute-start) | collective-permute-done | bytes 147488 | tf_op jit(solution)/shard_map/ppermute | solution.py:63
  35.3 1.7 %collective-permute-start.1 = (bf16[128,1152]{1,0:T(8,128)(2,1)S(1)}, bf16[128,1152]{1,0:T(8,128)(2,1)S(1)}, u32[]{:S(2)}, u32[]{:S(2)}) collective-permute-start(bf16[128,1152]{1,0:T(8,128)(2,1)S(1)} %shard_map.68.refs_0_), channel_id=1, source_target_pairs={{0,16},{1,17},{2,18},{3,19},{4,20},{5,21},{6,22},{7,23},{8,10},{9,... | collective-permute-start | bytes 884744 | tf_op jit(solution)/shard_map/ppermute | solution.py:63
  37.0 2.2 %collective-permute-start.2 = (bf16[128,1152]{1,0:T(8,128)(2,1)S(1)}, bf16[128,1152]{1,0:T(8,128)(2,1)S(1)}, u32[]{:S(2)}, u32[]{:S(2)}) collective-permute-start(bf16[128,1152]{1,0:T(8,128)(2,1)S(1)} %shard_map.68.refs_0_), channel_id=1, source_target_pairs={{0,48},{1,49},{2,50},{3,51},{4,52},{5,53},{6,54},{7,55},{8,14},{9,... | collective-permute-start | bytes 884744 | tf_op jit(solution)/shard_map/ppermute | solution.py:63
  40.4 1.5 fusion.9
  41.9 1.3 copy-done
  44.3 1.7 %collective-permute-done.2.refs_2_ = bf16[128,1152]{1,0:T(8,128)(2,1)S(1)} collective-permute-done((bf16[128,1152]{1,0:T(8,128)(2,1)S(1)}, bf16[128,1152]{1,0:T(8,128)(2,1)S(1)}, u32[]{:S(2)}, u32[]{:S(2)}) %collective-permute-start.2) | collective-permute-done | bytes 294944 | tf_op jit(solution)/shard_map/ppermute | solution.py:63
  46.0 1.8 %collective-permute-done.3.refs_3_ = bf16[128,1152]{1,0:T(8,128)(2,1)S(1)} collective-permute-done((bf16[128,1152]{1,0:T(8,128)(2,1)S(1)}, bf16[128,1152]{1,0:T(8,128)(2,1)S(1)}, u32[]{:S(2)}, u32[]{:S(2)}) %collective-permute-start.3) | collective-permute-done | bytes 294944 | tf_op jit(solution)/shard_map/ppermute | solution.py:63
  47.9 1.9 %shard_map.71.refs_0_ = bf16[576,1152]{1,0:T(8,128)(2,1)S(1)} custom-call(s32[1]{0:T(128)} %bitcast.2.refs_0_.total_ref, bf16[576,1152]{1,0:T(8,128)(2,1)S(1)} %shard_map.69.refs_4_.refs_1_, bf16[512,1152]{1,0:T(8,128)(2,1)S(1)} %collective-permute-done.4.refs_2_, bf16[256,1152]{1,0:T(8,128)(2,1)S(1)} %get-tuple-element.26.refs_3_.refs_2_), custom_call_target="tpu_custom_call" | custom-call | flops 679477248 | bytes 1048576 | tf_op jit(solution)/shard_map/pallas_call | solution.py:87
  52.2 1.5 collective-permute-start.8
  54.6 6.8 %collective-permute-done.6.refs_2_ = bf16[256,1152]{1,0:T(8,128)(2,1)} collective-permute-done((bf16[256,1152]{1,0:T(8,128)(2,1)S(1)}, bf16[256,1152]{1,0:T(8,128)(2,1)}, u32[]{:S(2)}, u32[]{:S(2)}) %collective-permute-start.6) | collective-permute-done | bytes 589856 | tf_op jit(solution)/shard_map/ppermute | solution.py:63
  61.4 2.7 %collective-permute-start.9 = (bf16[256,1152]{1,0:T(8,128)(2,1)}, bf16[256,1152]{1,0:T(8,128)(2,1)}, u32[]{:S(2)}, u32[]{:S(2)}) collective-permute-start(bf16[256,1152]{1,0:T(8,128)(2,1)} %collective-permute-done.8.refs_3_), channel_id=1, source_target_pairs={{0,6},{1,7},{2,0},{3,1},{4,2},{5,3},{6,4},{7,5},{8,56},{9,57},{10,... | collective-permute-start | bytes 1769480 | tf_op jit(solution)/shard_map/ppermute | solution.py:63
  66.7 2.4 %block_local.1 = (bf16[512,1152]{1,0:T(8,128)(2,1)S(1)}, bf16[512,1152]{1,0:T(8,128)(2,1)S(1)}) custom-call(f32[2]{0:T(128)S(1)} %pad_maximum_fusion.refs_0_, s32[64,2]{1,0:T(8,128)S(1)} %copy.13.refs_1_, bf16[256,1152]{1,0:T(8,128)(2,1)S(1)} %get-tuple-element.26.refs_3_.refs_2_, bf16[256,1152]{1,0:T(8,128)(2,1)S(1)} %copy-done.5, ...), custom_call_target="tpu_custom_call" | custom-call | flops 1358954496 | bytes 8388608 | tf_op jit(solution)/shard_map/block_local/pallas_call | solution.py:161
  69.2 4.9 %block_remote.3 = (bf16[512,1152]{1,0:T(8,128)(2,1)S(1)}, bf16[512,1152]{1,0:T(8,128)(2,1)S(1)}, f32[256,1152]{1,0:T(8,128)S(1)}, bf16[256,1152]{1,0:T(8,128)(2,1)S(1)}) custom-call(f32[2]{0:T(128)S(1)} %pad_maximum_fusion.refs_0_, s32[64,2]{1,0:T(8,128)S(1)} %copy.13.refs_1_, bf16[256,1152]{1,0:T(8,128)(2,1)} %collective-permute-done.10.refs_2_, ...), custom_call_target="tpu_custom_call" | custom-call | flops 2717908992 | bytes 8388608 | tf_op jit(solution)/shard_map/block_remote/pallas_call | solution.py:161
  74.1 4.9 %block_remote.4 = (bf16[512,1152]{1,0:T(8,128)(2,1)S(1)}, bf16[512,1152]{1,0:T(8,128)(2,1)S(1)}, bf16[256,1152]{1,0:T(8,128)(2,1)S(1)}, bf16[256,1152]{1,0:T(8,128)(2,1)S(1)}) custom-call(f32[2]{0:T(128)S(1)} %pad_maximum_fusion.refs_0_, s32[64,2]{1,0:T(8,128)S(1)} %copy.13.refs_1_, bf16[256,1152]{1,0:T(8,128)(2,1)} %collective-permute-done.7.refs_2_, ...), custom_call_target="tpu_custom_call" | custom-call | flops 2717908992 | bytes 8388608 | tf_op jit(solution)/shard_map/block_remote/pallas_call | solution.py:161
  79.2 2.7 %collective-permute-start.13 = (bf16[256,1152]{1,0:T(8,128)(2,1)S(1)}, bf16[256,1152]{1,0:T(8,128)(2,1)S(1)}, u32[]{:S(2)}, u32[]{:S(2)}) collective-permute-start(bf16[256,1152]{1,0:T(8,128)(2,1)S(1)} %get-tuple-element.41), channel_id=1, source_target_pairs={{0,6},{1,7},{2,0},{3,1},{4,2},{5,3},{6,4},{7,5},{8,56},{9,57},{10,... | collective-permute-start | bytes 1769480 | tf_op jit(solution)/shard_map/ppermute | solution.py:63
  82.0 4.8 %block_remote.5 = (bf16[512,1152]{1,0:T(8,128)(2,1)S(1)}, bf16[512,1152]{1,0:T(8,128)(2,1)S(1)}, bf16[256,1152]{1,0:T(8,128)(2,1)S(1)}, f32[256,1152]{1,0:T(8,128)S(1)}) custom-call(f32[2]{0:T(128)S(1)} %pad_maximum_fusion.refs_0_, s32[64,2]{1,0:T(8,128)S(1)} %copy.13.refs_1_, bf16[256,1152]{1,0:T(8,128)(2,1)} %collective-permute-done.6.refs_2_, ...), custom_call_target="tpu_custom_call" | custom-call | flops 2717908992 | bytes 8388608 | tf_op jit(solution)/shard_map/block_remote/pallas_call | solution.py:161
  86.7 2.6 %collective-permute-done.12.refs_2_ = bf16[256,1152]{1,0:T(8,128)(2,1)S(1)} collective-permute-done((bf16[256,1152]{1,0:T(8,128)(2,1)S(1)}, bf16[256,1152]{1,0:T(8,128)(2,1)S(1)}, u32[]{:S(2)}, u32[]{:S(2)}) %collective-permute-start.12) | collective-permute-done | bytes 589856 | tf_op jit(solution)/shard_map/ppermute | solution.py:63
  89.7 3.6 %shard_map.74 = (bf16[576,1152]{1,0:T(8,128)(2,1)S(1)}, f32[64,1152]{1,0:T(8,128)S(1)}) custom-call(bf16[512,1152]{1,0:T(8,128)(2,1)S(1)} %get-tuple-element.28.refs_5_.refs_0_, bf16[512,1152]{1,0:T(8,128)(2,1)S(1)} %get-tuple-element.30.refs_1_, bf16[512,1152]{1,0:T(8,128)(2,1)S(1)} %get-tuple-element.31.refs_2_, ...), custom_call_target="tpu_custom_call" | custom-call | flops 2717908992 | bytes 1048576 | tf_op jit(solution)/shard_map/pallas_call | solution.py:87
  93.3 3.3 %collective-permute-start.14 = (bf16[576,1152]{1,0:T(8,128)(2,1)S(1)}, bf16[576,1152]{1,0:T(8,128)(2,1)S(1)}, u32[]{:S(2)}, u32[]{:S(2)}) collective-permute-start(bf16[576,1152]{1,0:T(8,128)(2,1)S(1)} %get-tuple-element.43.refs_8_), channel_id=1, source_target_pairs={{0,8},{1,9},{2,10},{3,11},{4,12},{5,13},{6,14},{7,15},{8,0},{9,1},... | collective-permute-start | bytes 3981320 | tf_op jit(solution)/shard_map/ppermute | solution.py:63
  97.8 1.5 collective-permute-start.16
  99.3 2.9 %shard_map.75.refs_1_ = f32[512,1152]{1,0:T(8,128)S(1)} custom-call(bf16[512,1152]{1,0:T(8,128)(2,1)S(1)} %get-tuple-element.28.refs_5_.refs_0_, bf16[512,1152]{1,0:T(8,128)(2,1)S(1)} %get-tuple-element.30.refs_1_, bf16[512,1152]{1,0:T(8,128)(2,1)S(1)} %get-tuple-element.31.refs_2_, bf16[512,1152]{1,0:T(8,128)(2,1)S(1)} %get-tuple-element.33.refs_3_, ...), custom_call_target="tpu_custom_call" | custom-call | flops 2717908992 | bytes 1048576 | tf_op jit(solution)/shard_map/pallas_call | solution.py:87
  102.2 10.9 %collective-permute-done.15 = bf16[512,1152]{1,0:T(8,128)(2,1)S(1)} collective-permute-done((bf16[512,1152]{1,0:T(8,128)(2,1)S(1)}, bf16[512,1152]{1,0:T(8,128)(2,1)S(1)}, u32[]{:S(2)}, u32[]{:S(2)}) %collective-permute-start.15) | collective-permute-done | bytes 1179680 | tf_op jit(solution)/shard_map/ppermute | solution.py:63
  113.5 1.8 %shard_map.76 = (f32[512,1152]{1,0:T(8,128)S(1)}, bf16[512,1152]{1,0:T(8,128)(2,1)S(1)}) custom-call(s32[1]{0:T(128)} %bitcast.2.refs_0_.total_ref, f32[512,1152]{1,0:T(8,128)S(1)} %shard_map.75.refs_1_, f32[64,1152]{1,0:T(8,128)S(1)} %get-tuple-element.44.refs_2_, bf16[576,1152]{1,0:T(8,128)(2,1)S(1)} %collective-permute-done.14.refs_3_), custom_call_target="tpu_custom_call" | custom-call | flops 679477248 | bytes 1048576 | tf_op jit(solution)/shard_map/pallas_call | solution.py:87
  115.4 1.8 %shard_map.77 = (f32[256,1152]{1,0:T(8,128)S(1)}, f32[256,1152]{1,0:T(8,128)S(1)}) custom-call(bf16[512,1152]{1,0:T(8,128)(2,1)S(1)} %get-tuple-element.28.refs_5_.refs_0_, bf16[1152,1152]{1,0:T(8,128)(2,1)S(1)} %shard_map.72.refs_4_.refs_1_, bf16[512,1152]{1,0:T(8,128)(2,1)S(1)} %get-tuple-element.45.refs_2_), custom_call_target="tpu_custom_call" | custom-call | flops 1358954496 | bytes 1048576 | tf_op jit(solution)/shard_map/pallas_call | solution.py:87
  117.6 2.4 %collective-permute-start.17 = (bf16[128,1152]{1,0:T(8,128)(2,1)S(1)}, bf16[128,1152]{1,0:T(8,128)(2,1)S(1)}, u32[]{:S(2)}, u32[]{:S(2)}) collective-permute-start(bf16[128,1152]{1,0:T(8,128)(2,1)S(1)} %get-tuple-element.54), channel_id=1, source_target_pairs={{0,32},{1,33},{2,34},{3,35},{4,36},{5,37},{6,38},{7,39},{8,12},{9,... | collective-permute-start | bytes 884744 | tf_op jit(solution)/shard_map/ppermute | solution.py:63
  121.3 1.6 collective-permute-start.18
  123.0 2.0 %collective-permute-done.17 = bf16[128,1152]{1,0:T(8,128)(2,1)S(1)} collective-permute-done((bf16[128,1152]{1,0:T(8,128)(2,1)S(1)}, bf16[128,1152]{1,0:T(8,128)(2,1)S(1)}, u32[]{:S(2)}, u32[]{:S(2)}) %collective-permute-start.17) | collective-permute-done | bytes 294944 | tf_op jit(solution)/shard_map/ppermute | solution.py:63
  125.1 3.2 %collective-permute-done.19 = bf16[128,1152]{1,0:T(8,128)(2,1)S(1)} collective-permute-done((bf16[128,1152]{1,0:T(8,128)(2,1)S(1)}, bf16[128,1152]{1,0:T(8,128)(2,1)S(1)}, u32[]{:S(2)}, u32[]{:S(2)}) %collective-permute-start.19) | collective-permute-done | bytes 294944 | tf_op jit(solution)/shard_map/ppermute | solution.py:63
  129.4 23.5 %collective-permute-done.20 = bf16[64,1152]{1,0:T(8,128)(2,1)S(1)} collective-permute-done((bf16[64,1152]{1,0:T(8,128)(2,1)S(1)}, bf16[64,1152]{1,0:T(8,128)(2,1)S(1)}, u32[]{:S(2)}, u32[]{:S(2)}) %collective-permute-start.20) | collective-permute-done | bytes 147488 | tf_op jit(solution)/shard_map/ppermute | solution.py:63
  153.9 3.2 %caption_grad.1 = f32[512,1152]{1,0:T(8,128)} custom-call(s32[1]{0:T(128)} %bitcast.2.refs_0_.total_ref, bf16[512,1152]{1,0:T(8,128)(2,1)S(1)} %copy-done.1, f32[512,1152]{1,0:T(8,128)S(1)} %get-tuple-element.49.own_ref, bf16[512,1152]{1,0:T(8,128)(2,1)S(1)} %collective-permute-done.21.back_ref), custom_call_target="tpu_custom_call" | custom-call | flops 4718592 | bytes 4194304 | tf_op jit(solution)/shard_map/caption_grad/pallas_call | solution.py:246
  (56 shorter events, 13.9 us)
Async XLA Ops:
  0.6 47.3 %collective-permute-start.4 = (bf16[512,1152]{1,0:T(8,128)(2,1)}, bf16[512,1152]{1,0:T(8,128)(2,1)S(1)}, u32[]{:S(2)}, u32[]{:S(2)}) collective-permute-start(bf16[512,1152]{1,0:T(8,128)(2,1)} %raw_ref.1), channel_id=1, source_target_pairs={{0,64},{1,65},{2,66},{3,67},{4,68},{5,69},{6,70},{7,71},{8,72},{9,... | collective-permute-start | bytes 3538952 | tf_op jit(solution)/shard_map/ppermute | solution.py:63
  2.8 31.4 %collective-permute-start = (bf16[64,1152]{1,0:T(8,128)(2,1)}, bf16[64,1152]{1,0:T(8,128)(2,1)S(1)}, u32[]{:S(2)}, u32[]{:S(2)}) collective-permute-start(bf16[64,1152]{1,0:T(8,128)(2,1)} %refs_0_.1), channel_id=1, source_target_pairs={{0,1},{1,0},{2,3},{3,2},{4,5},{5,4},{6,7},{7,6},{8,9},{9,8},{10,11... | collective-permute-start | bytes 442376 | tf_op jit(solution)/shard_map/ppermute | solution.py:63
  34.2 0.9 copy-start.2
  35.3 9.0 %collective-permute-start.1 = (bf16[128,1152]{1,0:T(8,128)(2,1)S(1)}, bf16[128,1152]{1,0:T(8,128)(2,1)S(1)}, u32[]{:S(2)}, u32[]{:S(2)}) collective-permute-start(bf16[128,1152]{1,0:T(8,128)(2,1)S(1)} %shard_map.68.refs_0_), channel_id=1, source_target_pairs={{0,16},{1,17},{2,18},{3,19},{4,20},{5,21},{6,22},{7,23},{8,10},{9,... | collective-permute-start | bytes 884744 | tf_op jit(solution)/shard_map/ppermute | solution.py:63
  37.0 9.0 %collective-permute-start.2 = (bf16[128,1152]{1,0:T(8,128)(2,1)S(1)}, bf16[128,1152]{1,0:T(8,128)(2,1)S(1)}, u32[]{:S(2)}, u32[]{:S(2)}) collective-permute-start(bf16[128,1152]{1,0:T(8,128)(2,1)S(1)} %shard_map.68.refs_0_), channel_id=1, source_target_pairs={{0,48},{1,49},{2,50},{3,51},{4,52},{5,53},{6,54},{7,55},{8,14},{9,... | collective-permute-start | bytes 884744 | tf_op jit(solution)/shard_map/ppermute | solution.py:63
  39.2 8.7 %collective-permute-start.3 = (bf16[128,1152]{1,0:T(8,128)(2,1)S(1)}, bf16[128,1152]{1,0:T(8,128)(2,1)S(1)}, u32[]{:S(2)}, u32[]{:S(2)}) collective-permute-start(bf16[128,1152]{1,0:T(8,128)(2,1)S(1)} %shard_map.68.refs_0_), channel_id=1, source_target_pairs={{0,32},{1,33},{2,34},{3,35},{4,36},{5,37},{6,38},{7,39},{8,12},{9,... | collective-permute-start | bytes 884744 | tf_op jit(solution)/shard_map/ppermute | solution.py:63
  41.9 1.3 copy-start
  47.9 16.2 %copy-start.4 = (bf16[256,1152]{1,0:T(8,128)(2,1)}, bf16[256,1152]{1,0:T(8,128)(2,1)S(1)}, u32[]{:S(2)}) copy-start(bf16[256,1152]{1,0:T(8,128)(2,1)S(1)} %get-tuple-element.27.refs_3_) | copy-start | bytes 1769476
  49.9 16.0 %collective-permute-start.5 = (bf16[576,1152]{1,0:T(8,128)(2,1)S(1)}, bf16[576,1152]{1,0:T(8,128)(2,1)S(1)}, u32[]{:S(2)}, u32[]{:S(2)}) collective-permute-start(bf16[576,1152]{1,0:T(8,128)(2,1)S(1)} %shard_map.71.refs_0_), channel_id=1, source_target_pairs={{0,8},{1,9},{2,10},{3,11},{4,12},{5,13},{6,14},{7,15},{8,0},{9,1},... | collective-permute-start | bytes 3981320 | tf_op jit(solution)/shard_map/ppermute | solution.py:63
  51.1 10.3 %collective-permute-start.6 = (bf16[256,1152]{1,0:T(8,128)(2,1)S(1)}, bf16[256,1152]{1,0:T(8,128)(2,1)}, u32[]{:S(2)}, u32[]{:S(2)}) collective-permute-start(bf16[256,1152]{1,0:T(8,128)(2,1)S(1)} %get-tuple-element.26.refs_3_.refs_2_), channel_id=1, source_target_pairs={{0,2},{1,3},{2,4},{3,5},{4,6},{5,7},{6,0},{7,1},{8,24},{9,25},{10,... | collective-permute-start | bytes 1769480 | tf_op jit(solution)/shard_map/ppermute | solution.py:63
  52.2 9.2 %collective-permute-start.8 = (bf16[256,1152]{1,0:T(8,128)(2,1)S(1)}, bf16[256,1152]{1,0:T(8,128)(2,1)}, u32[]{:S(2)}, u32[]{:S(2)}) collective-permute-start(bf16[256,1152]{1,0:T(8,128)(2,1)S(1)} %get-tuple-element.27.refs_3_), channel_id=1, source_target_pairs={{0,6},{1,7},{2,0},{3,1},{4,2},{5,3},{6,4},{7,5},{8,56},{9,57},{10,... | collective-permute-start | bytes 1769480 | tf_op jit(solution)/shard_map/ppermute | solution.py:63
  53.8 15.4 %collective-permute-start.10 = (bf16[256,1152]{1,0:T(8,128)(2,1)S(1)}, bf16[256,1152]{1,0:T(8,128)(2,1)}, u32[]{:S(2)}, u32[]{:S(2)}) collective-permute-start(bf16[256,1152]{1,0:T(8,128)(2,1)S(1)} %get-tuple-element.26.refs_3_.refs_2_), channel_id=1, source_target_pairs={{0,6},{1,7},{2,0},{3,1},{4,2},{5,3},{6,4},{7,5},{8,56},{9,57},{10,... | collective-permute-start | bytes 1769480 | tf_op jit(solution)/shard_map/ppermute | solution.py:63
  61.4 12.7 %collective-permute-start.7 = (bf16[256,1152]{1,0:T(8,128)(2,1)}, bf16[256,1152]{1,0:T(8,128)(2,1)}, u32[]{:S(2)}, u32[]{:S(2)}) collective-permute-start(bf16[256,1152]{1,0:T(8,128)(2,1)} %collective-permute-done.6.refs_2_), channel_id=1, source_target_pairs={{0,2},{1,3},{2,4},{3,5},{4,6},{5,7},{6,0},{7,1},{8,24},{9,25},{10,... | collective-permute-start | bytes 1769480 | tf_op jit(solution)/shard_map/ppermute | solution.py:63
  61.4 12.7 %collective-permute-start.9 = (bf16[256,1152]{1,0:T(8,128)(2,1)}, bf16[256,1152]{1,0:T(8,128)(2,1)}, u32[]{:S(2)}, u32[]{:S(2)}) collective-permute-start(bf16[256,1152]{1,0:T(8,128)(2,1)} %collective-permute-done.8.refs_3_), channel_id=1, source_target_pairs={{0,6},{1,7},{2,0},{3,1},{4,2},{5,3},{6,4},{7,5},{8,56},{9,57},{10,... | collective-permute-start | bytes 1769480 | tf_op jit(solution)/shard_map/ppermute | solution.py:63
  65.6 1.1 copy-start.5
  65.6 16.3 %collective-permute-start.11 = (bf16[256,1152]{1,0:T(8,128)(2,1)}, bf16[256,1152]{1,0:T(8,128)(2,1)S(1)}, u32[]{:S(2)}, u32[]{:S(2)}) collective-permute-start(bf16[256,1152]{1,0:T(8,128)(2,1)} %copy-done.4), channel_id=1, source_target_pairs={{0,2},{1,3},{2,4},{3,5},{4,6},{5,7},{6,0},{7,1},{8,24},{9,25},{10,... | collective-permute-start | bytes 1769480 | tf_op jit(solution)/shard_map/ppermute | solution.py:63
  79.1 10.3 %collective-permute-start.12 = (bf16[256,1152]{1,0:T(8,128)(2,1)S(1)}, bf16[256,1152]{1,0:T(8,128)(2,1)S(1)}, u32[]{:S(2)}, u32[]{:S(2)}) collective-permute-start(bf16[256,1152]{1,0:T(8,128)(2,1)S(1)} %get-tuple-element.32.refs_5_), channel_id=1, source_target_pairs={{0,2},{1,3},{2,4},{3,5},{4,6},{5,7},{6,0},{7,1},{8,24},{9,25},{10,... | collective-permute-start | bytes 1769480 | tf_op jit(solution)/shard_map/ppermute | solution.py:63
  79.2 10.1 %collective-permute-start.13 = (bf16[256,1152]{1,0:T(8,128)(2,1)S(1)}, bf16[256,1152]{1,0:T(8,128)(2,1)S(1)}, u32[]{:S(2)}, u32[]{:S(2)}) collective-permute-start(bf16[256,1152]{1,0:T(8,128)(2,1)S(1)} %get-tuple-element.41), channel_id=1, source_target_pairs={{0,6},{1,7},{2,0},{3,1},{4,2},{5,3},{6,4},{7,5},{8,56},{9,57},{10,... | collective-permute-start | bytes 1769480 | tf_op jit(solution)/shard_map/ppermute | solution.py:63
  93.3 20.2 %collective-permute-start.14 = (bf16[576,1152]{1,0:T(8,128)(2,1)S(1)}, bf16[576,1152]{1,0:T(8,128)(2,1)S(1)}, u32[]{:S(2)}, u32[]{:S(2)}) collective-permute-start(bf16[576,1152]{1,0:T(8,128)(2,1)S(1)} %get-tuple-element.43.refs_8_), channel_id=1, source_target_pairs={{0,8},{1,9},{2,10},{3,11},{4,12},{5,13},{6,14},{7,15},{8,0},{9,1},... | collective-permute-start | bytes 3981320 | tf_op jit(solution)/shard_map/ppermute | solution.py:63
  96.6 16.6 %collective-permute-start.15 = (bf16[512,1152]{1,0:T(8,128)(2,1)S(1)}, bf16[512,1152]{1,0:T(8,128)(2,1)S(1)}, u32[]{:S(2)}, u32[]{:S(2)}) collective-permute-start(bf16[512,1152]{1,0:T(8,128)(2,1)S(1)} %get-tuple-element.47), channel_id=1, source_target_pairs={{0,2},{1,3},{2,4},{3,5},{4,6},{5,7},{6,0},{7,1},{8,24},{9,25},{10,... | collective-permute-start | bytes 3538952 | tf_op jit(solution)/shard_map/ppermute | solution.py:63
  97.8 15.6 %collective-permute-start.16 = (bf16[512,1152]{1,0:T(8,128)(2,1)S(1)}, bf16[512,1152]{1,0:T(8,128)(2,1)S(1)}, u32[]{:S(2)}, u32[]{:S(2)}) collective-permute-start(bf16[512,1152]{1,0:T(8,128)(2,1)S(1)} %get-tuple-element.42.refs_8_), channel_id=1, source_target_pairs={{0,6},{1,7},{2,0},{3,1},{4,2},{5,3},{6,4},{7,5},{8,56},{9,57},{10,... | collective-permute-start | bytes 3538952 | tf_op jit(solution)/shard_map/ppermute | solution.py:63
  117.5 5.3 %copy-start.3 = (bf16[64,1152]{1,0:T(8,128)(2,1)S(1)}, bf16[64,1152]{1,0:T(8,128)(2,1)}, u32[]{:S(2)}) copy-start(bf16[64,1152]{1,0:T(8,128)(2,1)} %refs_0_.1) | copy-start | bytes 442372
  117.6 7.5 %collective-permute-start.17 = (bf16[128,1152]{1,0:T(8,128)(2,1)S(1)}, bf16[128,1152]{1,0:T(8,128)(2,1)S(1)}, u32[]{:S(2)}, u32[]{:S(2)}) collective-permute-start(bf16[128,1152]{1,0:T(8,128)(2,1)S(1)} %get-tuple-element.54), channel_id=1, source_target_pairs={{0,32},{1,33},{2,34},{3,35},{4,36},{5,37},{6,38},{7,39},{8,12},{9,... | collective-permute-start | bytes 884744 | tf_op jit(solution)/shard_map/ppermute | solution.py:63
  120.0 8.2 %collective-permute-start.19 = (bf16[128,1152]{1,0:T(8,128)(2,1)S(1)}, bf16[128,1152]{1,0:T(8,128)(2,1)S(1)}, u32[]{:S(2)}, u32[]{:S(2)}) collective-permute-start(bf16[128,1152]{1,0:T(8,128)(2,1)S(1)} %get-tuple-element.55), channel_id=1, source_target_pairs={{0,16},{1,17},{2,18},{3,19},{4,20},{5,21},{6,22},{7,23},{8,10},{9,... | collective-permute-start | bytes 884744 | tf_op jit(solution)/shard_map/ppermute | solution.py:63
  121.3 7.5 %collective-permute-start.18 = (bf16[128,1152]{1,0:T(8,128)(2,1)S(1)}, bf16[128,1152]{1,0:T(8,128)(2,1)S(1)}, u32[]{:S(2)}, u32[]{:S(2)}) collective-permute-start(bf16[128,1152]{1,0:T(8,128)(2,1)S(1)} %slice.76), channel_id=1, source_target_pairs={{0,48},{1,49},{2,50},{3,51},{4,52},{5,53},{6,54},{7,55},{8,14},{9,... | collective-permute-start | bytes 884744 | tf_op jit(solution)/shard_map/ppermute | solution.py:63
  122.9 31.0 %collective-permute-start.21 = (bf16[512,1152]{1,0:T(8,128)(2,1)S(1)}, bf16[512,1152]{1,0:T(8,128)(2,1)S(1)}, u32[]{:S(2)}, u32[]{:S(2)}) collective-permute-start(bf16[512,1152]{1,0:T(8,128)(2,1)S(1)} %get-tuple-element.45.refs_2_), channel_id=1, source_target_pairs={{0,64},{1,65},{2,66},{3,67},{4,68},{5,69},{6,70},{7,71},{8,72},{9,... | collective-permute-start | bytes 3538952 | tf_op jit(solution)/shard_map/ppermute | solution.py:63
  128.9 25.0 %copy-start.1 = (bf16[512,1152]{1,0:T(8,128)(2,1)S(1)}, bf16[512,1152]{1,0:T(8,128)(2,1)}, u32[]{:S(2)}) copy-start(bf16[512,1152]{1,0:T(8,128)(2,1)} %raw_ref.1) | copy-start | bytes 3538948
  128.9 23.9 %collective-permute-start.20 = (bf16[64,1152]{1,0:T(8,128)(2,1)S(1)}, bf16[64,1152]{1,0:T(8,128)(2,1)S(1)}, u32[]{:S(2)}, u32[]{:S(2)}) collective-permute-start(bf16[64,1152]{1,0:T(8,128)(2,1)S(1)} %slice.77), channel_id=1, source_target_pairs={{0,1},{1,0},{2,3},{3,2},{4,5},{5,4},{6,7},{7,6},{8,9},{9,8},{10,11... | collective-permute-start | bytes 442376 | tf_op jit(solution)/shard_map/ppermute | solution.py:63

commit v2 on v1

--- a/solution.py
+++ b/solution.py
@@ -218,36 +218,44 @@
     minus_ref[rows:] = (up_b[...] + over_tail[...].astype(F32)).astype(BF16)
 
 
-def back_kernel(total_ref, own_ref, tail_ref, cross_ref, pair_ref, back_ref):
+def back_kernel(own_ref, tail_ref, cross_ref, pair_ref, back_a, back_b):
     slots, rest = own_ref.shape[0], tail_ref.shape[0]
     pair = own_ref[...] + cross_ref[:slots].astype(F32)
     tail = tail_ref[...] + cross_ref[slots:].astype(F32)
+    first = back_a.shape[0]
     pair_ref[...] = pair
-    offset = total_ref[0]
-    back_ref[...] = (
-        picked(slots, slots, offset, pair.astype(BF16))
-        + picked(slots, rest, offset - slots, tail.astype(BF16))
-    ).astype(BF16)
-
-
-def grad_kernel(total_ref, raw_ref, own_ref, back_ref, out_ref):
+    back_a[...] = pair[rest : rest + first].astype(BF16)
+    back_b[: slots - rest - first] = pair[rest + first :].astype(BF16)
+    back_b[slots - rest - first :] = tail.astype(BF16)
+
+
+def home_kernel(total_ref, own_ref, back_ref, out_ref):
+    slots = own_ref.shape[0]
+    out_ref[...] = own_ref[...] + picked(
+        slots, back_ref.shape[0], slots - total_ref[0], back_ref[...]
+    )
+
+
+def grad_kernel(skip, total_ref, raw_ref, own_ref, back_ref, out_ref):
     rows = out_ref.shape[0]
+    start = pl.program_id(0) * rows
     unit, inverse = unit_rows(raw_ref[...])
-    sums = own_ref[...] + back_ref[...].astype(F32)
+    offset = start + pl.num_programs(0) * rows - total_ref[0] - skip
+    sums = own_ref[...] + picked(rows, back_ref.shape[0], offset, back_ref[...])
     grads = (sums - unit * jnp.sum(unit * sums, axis=1, keepdims=True)) * inverse
-    slot = pl.program_id(0) * rows + lax.broadcasted_iota(jnp.int32, grads.shape, 0)
+    slot = start + lax.broadcasted_iota(jnp.int32, grads.shape, 0)
     out_ref[...] = jnp.where(slot < total_ref[0], grads, 0.0)
 
 
-def caption_grads(total, raw, own_rows, back):
+def caption_grads(skip, total, raw, own_rows, back):
     slots, width = raw.shape
     steps = 4
     some = pl.BlockSpec((slots // steps, width), lambda i: (i, 0))
     return pl.pallas_call(
-        grad_kernel,
+        functools.partial(grad_kernel, skip),
         grid=(steps,),
         out_shape=jax.ShapeDtypeStruct((slots, width), F32),
-        in_specs=[SMEM, some, some, some],
+        in_specs=[SMEM, some, some, pl.BlockSpec(back.shape, lambda i: (0, 0))],
         out_specs=some,
         compiler_params=pltpu.CompilerParams(vmem_limit_bytes=16 * MIB),
         cost_estimate=pl.CostEstimate(
@@ -320,14 +328,6 @@
     over_head = send(two_a, ring_route(1, 1))
     over_tail = send(two_b, ring_route(1, 3))
     w_up, i_up, up_a, up_b = terms(up_head, up_tail, (BF16, F32), after=(two_a,))
-    block_shape = jax.ShapeDtypeStruct((8 * count, width), BF16)
-    plus, minus = plain(
-        combine_kernel,
-        (block_shape, block_shape),
-        (down_a, down_b, over_head, up_a, up_b, over_tail),
-    )
-    below = send(plus, ring_route(1, 1)).astype(F32)
-    above = send(minus, ring_route(1, 3)).astype(F32)
     operands = [w_local, w_two, w_down, w_up, i_local, i_two, i_down, i_up]
     sum_flops = 2 * 32 * count * pair_rows * width
     cross, own_tail = plain(
@@ -339,36 +339,46 @@
         operands,
         sum_flops,
         limit=24,
-        after=(minus,),
+        after=(up_a,),
     )
     crossed = send(cross, flip_route(2))
+    block_shape = jax.ShapeDtypeStruct((8 * count, width), BF16)
+    plus, minus = plain(
+        combine_kernel,
+        (block_shape, block_shape),
+        (down_a, down_b, over_head, up_a, up_b, over_tail),
+        after=(cross,),
+    )
+    below = send(plus, ring_route(1, 1)).astype(F32)
+    above = send(minus, ring_route(1, 3)).astype(F32)
     own_part = plain(
         functools.partial(own_kernel, 4),
         jax.ShapeDtypeStruct((slots, width), F32),
         operands,
         sum_flops,
         limit=24,
-        after=(cross,),
-    )
-    own_rows, back = plain(
+        after=(minus,),
+    )
+    last = slots // 4
+    pair, back_a, back_b = plain(
         back_kernel,
         (
             jax.ShapeDtypeStruct((slots, width), F32),
-            jax.ShapeDtypeStruct((slots, width), BF16),
-        ),
-        (total, own_part, own_tail, crossed),
-        2 * pair_rows * slots * width,
-        1,
-        24,
-    )
-    returned = send(back, flip_route(0))
+            jax.ShapeDtypeStruct((slots - last, width), BF16),
+            jax.ShapeDtypeStruct((last, width), BF16),
+        ),
+        (own_part, own_tail, crossed),
+        limit=24,
+    )
+    returned_a = send(back_a, flip_route(0))
+    returned_b = send(back_b, flip_route(0))
     half_sum = jax.ShapeDtypeStruct((4 * count, width), F32)
     local_a, local_b = plain(
         local_sums_kernel,
         (half_sum, half_sum),
         (w_local, captions),
         16 * count * 2 * pair_rows * width,
-        after=(back,),
+        after=(back_a,),
     )
     rows = 4 * count
     head_sum = local_a + below[:rows] + above[:rows]
@@ -386,7 +396,14 @@
         own_sum - image_unit * jnp.sum(image_unit * own_sum, axis=1, keepdims=True)
     ) * image_inverse
 
-    caption_grad = caption_grads(total, caption_vectors, own_rows, returned)
+    own_rows = plain(
+        home_kernel,
+        jax.ShapeDtypeStruct((slots, width), F32),
+        (total, pair, returned_a),
+        2 * slots * slots * width,
+        1,
+    )
+    caption_grad = caption_grads(slots - last, total, caption_vectors, own_rows, returned_b)
     return image_grad, caption_grad
 
 

time: 157 us -> 149 us (0.949)
  the two profiles are of different devices: /device:TPU:1 before, /device:TPU:0 now
where the time goes in v2:
time: 149 us; the launch traced here: 148 us
  waiting for transfers between devices  70.9 us (48%)
  Pallas kernels  34.7 us (23%)
  starting transfers between devices  33.9 us (23%)
  other arithmetic  3.54 us (2%)
  local copies, waits for them, and re-layouts  3.04 us (2%)
  between operations  2.26 us (2%)
    ppermute x23, waiting for transfers between devices, send(): return lax.ppermute(value, AXES, pairs)  70.9 us
    ppermute x23, starting transfers between devices, send(): return lax.ppermute(value, AXES, pairs)  33.9 us
    pallas_call x4, Pallas kernels, weight_terms(): pl.pallas_call(lambda *refs: weight_kernel(local, bool(types), *refs[:ari...  17.1 us
    pallas_call x11, Pallas kernels, plain(): pl.pallas_call(lambda *refs: kernel(*refs[:len(args)], *refs[len(args) +...  14.1 us
    pallas_call x1, Pallas kernels, caption_grads(): pl.pallas_call(functools.partial(grad_kernel, skip), grid=(steps,), out_s...  3.52 us
  transfers between devices with their start and end apart: 23, of which 9 were waited for; matrix products, arithmetic and copies ran while one was open for 1% of the time, Pallas kernels for 22%

profile of v2, /device:TPU:0, one launch (start us, length us, event | category | flops | bytes accessed | tf_op | source)
XLA Modules:
  0.0 148.3 jit_solution(16933372433052833916)
XLA Ops:
  0.6 1.8 %collective-permute-start.4 = (bf16[512,1152]{1,0:T(8,128)(2,1)}, bf16[512,1152]{1,0:T(8,128)(2,1)S(1)}, u32[]{:S(2)}, u32[]{:S(2)}) collective-permute-start(bf16[512,1152]{1,0:T(8,128)(2,1)} %raw_ref.1), channel_id=1, source_target_pairs={{0,64},{1,65},{2,66},{3,67},{4,68},{5,69},{6,70},{7,71},{8,72},{9,... | collective-permute-start | bytes 3538952 | tf_op jit(solution)/shard_map/ppermute | solution.py:63
  2.4 2.9 %collective-permute-start = (bf16[64,1152]{1,0:T(8,128)(2,1)}, bf16[64,1152]{1,0:T(8,128)(2,1)S(1)}, u32[]{:S(2)}, u32[]{:S(2)}) collective-permute-start(bf16[64,1152]{1,0:T(8,128)(2,1)} %refs_0_.1), channel_id=1, source_target_pairs={{0,1},{1,0},{2,3},{3,2},{4,5},{5,4},{6,7},{7,6},{8,9},{9,8},{10,11... | collective-permute-start | bytes 442376 | tf_op jit(solution)/shard_map/ppermute | solution.py:63
  5.3 29.1 %collective-permute-done.refs_1_ = bf16[64,1152]{1,0:T(8,128)(2,1)S(1)} collective-permute-done((bf16[64,1152]{1,0:T(8,128)(2,1)}, bf16[64,1152]{1,0:T(8,128)(2,1)S(1)}, u32[]{:S(2)}, u32[]{:S(2)}) %collective-permute-start) | collective-permute-done | bytes 147488 | tf_op jit(solution)/shard_map/ppermute | solution.py:63
  35.4 1.6 %collective-permute-start.1 = (bf16[128,1152]{1,0:T(8,128)(2,1)S(1)}, bf16[128,1152]{1,0:T(8,128)(2,1)S(1)}, u32[]{:S(2)}, u32[]{:S(2)}) collective-permute-start(bf16[128,1152]{1,0:T(8,128)(2,1)S(1)} %shard_map.68.refs_0_), channel_id=1, source_target_pairs={{0,16},{1,17},{2,18},{3,19},{4,20},{5,21},{6,22},{7,23},{8,10},{9,... | collective-permute-start | bytes 884744 | tf_op jit(solution)/shard_map/ppermute | solution.py:63
  37.0 1.7 %collective-permute-start.2 = (bf16[128,1152]{1,0:T(8,128)(2,1)S(1)}, bf16[128,1152]{1,0:T(8,128)(2,1)S(1)}, u32[]{:S(2)}, u32[]{:S(2)}) collective-permute-start(bf16[128,1152]{1,0:T(8,128)(2,1)S(1)} %shard_map.68.refs_0_), channel_id=1, source_target_pairs={{0,48},{1,49},{2,50},{3,51},{4,52},{5,53},{6,54},{7,55},{8,14},{9,... | collective-permute-start | bytes 884744 | tf_op jit(solution)/shard_map/ppermute | solution.py:63
  38.7 1.8 %collective-permute-start.3 = (bf16[128,1152]{1,0:T(8,128)(2,1)S(1)}, bf16[128,1152]{1,0:T(8,128)(2,1)S(1)}, u32[]{:S(2)}, u32[]{:S(2)}) collective-permute-start(bf16[128,1152]{1,0:T(8,128)(2,1)S(1)} %shard_map.68.refs_0_), channel_id=1, source_target_pairs={{0,32},{1,33},{2,34},{3,35},{4,36},{5,37},{6,38},{7,39},{8,12},{9,... | collective-permute-start | bytes 884744 | tf_op jit(solution)/shard_map/ppermute | solution.py:63
  44.3 1.8 %collective-permute-done.2.refs_2_ = bf16[128,1152]{1,0:T(8,128)(2,1)S(1)} collective-permute-done((bf16[128,1152]{1,0:T(8,128)(2,1)S(1)}, bf16[128,1152]{1,0:T(8,128)(2,1)S(1)}, u32[]{:S(2)}, u32[]{:S(2)}) %collective-permute-start.2) | collective-permute-done | bytes 294944 | tf_op jit(solution)/shard_map/ppermute | solution.py:63
  46.2 1.4 collective-permute-done.3.refs_3_
  47.7 1.9 %shard_map.71.refs_0_ = bf16[576,1152]{1,0:T(8,128)(2,1)S(1)} custom-call(s32[1]{0:T(128)} %bitcast.2.refs_0_.total_ref, bf16[576,1152]{1,0:T(8,128)(2,1)S(1)} %shard_map.69.refs_4_.refs_1_, bf16[512,1152]{1,0:T(8,128)(2,1)S(1)} %collective-permute-done.4.refs_2_, bf16[256,1152]{1,0:T(8,128)(2,1)S(1)} %get-tuple-element.27.refs_3_.refs_2_), custom_call_target="tpu_custom_call" | custom-call | flops 679477248 | bytes 1048576 | tf_op jit(solution)/shard_map/pallas_call | solution.py:87
  49.7 2.0 %collective-permute-start.6 = (bf16[256,1152]{1,0:T(8,128)(2,1)S(1)}, bf16[256,1152]{1,0:T(8,128)(2,1)}, u32[]{:S(2)}, u32[]{:S(2)}) collective-permute-start(bf16[256,1152]{1,0:T(8,128)(2,1)S(1)} %get-tuple-element.27.refs_3_.refs_2_), channel_id=1, source_target_pairs={{0,2},{1,3},{2,4},{3,5},{4,6},{5,7},{6,0},{7,1},{8,24},{9,25},{10,... | collective-permute-start | bytes 1769480 | tf_op jit(solution)/shard_map/ppermute | solution.py:63
  51.7 2.2 %collective-permute-start.8 = (bf16[256,1152]{1,0:T(8,128)(2,1)S(1)}, bf16[256,1152]{1,0:T(8,128)(2,1)}, u32[]{:S(2)}, u32[]{:S(2)}) collective-permute-start(bf16[256,1152]{1,0:T(8,128)(2,1)S(1)} %get-tuple-element.28.refs_3_), channel_id=1, source_target_pairs={{0,6},{1,7},{2,0},{3,1},{4,2},{5,3},{6,4},{7,5},{8,56},{9,57},{10,... | collective-permute-start | bytes 1769480 | tf_op jit(solution)/shard_map/ppermute | solution.py:63
  53.9 1.9 %collective-permute-start.10 = (bf16[256,1152]{1,0:T(8,128)(2,1)S(1)}, bf16[256,1152]{1,0:T(8,128)(2,1)}, u32[]{:S(2)}, u32[]{:S(2)}) collective-permute-start(bf16[256,1152]{1,0:T(8,128)(2,1)S(1)} %get-tuple-element.27.refs_3_.refs_2_), channel_id=1, source_target_pairs={{0,6},{1,7},{2,0},{3,1},{4,2},{5,3},{6,4},{7,5},{8,56},{9,57},{10,... | collective-permute-start | bytes 1769480 | tf_op jit(solution)/shard_map/ppermute | solution.py:63
  55.9 5.8 %collective-permute-done.6.refs_2_ = bf16[256,1152]{1,0:T(8,128)(2,1)} collective-permute-done((bf16[256,1152]{1,0:T(8,128)(2,1)S(1)}, bf16[256,1152]{1,0:T(8,128)(2,1)}, u32[]{:S(2)}, u32[]{:S(2)}) %collective-permute-start.6) | collective-permute-done | bytes 589856 | tf_op jit(solution)/shard_map/ppermute | solution.py:63
  61.8 3.3 %collective-permute-start.9 = (bf16[256,1152]{1,0:T(8,128)(2,1)}, bf16[256,1152]{1,0:T(8,128)(2,1)}, u32[]{:S(2)}, u32[]{:S(2)}) collective-permute-start(bf16[256,1152]{1,0:T(8,128)(2,1)} %collective-permute-done.8.refs_3_), channel_id=1, source_target_pairs={{0,6},{1,7},{2,0},{3,1},{4,2},{5,3},{6,4},{7,5},{8,56},{9,57},{10,... | collective-permute-start | bytes 1769480 | tf_op jit(solution)/shard_map/ppermute | solution.py:63
  67.7 2.4 %block_local.1 = (bf16[512,1152]{1,0:T(8,128)(2,1)S(1)}, bf16[512,1152]{1,0:T(8,128)(2,1)S(1)}) custom-call(f32[2]{0:T(128)S(1)} %pad_maximum_fusion.refs_0_, s32[64,2]{1,0:T(8,128)S(1)} %copy.13.refs_1_, bf16[256,1152]{1,0:T(8,128)(2,1)S(1)} %get-tuple-element.27.refs_3_.refs_2_, bf16[256,1152]{1,0:T(8,128)(2,1)S(1)} %copy-done.5, ...), custom_call_target="tpu_custom_call" | custom-call | flops 1358954496 | bytes 8388608 | tf_op jit(solution)/shard_map/block_local/pallas_call | solution.py:161
  70.1 4.9 %block_remote.3 = (bf16[512,1152]{1,0:T(8,128)(2,1)S(1)}, bf16[512,1152]{1,0:T(8,128)(2,1)S(1)}, f32[256,1152]{1,0:T(8,128)S(1)}, bf16[256,1152]{1,0:T(8,128)(2,1)S(1)}) custom-call(f32[2]{0:T(128)S(1)} %pad_maximum_fusion.refs_0_, s32[64,2]{1,0:T(8,128)S(1)} %copy.13.refs_1_, bf16[256,1152]{1,0:T(8,128)(2,1)} %collective-permute-done.10.refs_2_, ...), custom_call_target="tpu_custom_call" | custom-call | flops 2717908992 | bytes 8388608 | tf_op jit(solution)/shard_map/block_remote/pallas_call | solution.py:161
  75.1 4.9 %block_remote.4 = (bf16[512,1152]{1,0:T(8,128)(2,1)S(1)}, bf16[512,1152]{1,0:T(8,128)(2,1)S(1)}, bf16[256,1152]{1,0:T(8,128)(2,1)S(1)}, bf16[256,1152]{1,0:T(8,128)(2,1)S(1)}) custom-call(f32[2]{0:T(128)S(1)} %pad_maximum_fusion.refs_0_, s32[64,2]{1,0:T(8,128)S(1)} %copy.13.refs_1_, bf16[256,1152]{1,0:T(8,128)(2,1)} %collective-permute-done.7.refs_2_, ...), custom_call_target="tpu_custom_call" | custom-call | flops 2717908992 | bytes 8388608 | tf_op jit(solution)/shard_map/block_remote/pallas_call | solution.py:161
  81.2 2.1 %collective-permute-start.13 = (bf16[256,1152]{1,0:T(8,128)(2,1)S(1)}, bf16[256,1152]{1,0:T(8,128)(2,1)S(1)}, u32[]{:S(2)}, u32[]{:S(2)}) collective-permute-start(bf16[256,1152]{1,0:T(8,128)(2,1)S(1)} %get-tuple-element.42), channel_id=1, source_target_pairs={{0,6},{1,7},{2,0},{3,1},{4,2},{5,3},{6,4},{7,5},{8,56},{9,57},{10,... | collective-permute-start | bytes 1769480 | tf_op jit(solution)/shard_map/ppermute | solution.py:63
  83.4 4.8 %block_remote.5 = (bf16[512,1152]{1,0:T(8,128)(2,1)S(1)}, bf16[512,1152]{1,0:T(8,128)(2,1)S(1)}, bf16[256,1152]{1,0:T(8,128)(2,1)S(1)}, f32[256,1152]{1,0:T(8,128)S(1)}) custom-call(f32[2]{0:T(128)S(1)} %pad_maximum_fusion.refs_0_, s32[64,2]{1,0:T(8,128)S(1)} %copy.13.refs_1_, bf16[256,1152]{1,0:T(8,128)(2,1)} %collective-permute-done.6.refs_2_, ...), custom_call_target="tpu_custom_call" | custom-call | flops 2717908992 | bytes 8388608 | tf_op jit(solution)/shard_map/block_remote/pallas_call | solution.py:161
  88.1 3.6 %shard_map.73 = (bf16[576,1152]{1,0:T(8,128)(2,1)S(1)}, f32[64,1152]{1,0:T(8,128)S(1)}) custom-call(bf16[512,1152]{1,0:T(8,128)(2,1)S(1)} %get-tuple-element.29.refs_5_.refs_0_, bf16[512,1152]{1,0:T(8,128)(2,1)S(1)} %get-tuple-element.31.refs_1_, bf16[512,1152]{1,0:T(8,128)(2,1)S(1)} %get-tuple-element.32.refs_2_, ...), custom_call_target="tpu_custom_call" | custom-call | flops 2717908992 | bytes 1048576 | tf_op jit(solution)/shard_map/pallas_call | solution.py:87
  93.2 2.4 %collective-permute-start.16 = (bf16[512,1152]{1,0:T(8,128)(2,1)S(1)}, bf16[512,1152]{1,0:T(8,128)(2,1)S(1)}, u32[]{:S(2)}, u32[]{:S(2)}) collective-permute-start(bf16[512,1152]{1,0:T(8,128)(2,1)S(1)} %get-tuple-element.44.refs_8_), channel_id=1, source_target_pairs={{0,6},{1,7},{2,0},{3,1},{4,2},{5,3},{6,4},{7,5},{8,56},{9,57},{10,... | collective-permute-start | bytes 3538952 | tf_op jit(solution)/shard_map/ppermute | solution.py:63
  95.6 2.9 %shard_map.75.refs_0_ = f32[512,1152]{1,0:T(8,128)S(1)} custom-call(bf16[512,1152]{1,0:T(8,128)(2,1)S(1)} %get-tuple-element.29.refs_5_.refs_0_, bf16[512,1152]{1,0:T(8,128)(2,1)S(1)} %get-tuple-element.31.refs_1_, bf16[512,1152]{1,0:T(8,128)(2,1)S(1)} %get-tuple-element.32.refs_2_, bf16[512,1152]{1,0:T(8,128)(2,1)S(1)} %get-tuple-element.34.refs_3_, ...), custom_call_target="tpu_custom_call" | custom-call | flops 2717908992 | bytes 1048576 | tf_op jit(solution)/shard_map/pallas_call | solution.py:87
  98.9 1.8 %shard_map.77 = (f32[256,1152]{1,0:T(8,128)S(1)}, f32[256,1152]{1,0:T(8,128)S(1)}) custom-call(bf16[512,1152]{1,0:T(8,128)(2,1)S(1)} %get-tuple-element.29.refs_5_.refs_0_, bf16[1152,1152]{1,0:T(8,128)(2,1)S(1)} %shard_map.72.refs_4_.refs_1_, bf16[384,1152]{1,0:T(8,128)(2,1)S(1)} %get-tuple-element.46.refs_2_), custom_call_target="tpu_custom_call" | custom-call | flops 1358954496 | bytes 1048576 | tf_op jit(solution)/shard_map/pallas_call | solution.py:87
  100.7 9.0 %collective-permute-done.15 = bf16[512,1152]{1,0:T(8,128)(2,1)S(1)} collective-permute-done((bf16[512,1152]{1,0:T(8,128)(2,1)S(1)}, bf16[512,1152]{1,0:T(8,128)(2,1)S(1)}, u32[]{:S(2)}, u32[]{:S(2)}) %collective-permute-start.15) | collective-permute-done | bytes 1179680 | tf_op jit(solution)/shard_map/ppermute | solution.py:63
  111.7 1.9 %collective-permute-start.19 = (bf16[128,1152]{1,0:T(8,128)(2,1)S(1)}, bf16[128,1152]{1,0:T(8,128)(2,1)S(1)}, u32[]{:S(2)}, u32[]{:S(2)}) collective-permute-start(bf16[128,1152]{1,0:T(8,128)(2,1)S(1)} %get-tuple-element.57), channel_id=1, source_target_pairs={{0,16},{1,17},{2,18},{3,19},{4,20},{5,21},{6,22},{7,23},{8,10},{9,... | collective-permute-start | bytes 884744 | tf_op jit(solution)/shard_map/ppermute | solution.py:63
  113.7 1.7 %collective-permute-start.18 = (bf16[128,1152]{1,0:T(8,128)(2,1)S(1)}, bf16[128,1152]{1,0:T(8,128)(2,1)S(1)}, u32[]{:S(2)}, u32[]{:S(2)}) collective-permute-start(bf16[128,1152]{1,0:T(8,128)(2,1)S(1)} %slice.76), channel_id=1, source_target_pairs={{0,48},{1,49},{2,50},{3,51},{4,52},{5,53},{6,54},{7,55},{8,14},{9,... | collective-permute-start | bytes 884744 | tf_op jit(solution)/shard_map/ppermute | solution.py:63
  115.6 2.0 %collective-permute-start.22 = (bf16[128,1152]{1,0:T(8,128)(2,1)S(1)}, bf16[128,1152]{1,0:T(8,128)(2,1)S(1)}, u32[]{:S(2)}, u32[]{:S(2)}) collective-permute-start(bf16[128,1152]{1,0:T(8,128)(2,1)S(1)} %get-tuple-element.51), channel_id=1, source_target_pairs={{0,64},{1,65},{2,66},{3,67},{4,68},{5,69},{6,70},{7,71},{8,72},{9,... | collective-permute-start | bytes 884744 | tf_op jit(solution)/shard_map/ppermute | solution.py:63
  118.9 3.1 %collective-permute-done.19 = bf16[128,1152]{1,0:T(8,128)(2,1)S(1)} collective-permute-done((bf16[128,1152]{1,0:T(8,128)(2,1)S(1)}, bf16[128,1152]{1,0:T(8,128)(2,1)S(1)}, u32[]{:S(2)}, u32[]{:S(2)}) %collective-permute-start.19) | collective-permute-done | bytes 294944 | tf_op jit(solution)/shard_map/ppermute | solution.py:63
  122.8 15.1 %collective-permute-done.21.refs_2_ = bf16[384,1152]{1,0:T(8,128)(2,1)S(1)} collective-permute-done((bf16[384,1152]{1,0:T(8,128)(2,1)S(1)}, bf16[384,1152]{1,0:T(8,128)(2,1)S(1)}, u32[]{:S(2)}, u32[]{:S(2)}) %collective-permute-start.21) | collective-permute-done | bytes 884768 | tf_op jit(solution)/shard_map/ppermute | solution.py:63
  137.9 1.5 %shard_map.78.own_ref = f32[512,1152]{1,0:T(8,128)S(1)} custom-call(s32[1]{0:T(128)} %bitcast.2.refs_0_.total_ref, f32[512,1152]{1,0:T(8,128)S(1)} %get-tuple-element.50.refs_1_, bf16[384,1152]{1,0:T(8,128)(2,1)S(1)} %collective-permute-done.21.refs_2_), custom_call_target="tpu_custom_call" | custom-call | flops 603979776 | bytes 1048576 | tf_op jit(solution)/shard_map/pallas_call | solution.py:87
  139.4 4.3 %collective-permute-done.22.back_ref = bf16[128,1152]{1,0:T(8,128)(2,1)S(1)} collective-permute-done((bf16[128,1152]{1,0:T(8,128)(2,1)S(1)}, bf16[128,1152]{1,0:T(8,128)(2,1)S(1)}, u32[]{:S(2)}, u32[]{:S(2)}) %collective-permute-start.22) | collective-permute-done | bytes 294944 | tf_op jit(solution)/shard_map/ppermute | solution.py:63
  143.7 3.5 %caption_grad.1 = f32[512,1152]{1,0:T(8,128)} custom-call(s32[1]{0:T(128)} %bitcast.2.refs_0_.total_ref, bf16[512,1152]{1,0:T(8,128)(2,1)S(1)} %copy-done.1, f32[512,1152]{1,0:T(8,128)S(1)} %shard_map.78.own_ref, bf16[128,1152]{1,0:T(8,128)(2,1)S(1)} %collective-permute-done.22.back_ref), custom_call_target="tpu_custom_call" | custom-call | flops 4718592 | bytes 4194304 | tf_op jit(solution)/shard_map/caption_grad/pallas_call | solution.py:254
  (59 shorter events, 14.7 us)
Async XLA Ops:
  0.6 47.0 %collective-permute-start.4 = (bf16[512,1152]{1,0:T(8,128)(2,1)}, bf16[512,1152]{1,0:T(8,128)(2,1)S(1)}, u32[]{:S(2)}, u32[]{:S(2)}) collective-permute-start(bf16[512,1152]{1,0:T(8,128)(2,1)} %raw_ref.1), channel_id=1, source_target_pairs={{0,64},{1,65},{2,66},{3,67},{4,68},{5,69},{6,70},{7,71},{8,72},{9,... | collective-permute-start | bytes 3538952 | tf_op jit(solution)/shard_map/ppermute | solution.py:63
  2.4 32.0 %collective-permute-start = (bf16[64,1152]{1,0:T(8,128)(2,1)}, bf16[64,1152]{1,0:T(8,128)(2,1)S(1)}, u32[]{:S(2)}, u32[]{:S(2)}) collective-permute-start(bf16[64,1152]{1,0:T(8,128)(2,1)} %refs_0_.1), channel_id=1, source_target_pairs={{0,1},{1,0},{2,3},{3,2},{4,5},{5,4},{6,7},{7,6},{8,9},{9,8},{10,11... | collective-permute-start | bytes 442376 | tf_op jit(solution)/shard_map/ppermute | solution.py:63
  34.3 0.9 copy-start.2
  35.4 8.9 %collective-permute-start.1 = (bf16[128,1152]{1,0:T(8,128)(2,1)S(1)}, bf16[128,1152]{1,0:T(8,128)(2,1)S(1)}, u32[]{:S(2)}, u32[]{:S(2)}) collective-permute-start(bf16[128,1152]{1,0:T(8,128)(2,1)S(1)} %shard_map.68.refs_0_), channel_id=1, source_target_pairs={{0,16},{1,17},{2,18},{3,19},{4,20},{5,21},{6,22},{7,23},{8,10},{9,... | collective-permute-start | bytes 884744 | tf_op jit(solution)/shard_map/ppermute | solution.py:63
  37.0 9.2 %collective-permute-start.2 = (bf16[128,1152]{1,0:T(8,128)(2,1)S(1)}, bf16[128,1152]{1,0:T(8,128)(2,1)S(1)}, u32[]{:S(2)}, u32[]{:S(2)}) collective-permute-start(bf16[128,1152]{1,0:T(8,128)(2,1)S(1)} %shard_map.68.refs_0_), channel_id=1, source_target_pairs={{0,48},{1,49},{2,50},{3,51},{4,52},{5,53},{6,54},{7,55},{8,14},{9,... | collective-permute-start | bytes 884744 | tf_op jit(solution)/shard_map/ppermute | solution.py:63
  38.7 8.8 %collective-permute-start.3 = (bf16[128,1152]{1,0:T(8,128)(2,1)S(1)}, bf16[128,1152]{1,0:T(8,128)(2,1)S(1)}, u32[]{:S(2)}, u32[]{:S(2)}) collective-permute-start(bf16[128,1152]{1,0:T(8,128)(2,1)S(1)} %shard_map.68.refs_0_), channel_id=1, source_target_pairs={{0,32},{1,33},{2,34},{3,35},{4,36},{5,37},{6,38},{7,39},{8,12},{9,... | collective-permute-start | bytes 884744 | tf_op jit(solution)/shard_map/ppermute | solution.py:63
  41.9 1.3 copy-start
  47.6 17.4 %copy-start.4 = (bf16[256,1152]{1,0:T(8,128)(2,1)}, bf16[256,1152]{1,0:T(8,128)(2,1)S(1)}, u32[]{:S(2)}) copy-start(bf16[256,1152]{1,0:T(8,128)(2,1)S(1)} %get-tuple-element.28.refs_3_) | copy-start | bytes 1769476
  49.6 17.2 %collective-permute-start.5 = (bf16[576,1152]{1,0:T(8,128)(2,1)S(1)}, bf16[576,1152]{1,0:T(8,128)(2,1)S(1)}, u32[]{:S(2)}, u32[]{:S(2)}) collective-permute-start(bf16[576,1152]{1,0:T(8,128)(2,1)S(1)} %shard_map.71.refs_0_), channel_id=1, source_target_pairs={{0,8},{1,9},{2,10},{3,11},{4,12},{5,13},{6,14},{7,15},{8,0},{9,1},... | collective-permute-start | bytes 3981320 | tf_op jit(solution)/shard_map/ppermute | solution.py:63
  49.7 12.1 %collective-permute-start.6 = (bf16[256,1152]{1,0:T(8,128)(2,1)S(1)}, bf16[256,1152]{1,0:T(8,128)(2,1)}, u32[]{:S(2)}, u32[]{:S(2)}) collective-permute-start(bf16[256,1152]{1,0:T(8,128)(2,1)S(1)} %get-tuple-element.27.refs_3_.refs_2_), channel_id=1, source_target_pairs={{0,2},{1,3},{2,4},{3,5},{4,6},{5,7},{6,0},{7,1},{8,24},{9,25},{10,... | collective-permute-start | bytes 1769480 | tf_op jit(solution)/shard_map/ppermute | solution.py:63
  51.7 10.1 %collective-permute-start.8 = (bf16[256,1152]{1,0:T(8,128)(2,1)S(1)}, bf16[256,1152]{1,0:T(8,128)(2,1)}, u32[]{:S(2)}, u32[]{:S(2)}) collective-permute-start(bf16[256,1152]{1,0:T(8,128)(2,1)S(1)} %get-tuple-element.28.refs_3_), channel_id=1, source_target_pairs={{0,6},{1,7},{2,0},{3,1},{4,2},{5,3},{6,4},{7,5},{8,56},{9,57},{10,... | collective-permute-start | bytes 1769480 | tf_op jit(solution)/shard_map/ppermute | solution.py:63
  53.9 16.2 %collective-permute-start.10 = (bf16[256,1152]{1,0:T(8,128)(2,1)S(1)}, bf16[256,1152]{1,0:T(8,128)(2,1)}, u32[]{:S(2)}, u32[]{:S(2)}) collective-permute-start(bf16[256,1152]{1,0:T(8,128)(2,1)S(1)} %get-tuple-element.27.refs_3_.refs_2_), channel_id=1, source_target_pairs={{0,6},{1,7},{2,0},{3,1},{4,2},{5,3},{6,4},{7,5},{8,56},{9,57},{10,... | collective-permute-start | bytes 1769480 | tf_op jit(solution)/shard_map/ppermute | solution.py:63
  61.8 13.3 %collective-permute-start.7 = (bf16[256,1152]{1,0:T(8,128)(2,1)}, bf16[256,1152]{1,0:T(8,128)(2,1)}, u32[]{:S(2)}, u32[]{:S(2)}) collective-permute-start(bf16[256,1152]{1,0:T(8,128)(2,1)} %collective-permute-done.6.refs_2_), channel_id=1, source_target_pairs={{0,2},{1,3},{2,4},{3,5},{4,6},{5,7},{6,0},{7,1},{8,24},{9,25},{10,... | collective-permute-start | bytes 1769480 | tf_op jit(solution)/shard_map/ppermute | solution.py:63
  61.8 13.3 %collective-permute-start.9 = (bf16[256,1152]{1,0:T(8,128)(2,1)}, bf16[256,1152]{1,0:T(8,128)(2,1)}, u32[]{:S(2)}, u32[]{:S(2)}) collective-permute-start(bf16[256,1152]{1,0:T(8,128)(2,1)} %collective-permute-done.8.refs_3_), channel_id=1, source_target_pairs={{0,6},{1,7},{2,0},{3,1},{4,2},{5,3},{6,4},{7,5},{8,56},{9,57},{10,... | collective-permute-start | bytes 1769480 | tf_op jit(solution)/shard_map/ppermute | solution.py:63
  66.6 1.1 copy-start.5
  66.6 16.8 %collective-permute-start.11 = (bf16[256,1152]{1,0:T(8,128)(2,1)}, bf16[256,1152]{1,0:T(8,128)(2,1)S(1)}, u32[]{:S(2)}, u32[]{:S(2)}) collective-permute-start(bf16[256,1152]{1,0:T(8,128)(2,1)} %copy-done.4), channel_id=1, source_target_pairs={{0,2},{1,3},{2,4},{3,5},{4,6},{5,7},{6,0},{7,1},{8,24},{9,25},{10,... | collective-permute-start | bytes 1769480 | tf_op jit(solution)/shard_map/ppermute | solution.py:63
  80.0 11.8 %collective-permute-start.12 = (bf16[256,1152]{1,0:T(8,128)(2,1)S(1)}, bf16[256,1152]{1,0:T(8,128)(2,1)S(1)}, u32[]{:S(2)}, u32[]{:S(2)}) collective-permute-start(bf16[256,1152]{1,0:T(8,128)(2,1)S(1)} %get-tuple-element.33.refs_5_), channel_id=1, source_target_pairs={{0,2},{1,3},{2,4},{3,5},{4,6},{5,7},{6,0},{7,1},{8,24},{9,25},{10,... | collective-permute-start | bytes 1769480 | tf_op jit(solution)/shard_map/ppermute | solution.py:63
  81.2 10.7 %collective-permute-start.13 = (bf16[256,1152]{1,0:T(8,128)(2,1)S(1)}, bf16[256,1152]{1,0:T(8,128)(2,1)S(1)}, u32[]{:S(2)}, u32[]{:S(2)}) collective-permute-start(bf16[256,1152]{1,0:T(8,128)(2,1)S(1)} %get-tuple-element.42), channel_id=1, source_target_pairs={{0,6},{1,7},{2,0},{3,1},{4,2},{5,3},{6,4},{7,5},{8,56},{9,57},{10,... | collective-permute-start | bytes 1769480 | tf_op jit(solution)/shard_map/ppermute | solution.py:63
  91.8 6.7 %collective-permute-start.14 = (bf16[576,1152]{1,0:T(8,128)(2,1)S(1)}, bf16[576,1152]{1,0:T(8,128)(2,1)S(1)}, u32[]{:S(2)}, u32[]{:S(2)}) collective-permute-start(bf16[576,1152]{1,0:T(8,128)(2,1)S(1)} %get-tuple-element.43.refs_6_), channel_id=1, source_target_pairs={{0,8},{1,9},{2,10},{3,11},{4,12},{5,13},{6,14},{7,15},{8,0},{9,1},... | collective-permute-start | bytes 3981320 | tf_op jit(solution)/shard_map/ppermute | solution.py:63
  92.3 17.5 %collective-permute-start.15 = (bf16[512,1152]{1,0:T(8,128)(2,1)S(1)}, bf16[512,1152]{1,0:T(8,128)(2,1)S(1)}, u32[]{:S(2)}, u32[]{:S(2)}) collective-permute-start(bf16[512,1152]{1,0:T(8,128)(2,1)S(1)} %get-tuple-element.48), channel_id=1, source_target_pairs={{0,2},{1,3},{2,4},{3,5},{4,6},{5,7},{6,0},{7,1},{8,24},{9,25},{10,... | collective-permute-start | bytes 3538952 | tf_op jit(solution)/shard_map/ppermute | solution.py:63
  93.2 16.7 %collective-permute-start.16 = (bf16[512,1152]{1,0:T(8,128)(2,1)S(1)}, bf16[512,1152]{1,0:T(8,128)(2,1)S(1)}, u32[]{:S(2)}, u32[]{:S(2)}) collective-permute-start(bf16[512,1152]{1,0:T(8,128)(2,1)S(1)} %get-tuple-element.44.refs_8_), channel_id=1, source_target_pairs={{0,6},{1,7},{2,0},{3,1},{4,2},{5,3},{6,4},{7,5},{8,56},{9,57},{10,... | collective-permute-start | bytes 3538952 | tf_op jit(solution)/shard_map/ppermute | solution.py:63
  110.4 5.1 %copy-start.3 = (bf16[64,1152]{1,0:T(8,128)(2,1)S(1)}, bf16[64,1152]{1,0:T(8,128)(2,1)}, u32[]{:S(2)}) copy-start(bf16[64,1152]{1,0:T(8,128)(2,1)} %refs_0_.1) | copy-start | bytes 442372
  110.5 8.4 %collective-permute-start.17 = (bf16[128,1152]{1,0:T(8,128)(2,1)S(1)}, bf16[128,1152]{1,0:T(8,128)(2,1)S(1)}, u32[]{:S(2)}, u32[]{:S(2)}) collective-permute-start(bf16[128,1152]{1,0:T(8,128)(2,1)S(1)} %get-tuple-element.56), channel_id=1, source_target_pairs={{0,32},{1,33},{2,34},{3,35},{4,36},{5,37},{6,38},{7,39},{8,12},{9,... | collective-permute-start | bytes 884744 | tf_op jit(solution)/shard_map/ppermute | solution.py:63
  111.7 10.2 %collective-permute-start.19 = (bf16[128,1152]{1,0:T(8,128)(2,1)S(1)}, bf16[128,1152]{1,0:T(8,128)(2,1)S(1)}, u32[]{:S(2)}, u32[]{:S(2)}) collective-permute-start(bf16[128,1152]{1,0:T(8,128)(2,1)S(1)} %get-tuple-element.57), channel_id=1, source_target_pairs={{0,16},{1,17},{2,18},{3,19},{4,20},{5,21},{6,22},{7,23},{8,10},{9,... | collective-permute-start | bytes 884744 | tf_op jit(solution)/shard_map/ppermute | solution.py:63
  113.7 8.2 %collective-permute-start.18 = (bf16[128,1152]{1,0:T(8,128)(2,1)S(1)}, bf16[128,1152]{1,0:T(8,128)(2,1)S(1)}, u32[]{:S(2)}, u32[]{:S(2)}) collective-permute-start(bf16[128,1152]{1,0:T(8,128)(2,1)S(1)} %slice.76), channel_id=1, source_target_pairs={{0,48},{1,49},{2,50},{3,51},{4,52},{5,53},{6,54},{7,55},{8,14},{9,... | collective-permute-start | bytes 884744 | tf_op jit(solution)/shard_map/ppermute | solution.py:63
  115.4 22.5 %collective-permute-start.21 = (bf16[384,1152]{1,0:T(8,128)(2,1)S(1)}, bf16[384,1152]{1,0:T(8,128)(2,1)S(1)}, u32[]{:S(2)}, u32[]{:S(2)}) collective-permute-start(bf16[384,1152]{1,0:T(8,128)(2,1)S(1)} %get-tuple-element.46.refs_2_), channel_id=1, source_target_pairs={{0,64},{1,65},{2,66},{3,67},{4,68},{5,69},{6,70},{7,71},{8,72},{9,... | collective-permute-start | bytes 2654216 | tf_op jit(solution)/shard_map/ppermute | solution.py:63
  115.6 28.1 %collective-permute-start.22 = (bf16[128,1152]{1,0:T(8,128)(2,1)S(1)}, bf16[128,1152]{1,0:T(8,128)(2,1)S(1)}, u32[]{:S(2)}, u32[]{:S(2)}) collective-permute-start(bf16[128,1152]{1,0:T(8,128)(2,1)S(1)} %get-tuple-element.51), channel_id=1, source_target_pairs={{0,64},{1,65},{2,66},{3,67},{4,68},{5,69},{6,70},{7,71},{8,72},{9,... | collective-permute-start | bytes 884744 | tf_op jit(solution)/shard_map/ppermute | solution.py:63
  122.1 25.1 %collective-permute-start.20 = (bf16[64,1152]{1,0:T(8,128)(2,1)S(1)}, bf16[64,1152]{1,0:T(8,128)(2,1)S(1)}, u32[]{:S(2)}, u32[]{:S(2)}) collective-permute-start(bf16[64,1152]{1,0:T(8,128)(2,1)S(1)} %slice.77), channel_id=1, source_target_pairs={{0,1},{1,0},{2,3},{3,2},{4,5},{5,4},{6,7},{7,6},{8,9},{9,8},{10,11... | collective-permute-start | bytes 442376 | tf_op jit(solution)/shard_map/ppermute | solution.py:63
  137.9 5.9 %copy-start.1 = (bf16[512,1152]{1,0:T(8,128)(2,1)S(1)}, bf16[512,1152]{1,0:T(8,128)(2,1)}, u32[]{:S(2)}) copy-start(bf16[512,1152]{1,0:T(8,128)(2,1)} %raw_ref.1) | copy-start | bytes 3538948

commit v3 on v2

--- a/solution.py
+++ b/solution.py
@@ -52,9 +52,10 @@
     return route(move)
 
 
-def flip_route(axis):
+def flip_route(*axes):
     def move(c):
-        c[axis] = 1 - c[axis]
+        for axis in axes:
+            c[axis] = 1 - c[axis]
 
     return route(move)
 
@@ -69,9 +70,13 @@
     return values * inverse, inverse
 
 
+def low_kernel(raw_ref, out_ref):
+    out_ref[...] = unit_rows(raw_ref[...])[0].astype(BF16)
+
+
 def near_kernel(own_ref, far_ref, near_ref):
     count = own_ref.shape[0]
-    near_ref[:count] = unit_rows(own_ref[...])[0].astype(BF16)
+    near_ref[:count] = own_ref[...]
     near_ref[count:] = unit_rows(far_ref[...])[0].astype(BF16)
 
 
@@ -229,40 +234,100 @@
     back_b[slots - rest - first :] = tail.astype(BF16)
 
 
-def home_kernel(total_ref, own_ref, back_ref, out_ref):
+def image_kernel(raw_ref, own_ref, a_ref, b_ref, c_ref, far_ref, out_ref):
+    count = own_ref.shape[0]
+    sums = own_ref[...] + a_ref[:count].astype(F32) + b_ref[:count].astype(F32)
+    sums = sums + c_ref[:count].astype(F32) + far_ref[...].astype(F32)
+    out_ref[...] = project(raw_ref[...], sums)
+
+
+def project(raw, sums):
+    unit, inverse = unit_rows(raw)
+    return (sums - unit * jnp.sum(unit * sums, axis=1, keepdims=True)) * inverse
+
+
+def window_start(total, last, rows, slots):
+    return pl.multiple_of(jnp.clip((total - last) // 16 * 16, 0, slots - rows), 16)
+
+
+def home_kernel(
+    last, total_ref, raw_ref, own_ref, back_ref, out_ref, part_raw, part_sums, sums_ref, grads_ref,
+    sems,
+):
     slots = own_ref.shape[0]
-    out_ref[...] = own_ref[...] + picked(
-        slots, back_ref.shape[0], slots - total_ref[0], back_ref[...]
-    )
-
-
-def grad_kernel(skip, total_ref, raw_ref, own_ref, back_ref, out_ref):
-    rows = out_ref.shape[0]
-    start = pl.program_id(0) * rows
-    unit, inverse = unit_rows(raw_ref[...])
-    offset = start + pl.num_programs(0) * rows - total_ref[0] - skip
-    sums = own_ref[...] + picked(rows, back_ref.shape[0], offset, back_ref[...])
-    grads = (sums - unit * jnp.sum(unit * sums, axis=1, keepdims=True)) * inverse
-    slot = start + lax.broadcasted_iota(jnp.int32, grads.shape, 0)
-    out_ref[...] = jnp.where(slot < total_ref[0], grads, 0.0)
-
-
-def caption_grads(skip, total, raw, own_rows, back):
+    rows = part_raw.shape[0]
+    total = total_ref[0]
+    steps = sems.shape[0]
+    tile = slots // steps
+    copies = []
+    for step in range(steps):
+        part = slice(step * tile, (step + 1) * tile)
+        offset = slots - total + step * tile
+        sums = own_ref[part] + picked(tile, back_ref.shape[0], offset, back_ref[...])
+        sums_ref[part] = sums
+        slot = step * tile + lax.broadcasted_iota(jnp.int32, sums.shape, 0)
+        grads_ref[part] = jnp.where(slot < total, project(raw_ref[part], sums), 0.0)
+        copies.append(
+            pltpu.make_async_copy(grads_ref.at[part], out_ref.at[part], sems.at[step])
+        )
+        copies[-1].start()
+    window = pl.ds(window_start(total, last, rows, slots), rows)
+    part_raw[...] = raw_ref[window, :]
+    part_sums[...] = sums_ref[window, :]
+    for copy in copies:
+        copy.wait()
+
+
+def last_kernel(total_ref, raw_ref, sums_ref, back_ref, early_ref, out_ref, grads_ref, sem):
+    last, rows = back_ref.shape[0], grads_ref.shape[0]
+    total = total_ref[0]
+    start = window_start(total, last, rows, out_ref.shape[0])
+    sums = sums_ref[...] + picked(rows, last, start + last - total, back_ref[...])
+    slot = start + lax.broadcasted_iota(jnp.int32, sums.shape, 0)
+    grads_ref[...] = jnp.where(slot < total, project(raw_ref[...], sums), 0.0)
+    copy = pltpu.make_async_copy(grads_ref, out_ref.at[pl.ds(start, rows), :], sem)
+    copy.start()
+    copy.wait()
+
+
+def caption_grads(total, raw, own, back, last):
     slots, width = raw.shape
-    steps = 4
-    some = pl.BlockSpec((slots // steps, width), lambda i: (i, 0))
+    rows = last + 16
     return pl.pallas_call(
-        functools.partial(grad_kernel, skip),
-        grid=(steps,),
+        functools.partial(home_kernel, last),
+        out_shape=(
+            jax.ShapeDtypeStruct((slots, width), F32),
+            jax.ShapeDtypeStruct((rows, width), BF16),
+            jax.ShapeDtypeStruct((rows, width), F32),
+        ),
+        in_specs=[SMEM, VMEM, VMEM, VMEM],
+        out_specs=(ANY, VMEM, VMEM),
+        scratch_shapes=[
+            pltpu.VMEM((slots, width), F32),
+            pltpu.VMEM((slots, width), F32),
+            pltpu.SemaphoreType.DMA((4,)),
+        ],
+        compiler_params=pltpu.CompilerParams(vmem_limit_bytes=20 * MIB),
+        cost_estimate=pl.CostEstimate(
+            flops=2 * slots * slots * width, bytes_accessed=8 * MIB, transcendentals=0
+        ),
+        name="caption_grad",
+    )(total, raw, own, back)
+
+
+def last_rows(total, raw, sums, back, early):
+    slots, width = early.shape
+    return pl.pallas_call(
+        last_kernel,
         out_shape=jax.ShapeDtypeStruct((slots, width), F32),
-        in_specs=[SMEM, some, some, pl.BlockSpec(back.shape, lambda i: (0, 0))],
-        out_specs=some,
-        compiler_params=pltpu.CompilerParams(vmem_limit_bytes=16 * MIB),
-        cost_estimate=pl.CostEstimate(
-            flops=8 * slots * width, bytes_accessed=4 * MIB, transcendentals=0
-        ),
-        name="caption_grad",
-    )(total, raw, own_rows, back)
+        in_specs=[SMEM, VMEM, VMEM, VMEM, ANY],
+        out_specs=ANY,
+        scratch_shapes=[pltpu.VMEM(sums.shape, F32), pltpu.SemaphoreType.DMA],
+        input_output_aliases={4: 0},
+        compiler_params=pltpu.CompilerParams(vmem_limit_bytes=8 * MIB),
+        cost_estimate=pl.CostEstimate(flops=10**6, bytes_accessed=MIB, transcendentals=0),
+        name="caption_grad_last",
+    )(total, raw, sums, back, early)
 
 
 def program(image_embed, caption_vectors, caption_counts, natural_log_multiplier, match_odds_offset):
@@ -274,8 +339,8 @@
     scale = jnp.exp(natural_log_multiplier[0])
     scalars = jnp.stack([scale, match_odds_offset[0]])
 
-    far_raw = send(image_embed, flip_route(4))
     partner_raw = send(caption_vectors, flip_route(0))
+    far_raw = send(image_embed, flip_route(0, 4))
 
     counts = lax.dynamic_slice_in_dim(caption_counts, home * count, count)
     earlier = lax.iota(jnp.int32, count)[None, :] <= lax.iota(jnp.int32, count)[:, None]
@@ -284,8 +349,9 @@
     total = jnp.sum(counts).reshape(1)
 
     half = jax.ShapeDtypeStruct((4 * count, width), BF16)
+    own_low = plain(low_kernel, jax.ShapeDtypeStruct((count, width), BF16), (image_embed,), limit=4)
     near = plain(
-        near_kernel, jax.ShapeDtypeStruct((2 * count, width), BF16), (image_embed, far_raw)
+        near_kernel, jax.ShapeDtypeStruct((2 * count, width), BF16), (own_low, far_raw), limit=4
     )
     first = {}
     for k in (2, 1, 3):
@@ -359,7 +425,7 @@
         limit=24,
         after=(minus,),
     )
-    last = slots // 4
+    last = 3 * slots // 8
     pair, back_a, back_b = plain(
         back_kernel,
         (
@@ -386,24 +452,20 @@
 
     near_rows = 2 * count
     pieces = {1: head_sum[near_rows:], 3: tail_sum[:near_rows], 2: tail_sum[near_rows:]}
-    near_sum = head_sum[:near_rows]
+    far_sum = head_sum[count:near_rows]
+    near_back = []
     for k in (2, 1, 3):
-        near_sum = near_sum + send(pieces[k].astype(BF16), ring_route(0, -k)).astype(F32)
-    far_sum = send(near_sum[count:].astype(BF16), flip_route(4)).astype(F32)
-    own_sum = near_sum[:count] + far_sum
-    image_unit, image_inverse = unit_rows(image_embed)
-    image_grad = (
-        own_sum - image_unit * jnp.sum(image_unit * own_sum, axis=1, keepdims=True)
-    ) * image_inverse
-
-    own_rows = plain(
-        home_kernel,
-        jax.ShapeDtypeStruct((slots, width), F32),
-        (total, pair, returned_a),
-        2 * slots * slots * width,
-        1,
-    )
-    caption_grad = caption_grads(slots - last, total, caption_vectors, own_rows, returned_b)
+        near_back.append(send(pieces[k].astype(BF16), ring_route(0, -k)))
+        far_sum = far_sum + near_back[-1][count:].astype(F32)
+    far_back = send(far_sum.astype(BF16), flip_route(0, 4))
+    early_grad, part_raw, part_sums = caption_grads(total, caption_vectors, pair, returned_a, last)
+    image_grad = plain(
+        image_kernel,
+        jax.ShapeDtypeStruct((count, width), F32),
+        (image_embed, head_sum[:count], *near_back, far_back),
+        limit=8,
+    )
+    caption_grad = last_rows(total, part_raw, part_sums, returned_b, early_grad)
     return image_grad, caption_grad
 
 

time: 149 us -> 126 us (0.85)
  waiting for transfers between devices: 70.9 us -> 46.1 us
  starting transfers between devices: 33.9 us -> 36.4 us
    ppermute x23, waiting for transfers between devices: 70.9 us -> 46.1 us  [send(): return lax.ppermute(value, AXES, pairs)]
    ppermute x23, starting transfers between devices: 33.9 us -> 36.4 us  [send(): return lax.ppermute(value, AXES, pairs)]
    pallas_call x1 -> x2, Pallas kernels: 3.52 us -> 5.27 us  [the longest x1 3.11 us: caption_grads(): pl.pallas_call(functools.partial(home_kernel, last), out_shape=(jax.Shape...]
    pallas_call x11 -> x12, Pallas kernels: 14.1 us -> 13.5 us  [plain(): pl.pallas_call(lambda *refs: kernel(*refs[:len(args)], *refs[len(args) +...]
  transfers between devices with their start and end apart: 23 -> 23, of which waited for: 9 -> 12; matrix products, arithmetic and copies ran while one was open for 1% -> 2% of each run, Pallas kernels for 22% -> 26%
where the time goes in v3:
time: 126 us
  waiting for transfers between devices  46.1 us (37%)
  starting transfers between devices  36.4 us (29%)
  Pallas kernels  35.9 us (28%)
  local copies, waits for them, and re-layouts  3.05 us (2%)
  other arithmetic  2.32 us (2%)
  between operations  2.28 us (2%)
    ppermute x23, waiting for transfers between devices, send(): return lax.ppermute(value, AXES, pairs)  46.1 us
    ppermute x23, starting transfers between devices, send(): return lax.ppermute(value, AXES, pairs)  36.4 us
    pallas_call x4, Pallas kernels, weight_terms(): pl.pallas_call(lambda *refs: weight_kernel(local, bool(types), *refs[:ari...  17.1 us
    pallas_call x12, Pallas kernels, plain(): pl.pallas_call(lambda *refs: kernel(*refs[:len(args)], *refs[len(args) +...  13.5 us
    pallas_call x1, Pallas kernels, caption_grads(): pl.pallas_call(functools.partial(home_kernel, last), out_shape=(jax.Shape...  3.11 us
    unnamed x12, local copies, waits for them, and re-layouts  2.88 us
  transfers between devices with their start and end apart: 23, of which 12 were waited for; matrix products, arithmetic and copies ran while one was open for 2% of the time, Pallas kernels for 26%

profile of v3, /device:TPU:0, one launch (start us, length us, event | category | flops | bytes accessed | tf_op | source)
XLA Modules:
  0.0 126.0 jit_solution(12755532293109043971)
XLA Ops:
  0.6 1.8 %collective-permute-start.4 = (bf16[512,1152]{1,0:T(8,128)(2,1)}, bf16[512,1152]{1,0:T(8,128)(2,1)S(1)}, u32[]{:S(2)}, u32[]{:S(2)}) collective-permute-start(bf16[512,1152]{1,0:T(8,128)(2,1)} %raw_ref.1), channel_id=1, source_target_pairs={{0,64},{1,65},{2,66},{3,67},{4,68},{5,69},{6,70},{7,71},{8,72},{9,... | collective-permute-start | bytes 3538952 | tf_op jit(solution)/shard_map/ppermute | solution.py:64
  2.4 2.2 %collective-permute-start = (bf16[64,1152]{1,0:T(8,128)(2,1)}, bf16[64,1152]{1,0:T(8,128)(2,1)S(1)}, u32[]{:S(2)}, u32[]{:S(2)}) collective-permute-start(bf16[64,1152]{1,0:T(8,128)(2,1)} %refs_0_.3), channel_id=1, source_target_pairs={{0,65},{1,64},{2,67},{3,66},{4,69},{5,68},{6,71},{7,70},{8,73},{9,... | collective-permute-start | bytes 442376 | tf_op jit(solution)/shard_map/ppermute | solution.py:64
  5.6 3.5 %collective-permute-done.refs_1_ = bf16[64,1152]{1,0:T(8,128)(2,1)S(1)} collective-permute-done((bf16[64,1152]{1,0:T(8,128)(2,1)}, bf16[64,1152]{1,0:T(8,128)(2,1)S(1)}, u32[]{:S(2)}, u32[]{:S(2)}) %collective-permute-start) | collective-permute-done | bytes 147488 | tf_op jit(solution)/shard_map/ppermute | solution.py:64
  9.2 3.1 %collective-permute-start.3 = (bf16[128,1152]{1,0:T(8,128)(2,1)S(1)}, bf16[128,1152]{1,0:T(8,128)(2,1)S(1)}, u32[]{:S(2)}, u32[]{:S(2)}) collective-permute-start(bf16[128,1152]{1,0:T(8,128)(2,1)S(1)} %shard_map.69.refs_0_), channel_id=1, source_target_pairs={{0,32},{1,33},{2,34},{3,35},{4,36},{5,37},{6,38},{7,39},{8,12},{9,... | collective-permute-start | bytes 884744 | tf_op jit(solution)/shard_map/ppermute | solution.py:64
  14.4 1.4 %fusion.4 = (s32[]{:T(128)}, s32[64]{0:T(128)S(1)}) fusion(s32[8192]{0:T(1024)} %param.7, s32[]{:T(128)S(6)} %select_n.7), kind=kLoop, calls=%fused_computation.15 | loop fusion | flops 63 | bytes 520 | tf_op jit(solution)/shard_map/reduce_sum | solution.py:349
  18.2 2.7 %collective-permute-done.2.refs_2_ = bf16[128,1152]{1,0:T(8,128)(2,1)S(1)} collective-permute-done((bf16[128,1152]{1,0:T(8,128)(2,1)S(1)}, bf16[128,1152]{1,0:T(8,128)(2,1)S(1)}, u32[]{:S(2)}, u32[]{:S(2)}) %collective-permute-start.2) | collective-permute-done | bytes 294944 | tf_op jit(solution)/shard_map/ppermute | solution.py:64
  21.5 7.0 %collective-permute-done.4.refs_2_ = bf16[512,1152]{1,0:T(8,128)(2,1)S(1)} collective-permute-done((bf16[512,1152]{1,0:T(8,128)(2,1)}, bf16[512,1152]{1,0:T(8,128)(2,1)S(1)}, u32[]{:S(2)}, u32[]{:S(2)}) %collective-permute-start.4) | collective-permute-done | bytes 1179680 | tf_op jit(solution)/shard_map/ppermute | solution.py:64
  28.6 1.9 %shard_map.72.refs_0_ = bf16[576,1152]{1,0:T(8,128)(2,1)S(1)} custom-call(s32[1]{0:T(128)} %bitcast.2.refs_0_.total_ref, bf16[576,1152]{1,0:T(8,128)(2,1)S(1)} %shard_map.70.refs_4_.refs_1_, bf16[512,1152]{1,0:T(8,128)(2,1)S(1)} %collective-permute-done.4.refs_2_, bf16[256,1152]{1,0:T(8,128)(2,1)S(1)} %get-tuple-element.30.refs_3_.refs_2_), custom_call_target="tpu_custom_call" | custom-call | flops 679477248 | bytes 1048576 | tf_op jit(solution)/shard_map/pallas_call | solution.py:92
  30.5 4.3 %collective-permute-start.8 = (bf16[256,1152]{1,0:T(8,128)(2,1)S(1)}, bf16[256,1152]{1,0:T(8,128)(2,1)}, u32[]{:S(2)}, u32[]{:S(2)}) collective-permute-start(bf16[256,1152]{1,0:T(8,128)(2,1)S(1)} %get-tuple-element.31.refs_3_), channel_id=1, source_target_pairs={{0,6},{1,7},{2,0},{3,1},{4,2},{5,3},{6,4},{7,5},{8,56},{9,57},{10,... | collective-permute-start | bytes 1769480 | tf_op jit(solution)/shard_map/ppermute | solution.py:64
  34.8 3.2 %collective-permute-start.10 = (bf16[256,1152]{1,0:T(8,128)(2,1)S(1)}, bf16[256,1152]{1,0:T(8,128)(2,1)}, u32[]{:S(2)}, u32[]{:S(2)}) collective-permute-start(bf16[256,1152]{1,0:T(8,128)(2,1)S(1)} %get-tuple-element.30.refs_3_.refs_2_), channel_id=1, source_target_pairs={{0,6},{1,7},{2,0},{3,1},{4,2},{5,3},{6,4},{7,5},{8,56},{9,57},{10,... | collective-permute-start | bytes 1769480 | tf_op jit(solution)/shard_map/ppermute | solution.py:64
  39.5 2.7 %collective-permute-done.8.refs_3_ = bf16[256,1152]{1,0:T(8,128)(2,1)} collective-permute-done((bf16[256,1152]{1,0:T(8,128)(2,1)S(1)}, bf16[256,1152]{1,0:T(8,128)(2,1)}, u32[]{:S(2)}, u32[]{:S(2)}) %collective-permute-start.8) | collective-permute-done | bytes 589856 | tf_op jit(solution)/shard_map/ppermute | solution.py:64
  42.2 3.8 %collective-permute-start.9 = (bf16[256,1152]{1,0:T(8,128)(2,1)}, bf16[256,1152]{1,0:T(8,128)(2,1)}, u32[]{:S(2)}, u32[]{:S(2)}) collective-permute-start(bf16[256,1152]{1,0:T(8,128)(2,1)} %collective-permute-done.8.refs_3_), channel_id=1, source_target_pairs={{0,6},{1,7},{2,0},{3,1},{4,2},{5,3},{6,4},{7,5},{8,56},{9,57},{10,... | collective-permute-start | bytes 1769480 | tf_op jit(solution)/shard_map/ppermute | solution.py:64
  47.3 2.4 %block_local.1 = (bf16[512,1152]{1,0:T(8,128)(2,1)S(1)}, bf16[512,1152]{1,0:T(8,128)(2,1)S(1)}) custom-call(f32[2]{0:T(128)S(1)} %pad_maximum_fusion.refs_0_, s32[64,2]{1,0:T(8,128)S(1)} %copy.14.refs_1_, bf16[256,1152]{1,0:T(8,128)(2,1)S(1)} %get-tuple-element.30.refs_3_.refs_2_, bf16[256,1152]{1,0:T(8,128)(2,1)S(1)} %copy-done.5, ...), custom_call_target="tpu_custom_call" | custom-call | flops 1358954496 | bytes 8388608 | tf_op jit(solution)/shard_map/block_local/pallas_call | solution.py:166
  49.7 4.9 %block_remote.3 = (bf16[512,1152]{1,0:T(8,128)(2,1)S(1)}, bf16[512,1152]{1,0:T(8,128)(2,1)S(1)}, f32[256,1152]{1,0:T(8,128)S(1)}, bf16[256,1152]{1,0:T(8,128)(2,1)S(1)}) custom-call(f32[2]{0:T(128)S(1)} %pad_maximum_fusion.refs_0_, s32[64,2]{1,0:T(8,128)S(1)} %copy.14.refs_1_, bf16[256,1152]{1,0:T(8,128)(2,1)} %collective-permute-done.10.refs_2_, ...), custom_call_target="tpu_custom_call" | custom-call | flops 2717908992 | bytes 8388608 | tf_op jit(solution)/shard_map/block_remote/pallas_call | solution.py:166
  55.0 2.5 %collective-permute-done.7.refs_2_ = bf16[256,1152]{1,0:T(8,128)(2,1)} collective-permute-done((bf16[256,1152]{1,0:T(8,128)(2,1)}, bf16[256,1152]{1,0:T(8,128)(2,1)}, u32[]{:S(2)}, u32[]{:S(2)}) %collective-permute-start.7) | collective-permute-done | bytes 589856 | tf_op jit(solution)/shard_map/ppermute | solution.py:64
  57.4 4.9 %block_remote.4 = (bf16[512,1152]{1,0:T(8,128)(2,1)S(1)}, bf16[512,1152]{1,0:T(8,128)(2,1)S(1)}, bf16[256,1152]{1,0:T(8,128)(2,1)S(1)}, bf16[256,1152]{1,0:T(8,128)(2,1)S(1)}) custom-call(f32[2]{0:T(128)S(1)} %pad_maximum_fusion.refs_0_, s32[64,2]{1,0:T(8,128)S(1)} %copy.14.refs_1_, bf16[256,1152]{1,0:T(8,128)(2,1)} %collective-permute-done.7.refs_2_, ...), custom_call_target="tpu_custom_call" | custom-call | flops 2717908992 | bytes 8388608 | tf_op jit(solution)/shard_map/block_remote/pallas_call | solution.py:166
  64.5 4.8 %block_remote.5 = (bf16[512,1152]{1,0:T(8,128)(2,1)S(1)}, bf16[512,1152]{1,0:T(8,128)(2,1)S(1)}, bf16[256,1152]{1,0:T(8,128)(2,1)S(1)}, f32[256,1152]{1,0:T(8,128)S(1)}) custom-call(f32[2]{0:T(128)S(1)} %pad_maximum_fusion.refs_0_, s32[64,2]{1,0:T(8,128)S(1)} %copy.14.refs_1_, bf16[256,1152]{1,0:T(8,128)(2,1)} %collective-permute-done.6.refs_2_, ...), custom_call_target="tpu_custom_call" | custom-call | flops 2717908992 | bytes 8388608 | tf_op jit(solution)/shard_map/block_remote/pallas_call | solution.py:166
  69.3 3.6 %shard_map.74 = (bf16[576,1152]{1,0:T(8,128)(2,1)S(1)}, f32[64,1152]{1,0:T(8,128)S(1)}) custom-call(bf16[512,1152]{1,0:T(8,128)(2,1)S(1)} %get-tuple-element.32.refs_5_.refs_0_, bf16[512,1152]{1,0:T(8,128)(2,1)S(1)} %get-tuple-element.34.refs_1_, bf16[512,1152]{1,0:T(8,128)(2,1)S(1)} %get-tuple-element.35.refs_2_, ...), custom_call_target="tpu_custom_call" | custom-call | flops 2717908992 | bytes 1048576 | tf_op jit(solution)/shard_map/pallas_call | solution.py:92
  73.0 1.8 %collective-permute-done.12.refs_2_ = bf16[256,1152]{1,0:T(8,128)(2,1)S(1)} collective-permute-done((bf16[256,1152]{1,0:T(8,128)(2,1)S(1)}, bf16[256,1152]{1,0:T(8,128)(2,1)S(1)}, u32[]{:S(2)}, u32[]{:S(2)}) %collective-permute-start.12) | collective-permute-done | bytes 589856 | tf_op jit(solution)/shard_map/ppermute | solution.py:64
  75.2 3.2 %collective-permute-start.16 = (bf16[512,1152]{1,0:T(8,128)(2,1)S(1)}, bf16[512,1152]{1,0:T(8,128)(2,1)S(1)}, u32[]{:S(2)}, u32[]{:S(2)}) collective-permute-start(bf16[512,1152]{1,0:T(8,128)(2,1)S(1)} %get-tuple-element.47.refs_8_), channel_id=1, source_target_pairs={{0,6},{1,7},{2,0},{3,1},{4,2},{5,3},{6,4},{7,5},{8,56},{9,57},{10,... | collective-permute-start | bytes 3538952 | tf_op jit(solution)/shard_map/ppermute | solution.py:64
  78.4 2.9 %shard_map.76.refs_0_ = f32[512,1152]{1,0:T(8,128)S(1)} custom-call(bf16[512,1152]{1,0:T(8,128)(2,1)S(1)} %get-tuple-element.32.refs_5_.refs_0_, bf16[512,1152]{1,0:T(8,128)(2,1)S(1)} %get-tuple-element.34.refs_1_, bf16[512,1152]{1,0:T(8,128)(2,1)S(1)} %get-tuple-element.35.refs_2_, bf16[512,1152]{1,0:T(8,128)(2,1)S(1)} %get-tuple-element.37.refs_3_, ...), custom_call_target="tpu_custom_call" | custom-call | flops 2717908992 | bytes 1048576 | tf_op jit(solution)/shard_map/pallas_call | solution.py:92
  81.7 1.8 %shard_map.78 = (f32[256,1152]{1,0:T(8,128)S(1)}, f32[256,1152]{1,0:T(8,128)S(1)}) custom-call(bf16[512,1152]{1,0:T(8,128)(2,1)S(1)} %get-tuple-element.32.refs_5_.refs_0_, bf16[1152,1152]{1,0:T(8,128)(2,1)S(1)} %shard_map.73.refs_4_.refs_1_, bf16[320,1152]{1,0:T(8,128)(2,1)S(1)} %get-tuple-element.49.refs_2_), custom_call_target="tpu_custom_call" | custom-call | flops 1358954496 | bytes 1048576 | tf_op jit(solution)/shard_map/pallas_call | solution.py:92
  83.6 9.0 %collective-permute-done.15 = bf16[512,1152]{1,0:T(8,128)(2,1)S(1)} collective-permute-done((bf16[512,1152]{1,0:T(8,128)(2,1)S(1)}, bf16[512,1152]{1,0:T(8,128)(2,1)S(1)}, u32[]{:S(2)}, u32[]{:S(2)}) %collective-permute-start.15) | collective-permute-done | bytes 1179680 | tf_op jit(solution)/shard_map/ppermute | solution.py:64
  93.4 2.8 %collective-permute-start.18 = (bf16[128,1152]{1,0:T(8,128)(2,1)S(1)}, bf16[128,1152]{1,0:T(8,128)(2,1)S(1)}, u32[]{:S(2)}, u32[]{:S(2)}) collective-permute-start(bf16[128,1152]{1,0:T(8,128)(2,1)S(1)} %slice.84), channel_id=1, source_target_pairs={{0,48},{1,49},{2,50},{3,51},{4,52},{5,53},{6,54},{7,55},{8,14},{9,... | collective-permute-start | bytes 884744 | tf_op jit(solution)/shard_map/ppermute | solution.py:64
  96.2 2.3 %collective-permute-start.17 = (bf16[128,1152]{1,0:T(8,128)(2,1)S(1)}, bf16[128,1152]{1,0:T(8,128)(2,1)S(1)}, u32[]{:S(2)}, u32[]{:S(2)}) collective-permute-start(bf16[128,1152]{1,0:T(8,128)(2,1)S(1)} %get-tuple-element.65), channel_id=1, source_target_pairs={{0,32},{1,33},{2,34},{3,35},{4,36},{5,37},{6,38},{7,39},{8,12},{9,... | collective-permute-start | bytes 884744 | tf_op jit(solution)/shard_map/ppermute | solution.py:64
  98.5 1.6 %collective-permute-start.21 = (bf16[320,1152]{1,0:T(8,128)(2,1)S(1)}, bf16[320,1152]{1,0:T(8,128)(2,1)S(1)}, u32[]{:S(2)}, u32[]{:S(2)}) collective-permute-start(bf16[320,1152]{1,0:T(8,128)(2,1)S(1)} %get-tuple-element.49.refs_2_), channel_id=1, source_target_pairs={{0,64},{1,65},{2,66},{3,67},{4,68},{5,69},{6,70},{7,71},{8,72},{9,... | collective-permute-start | bytes 2211848 | tf_op jit(solution)/shard_map/ppermute | solution.py:64
  100.5 6.8 %collective-permute-done.19.refs_4_ = bf16[128,1152]{1,0:T(8,128)(2,1)S(1)} collective-permute-done((bf16[128,1152]{1,0:T(8,128)(2,1)S(1)}, bf16[128,1152]{1,0:T(8,128)(2,1)S(1)}, u32[]{:S(2)}, u32[]{:S(2)}) %collective-permute-start.19) | collective-permute-done | bytes 294944 | tf_op jit(solution)/shard_map/ppermute | solution.py:64
  107.4 3.1 %collective-permute-start.20 = (bf16[64,1152]{1,0:T(8,128)(2,1)S(1)}, bf16[64,1152]{1,0:T(8,128)(2,1)S(1)}, u32[]{:S(2)}, u32[]{:S(2)}) collective-permute-start(bf16[64,1152]{1,0:T(8,128)(2,1)S(1)} %get-tuple-element.62), channel_id=1, source_target_pairs={{0,65},{1,64},{2,67},{3,66},{4,69},{5,68},{6,71},{7,70},{8,73},{9,... | collective-permute-start | bytes 442376 | tf_op jit(solution)/shard_map/ppermute | solution.py:64
  110.5 7.4 %collective-permute-done.21.back_ref = bf16[320,1152]{1,0:T(8,128)(2,1)S(1)} collective-permute-done((bf16[320,1152]{1,0:T(8,128)(2,1)S(1)}, bf16[320,1152]{1,0:T(8,128)(2,1)S(1)}, u32[]{:S(2)}, u32[]{:S(2)}) %collective-permute-start.21) | collective-permute-done | bytes 737312 | tf_op jit(solution)/shard_map/ppermute | solution.py:64
  117.9 3.1 %caption_grad.1 = (f32[512,1152]{1,0:T(8,128)}, bf16[208,1152]{1,0:T(8,128)(2,1)S(1)}, f32[208,1152]{1,0:T(8,128)S(1)}) custom-call(s32[1]{0:T(128)} %bitcast.2.refs_0_.total_ref, bf16[512,1152]{1,0:T(8,128)(2,1)S(1)} %copy-done.1, f32[512,1152]{1,0:T(8,128)S(1)} %get-tuple-element.53.own_ref, bf16[320,1152]{1,0:T(8,128)(2,1)S(1)} %collective-permute-done.21.back_ref), custom_call_target="tpu_custom_call" | custom-call | flops 603979776 | bytes 8388608 | tf_op jit(solution)/shard_map/caption_grad/pallas_call | solution.py:296
  121.0 1.9 %collective-permute-done.22.back_ref = bf16[192,1152]{1,0:T(8,128)(2,1)S(1)} collective-permute-done((bf16[192,1152]{1,0:T(8,128)(2,1)S(1)}, bf16[192,1152]{1,0:T(8,128)(2,1)S(1)}, u32[]{:S(2)}, u32[]{:S(2)}) %collective-permute-start.22) | collective-permute-done | bytes 442400 | tf_op jit(solution)/shard_map/ppermute | solution.py:64
  122.9 2.2 %caption_grad_last.1 = f32[512,1152]{1,0:T(8,128)} custom-call(s32[1]{0:T(128)} %bitcast.2.refs_0_.total_ref, bf16[208,1152]{1,0:T(8,128)(2,1)S(1)} %get-tuple-element.54.raw_ref, f32[208,1152]{1,0:T(8,128)S(1)} %get-tuple-element.55.sums_ref, bf16[192,1152]{1,0:T(8,128)(2,1)S(1)} %collective-permute-done.22.back_ref, ...), custom_call_target="tpu_custom_call", output_to_operand_aliasing={{}: (4, {})} | custom-call | flops 1000000 | bytes 1048576 | tf_op jit(solution)/shard_map/caption_grad_last/pallas_call | solution.py:320
  (56 shorter events, 13.1 us)
Async XLA Ops:
  0.6 27.9 %collective-permute-start.4 = (bf16[512,1152]{1,0:T(8,128)(2,1)}, bf16[512,1152]{1,0:T(8,128)(2,1)S(1)}, u32[]{:S(2)}, u32[]{:S(2)}) collective-permute-start(bf16[512,1152]{1,0:T(8,128)(2,1)} %raw_ref.1), channel_id=1, source_target_pairs={{0,64},{1,65},{2,66},{3,67},{4,68},{5,69},{6,70},{7,71},{8,72},{9,... | collective-permute-start | bytes 3538952 | tf_op jit(solution)/shard_map/ppermute | solution.py:64
  2.4 6.7 %collective-permute-start = (bf16[64,1152]{1,0:T(8,128)(2,1)}, bf16[64,1152]{1,0:T(8,128)(2,1)S(1)}, u32[]{:S(2)}, u32[]{:S(2)}) collective-permute-start(bf16[64,1152]{1,0:T(8,128)(2,1)} %refs_0_.3), channel_id=1, source_target_pairs={{0,65},{1,64},{2,67},{3,66},{4,69},{5,68},{6,71},{7,70},{8,73},{9,... | collective-permute-start | bytes 442376 | tf_op jit(solution)/shard_map/ppermute | solution.py:64
  4.6 0.9 copy-start.2
  9.2 8.9 %collective-permute-start.3 = (bf16[128,1152]{1,0:T(8,128)(2,1)S(1)}, bf16[128,1152]{1,0:T(8,128)(2,1)S(1)}, u32[]{:S(2)}, u32[]{:S(2)}) collective-permute-start(bf16[128,1152]{1,0:T(8,128)(2,1)S(1)} %shard_map.69.refs_0_), channel_id=1, source_target_pairs={{0,32},{1,33},{2,34},{3,35},{4,36},{5,37},{6,38},{7,39},{8,12},{9,... | collective-permute-start | bytes 884744 | tf_op jit(solution)/shard_map/ppermute | solution.py:64
  12.4 8.5 %collective-permute-start.2 = (bf16[128,1152]{1,0:T(8,128)(2,1)S(1)}, bf16[128,1152]{1,0:T(8,128)(2,1)S(1)}, u32[]{:S(2)}, u32[]{:S(2)}) collective-permute-start(bf16[128,1152]{1,0:T(8,128)(2,1)S(1)} %shard_map.69.refs_0_), channel_id=1, source_target_pairs={{0,48},{1,49},{2,50},{3,51},{4,52},{5,53},{6,54},{7,55},{8,14},{9,... | collective-permute-start | bytes 884744 | tf_op jit(solution)/shard_map/ppermute | solution.py:64
  13.5 7.9 %collective-permute-start.1 = (bf16[128,1152]{1,0:T(8,128)(2,1)S(1)}, bf16[128,1152]{1,0:T(8,128)(2,1)S(1)}, u32[]{:S(2)}, u32[]{:S(2)}) collective-permute-start(bf16[128,1152]{1,0:T(8,128)(2,1)S(1)} %shard_map.69.refs_0_), channel_id=1, source_target_pairs={{0,16},{1,17},{2,18},{3,19},{4,20},{5,21},{6,22},{7,23},{8,10},{9,... | collective-permute-start | bytes 884744 | tf_op jit(solution)/shard_map/ppermute | solution.py:64
  15.8 1.3 %copy-start = (bf16[512,1152]{1,0:T(8,128)(2,1)S(1)}, bf16[512,1152]{1,0:T(8,128)(2,1)}, u32[]{:S(2)}) copy-start(bf16[512,1152]{1,0:T(8,128)(2,1)} %raw_ref.1) | copy-start | bytes 3538948
  21.5 24.5 %copy-start.4 = (bf16[256,1152]{1,0:T(8,128)(2,1)}, bf16[256,1152]{1,0:T(8,128)(2,1)S(1)}, u32[]{:S(2)}) copy-start(bf16[256,1152]{1,0:T(8,128)(2,1)S(1)} %get-tuple-element.31.refs_3_) | copy-start | bytes 1769476
  30.4 16.0 %collective-permute-start.5 = (bf16[576,1152]{1,0:T(8,128)(2,1)S(1)}, bf16[576,1152]{1,0:T(8,128)(2,1)S(1)}, u32[]{:S(2)}, u32[]{:S(2)}) collective-permute-start(bf16[576,1152]{1,0:T(8,128)(2,1)S(1)} %shard_map.72.refs_0_), channel_id=1, source_target_pairs={{0,8},{1,9},{2,10},{3,11},{4,12},{5,13},{6,14},{7,15},{8,0},{9,1},... | collective-permute-start | bytes 3981320 | tf_op jit(solution)/shard_map/ppermute | solution.py:64
  30.5 11.7 %collective-permute-start.8 = (bf16[256,1152]{1,0:T(8,128)(2,1)S(1)}, bf16[256,1152]{1,0:T(8,128)(2,1)}, u32[]{:S(2)}, u32[]{:S(2)}) collective-permute-start(bf16[256,1152]{1,0:T(8,128)(2,1)S(1)} %get-tuple-element.31.refs_3_), channel_id=1, source_target_pairs={{0,6},{1,7},{2,0},{3,1},{4,2},{5,3},{6,4},{7,5},{8,56},{9,57},{10,... | collective-permute-start | bytes 1769480 | tf_op jit(solution)/shard_map/ppermute | solution.py:64
  34.8 11.2 %collective-permute-start.6 = (bf16[256,1152]{1,0:T(8,128)(2,1)S(1)}, bf16[256,1152]{1,0:T(8,128)(2,1)}, u32[]{:S(2)}, u32[]{:S(2)}) collective-permute-start(bf16[256,1152]{1,0:T(8,128)(2,1)S(1)} %get-tuple-element.30.refs_3_.refs_2_), channel_id=1, source_target_pairs={{0,2},{1,3},{2,4},{3,5},{4,6},{5,7},{6,0},{7,1},{8,24},{9,25},{10,... | collective-permute-start | bytes 1769480 | tf_op jit(solution)/shard_map/ppermute | solution.py:64
  34.8 14.9 %collective-permute-start.10 = (bf16[256,1152]{1,0:T(8,128)(2,1)S(1)}, bf16[256,1152]{1,0:T(8,128)(2,1)}, u32[]{:S(2)}, u32[]{:S(2)}) collective-permute-start(bf16[256,1152]{1,0:T(8,128)(2,1)S(1)} %get-tuple-element.30.refs_3_.refs_2_), channel_id=1, source_target_pairs={{0,6},{1,7},{2,0},{3,1},{4,2},{5,3},{6,4},{7,5},{8,56},{9,57},{10,... | collective-permute-start | bytes 1769480 | tf_op jit(solution)/shard_map/ppermute | solution.py:64
  42.2 12.7 %collective-permute-start.9 = (bf16[256,1152]{1,0:T(8,128)(2,1)}, bf16[256,1152]{1,0:T(8,128)(2,1)}, u32[]{:S(2)}, u32[]{:S(2)}) collective-permute-start(bf16[256,1152]{1,0:T(8,128)(2,1)} %collective-permute-done.8.refs_3_), channel_id=1, source_target_pairs={{0,6},{1,7},{2,0},{3,1},{4,2},{5,3},{6,4},{7,5},{8,56},{9,57},{10,... | collective-permute-start | bytes 1769480 | tf_op jit(solution)/shard_map/ppermute | solution.py:64
  46.0 11.4 %collective-permute-start.7 = (bf16[256,1152]{1,0:T(8,128)(2,1)}, bf16[256,1152]{1,0:T(8,128)(2,1)}, u32[]{:S(2)}, u32[]{:S(2)}) collective-permute-start(bf16[256,1152]{1,0:T(8,128)(2,1)} %collective-permute-done.6.refs_2_), channel_id=1, source_target_pairs={{0,2},{1,3},{2,4},{3,5},{4,6},{5,7},{6,0},{7,1},{8,24},{9,25},{10,... | collective-permute-start | bytes 1769480 | tf_op jit(solution)/shard_map/ppermute | solution.py:64
  46.2 1.1 copy-start.5
  46.2 18.3 %collective-permute-start.11 = (bf16[256,1152]{1,0:T(8,128)(2,1)}, bf16[256,1152]{1,0:T(8,128)(2,1)S(1)}, u32[]{:S(2)}, u32[]{:S(2)}) collective-permute-start(bf16[256,1152]{1,0:T(8,128)(2,1)} %copy-done.4), channel_id=1, source_target_pairs={{0,2},{1,3},{2,4},{3,5},{4,6},{5,7},{6,0},{7,1},{8,24},{9,25},{10,... | collective-permute-start | bytes 1769480 | tf_op jit(solution)/shard_map/ppermute | solution.py:64
  62.4 10.6 %collective-permute-start.13 = (bf16[256,1152]{1,0:T(8,128)(2,1)S(1)}, bf16[256,1152]{1,0:T(8,128)(2,1)S(1)}, u32[]{:S(2)}, u32[]{:S(2)}) collective-permute-start(bf16[256,1152]{1,0:T(8,128)(2,1)S(1)} %get-tuple-element.45), channel_id=1, source_target_pairs={{0,6},{1,7},{2,0},{3,1},{4,2},{5,3},{6,4},{7,5},{8,56},{9,57},{10,... | collective-permute-start | bytes 1769480 | tf_op jit(solution)/shard_map/ppermute | solution.py:64
  63.7 11.1 %collective-permute-start.12 = (bf16[256,1152]{1,0:T(8,128)(2,1)S(1)}, bf16[256,1152]{1,0:T(8,128)(2,1)S(1)}, u32[]{:S(2)}, u32[]{:S(2)}) collective-permute-start(bf16[256,1152]{1,0:T(8,128)(2,1)S(1)} %get-tuple-element.36.refs_5_), channel_id=1, source_target_pairs={{0,2},{1,3},{2,4},{3,5},{4,6},{5,7},{6,0},{7,1},{8,24},{9,25},{10,... | collective-permute-start | bytes 1769480 | tf_op jit(solution)/shard_map/ppermute | solution.py:64
  72.9 8.5 %collective-permute-start.14 = (bf16[576,1152]{1,0:T(8,128)(2,1)S(1)}, bf16[576,1152]{1,0:T(8,128)(2,1)S(1)}, u32[]{:S(2)}, u32[]{:S(2)}) collective-permute-start(bf16[576,1152]{1,0:T(8,128)(2,1)S(1)} %get-tuple-element.46.refs_6_), channel_id=1, source_target_pairs={{0,8},{1,9},{2,10},{3,11},{4,12},{5,13},{6,14},{7,15},{8,0},{9,1},... | collective-permute-start | bytes 3981320 | tf_op jit(solution)/shard_map/ppermute | solution.py:64
  75.1 17.5 %collective-permute-start.15 = (bf16[512,1152]{1,0:T(8,128)(2,1)S(1)}, bf16[512,1152]{1,0:T(8,128)(2,1)S(1)}, u32[]{:S(2)}, u32[]{:S(2)}) collective-permute-start(bf16[512,1152]{1,0:T(8,128)(2,1)S(1)} %get-tuple-element.51), channel_id=1, source_target_pairs={{0,2},{1,3},{2,4},{3,5},{4,6},{5,7},{6,0},{7,1},{8,24},{9,25},{10,... | collective-permute-start | bytes 3538952 | tf_op jit(solution)/shard_map/ppermute | solution.py:64
  75.2 17.6 %collective-permute-start.16 = (bf16[512,1152]{1,0:T(8,128)(2,1)S(1)}, bf16[512,1152]{1,0:T(8,128)(2,1)S(1)}, u32[]{:S(2)}, u32[]{:S(2)}) collective-permute-start(bf16[512,1152]{1,0:T(8,128)(2,1)S(1)} %get-tuple-element.47.refs_8_), channel_id=1, source_target_pairs={{0,6},{1,7},{2,0},{3,1},{4,2},{5,3},{6,4},{7,5},{8,56},{9,57},{10,... | collective-permute-start | bytes 3538952 | tf_op jit(solution)/shard_map/ppermute | solution.py:64
  93.3 24.5 %copy-start.1 = (bf16[512,1152]{1,0:T(8,128)(2,1)S(1)}, bf16[512,1152]{1,0:T(8,128)(2,1)}, u32[]{:S(2)}) copy-start(bf16[512,1152]{1,0:T(8,128)(2,1)} %raw_ref.1) | copy-start | bytes 3538948
  93.4 7.2 %collective-permute-start.18 = (bf16[128,1152]{1,0:T(8,128)(2,1)S(1)}, bf16[128,1152]{1,0:T(8,128)(2,1)S(1)}, u32[]{:S(2)}, u32[]{:S(2)}) collective-permute-start(bf16[128,1152]{1,0:T(8,128)(2,1)S(1)} %slice.84), channel_id=1, source_target_pairs={{0,48},{1,49},{2,50},{3,51},{4,52},{5,53},{6,54},{7,55},{8,14},{9,... | collective-permute-start | bytes 884744 | tf_op jit(solution)/shard_map/ppermute | solution.py:64
  96.2 11.1 %collective-permute-start.19 = (bf16[128,1152]{1,0:T(8,128)(2,1)S(1)}, bf16[128,1152]{1,0:T(8,128)(2,1)S(1)}, u32[]{:S(2)}, u32[]{:S(2)}) collective-permute-start(bf16[128,1152]{1,0:T(8,128)(2,1)S(1)} %get-tuple-element.64), channel_id=1, source_target_pairs={{0,16},{1,17},{2,18},{3,19},{4,20},{5,21},{6,22},{7,23},{8,10},{9,... | collective-permute-start | bytes 884744 | tf_op jit(solution)/shard_map/ppermute | solution.py:64
  96.2 11.1 %collective-permute-start.17 = (bf16[128,1152]{1,0:T(8,128)(2,1)S(1)}, bf16[128,1152]{1,0:T(8,128)(2,1)S(1)}, u32[]{:S(2)}, u32[]{:S(2)}) collective-permute-start(bf16[128,1152]{1,0:T(8,128)(2,1)S(1)} %get-tuple-element.65), channel_id=1, source_target_pairs={{0,32},{1,33},{2,34},{3,35},{4,36},{5,37},{6,38},{7,39},{8,12},{9,... | collective-permute-start | bytes 884744 | tf_op jit(solution)/shard_map/ppermute | solution.py:64
  98.5 19.4 %collective-permute-start.21 = (bf16[320,1152]{1,0:T(8,128)(2,1)S(1)}, bf16[320,1152]{1,0:T(8,128)(2,1)S(1)}, u32[]{:S(2)}, u32[]{:S(2)}) collective-permute-start(bf16[320,1152]{1,0:T(8,128)(2,1)S(1)} %get-tuple-element.49.refs_2_), channel_id=1, source_target_pairs={{0,64},{1,65},{2,66},{3,67},{4,68},{5,69},{6,70},{7,71},{8,72},{9,... | collective-permute-start | bytes 2211848 | tf_op jit(solution)/shard_map/ppermute | solution.py:64
  100.1 22.8 %collective-permute-start.22 = (bf16[192,1152]{1,0:T(8,128)(2,1)S(1)}, bf16[192,1152]{1,0:T(8,128)(2,1)S(1)}, u32[]{:S(2)}, u32[]{:S(2)}) collective-permute-start(bf16[192,1152]{1,0:T(8,128)(2,1)S(1)} %get-tuple-element.56), channel_id=1, source_target_pairs={{0,64},{1,65},{2,66},{3,67},{4,68},{5,69},{6,70},{7,71},{8,72},{9,... | collective-permute-start | bytes 1327112 | tf_op jit(solution)/shard_map/ppermute | solution.py:64
  107.4 17.7 %collective-permute-start.20 = (bf16[64,1152]{1,0:T(8,128)(2,1)S(1)}, bf16[64,1152]{1,0:T(8,128)(2,1)S(1)}, u32[]{:S(2)}, u32[]{:S(2)}) collective-permute-start(bf16[64,1152]{1,0:T(8,128)(2,1)S(1)} %get-tuple-element.62), channel_id=1, source_target_pairs={{0,65},{1,64},{2,67},{3,66},{4,69},{5,68},{6,71},{7,70},{8,73},{9,... | collective-permute-start | bytes 442376 | tf_op jit(solution)/shard_map/ppermute | solution.py:64
  122.9 2.2 %copy-start.3 = (bf16[64,1152]{1,0:T(8,128)(2,1)S(1)}, bf16[64,1152]{1,0:T(8,128)(2,1)}, u32[]{:S(2)}) copy-start(bf16[64,1152]{1,0:T(8,128)(2,1)} %refs_0_.3) | copy-start | bytes 442372

commit v4 on v3

--- a/solution.py
+++ b/solution.py
@@ -99,12 +99,15 @@
     )(*args, *after)
 
 
-def prep_kernel(total_ref, own_ref, out_ref):
+def prep_kernel(total_ref, own_ref, out_ref, pick_ref):
     slots = own_ref.shape[0]
     low = unit_rows(own_ref[...])[0]
     slot = lax.broadcasted_iota(jnp.int32, low.shape, 0)
     out_ref[:slots] = jnp.where(slot < total_ref[0], low, 0.0).astype(BF16)
     out_ref[slots:] = jnp.zeros((out_ref.shape[0] - slots, low.shape[1]), BF16)
+    row = lax.broadcasted_iota(jnp.int32, pick_ref.shape, 0)
+    column = lax.broadcasted_iota(jnp.int32, pick_ref.shape, 1)
+    pick_ref[...] = jnp.where(column == row - total_ref[0], 1.0, 0.0).astype(BF16)
 
 
 def picked(rows, columns, offset, values):
@@ -114,10 +117,10 @@
     return jnp.dot(pick, values, preferred_element_type=F32)
 
 
-def merge_kernel(total_ref, own_ref, raw_ref, out_ref):
+def merge_kernel(own_ref, pick_ref, raw_ref, out_ref):
     low = unit_rows(raw_ref[...])[0].astype(BF16)
-    other = picked(out_ref.shape[0], low.shape[0], -total_ref[0], low)
-    out_ref[...] = (own_ref[...].astype(F32) + other).astype(BF16)
+    other = jnp.dot(pick_ref[...], low, preferred_element_type=F32).astype(BF16)
+    out_ref[...] = own_ref[...] + other
 
 
 def stack_kernel(own_ref, other_ref, out_ref):
@@ -356,9 +359,12 @@
     first = {}
     for k in (2, 1, 3):
         first[k] = send(near, ring_route(0, k))
-    own_pad = plain(
+    own_pad, pick = plain(
         prep_kernel,
-        jax.ShapeDtypeStruct((pair_rows, width), BF16),
+        (
+            jax.ShapeDtypeStruct((pair_rows, width), BF16),
+            jax.ShapeDtypeStruct((pair_rows, slots), BF16),
+        ),
         (total, caption_vectors),
         smem=1,
     )
@@ -375,9 +381,8 @@
     own_pair = plain(
         merge_kernel,
         jax.ShapeDtypeStruct((pair_rows, width), BF16),
-        (total, own_pad, partner_raw),
+        (own_pad, pick, partner_raw),
         2 * pair_rows * slots * width,
-        1,
         after=(head,),
     )
     other_pair = send(own_pair, flip_route(2))

time: 126 us -> 126 us (level)
  no operation moved by 1% of the time
where the time goes in v4:
time: 126 us; the launch traced here: 125 us
  waiting for transfers between devices  46 us (37%)
  starting transfers between devices  36.4 us (29%)
  Pallas kernels  35.4 us (28%)
  local copies, waits for them, and re-layouts  3.05 us (2%)
  other arithmetic  2.32 us (2%)
  between operations  2.28 us (2%)
    ppermute x23, waiting for transfers between devices, send(): return lax.ppermute(value, AXES, pairs)  46 us
    ppermute x23, starting transfers between devices, send(): return lax.ppermute(value, AXES, pairs)  36.4 us
    pallas_call x4, Pallas kernels, weight_terms(): pl.pallas_call(lambda *refs: weight_kernel(local, bool(types), *refs[:ari...  17.1 us
    pallas_call x12, Pallas kernels, plain(): pl.pallas_call(lambda *refs: kernel(*refs[:len(args)], *refs[len(args) +...  13 us
    pallas_call x1, Pallas kernels, caption_grads(): pl.pallas_call(functools.partial(home_kernel, last), out_shape=(jax.Shape...  3.11 us
    unnamed x12, local copies, waits for them, and re-layouts  2.88 us
  transfers between devices with their start and end apart: 23, of which 12 were waited for; matrix products, arithmetic and copies ran while one was open for 2% of the time, Pallas kernels for 26%

profile of v4, /device:TPU:0, one launch (start us, length us, event | category | flops | bytes accessed | tf_op | source)
XLA Modules:
  0.0 125.4 jit_solution(10080781427686420496)
XLA Ops:
  0.6 1.8 %collective-permute-start.4 = (bf16[512,1152]{1,0:T(8,128)(2,1)}, bf16[512,1152]{1,0:T(8,128)(2,1)S(1)}, u32[]{:S(2)}, u32[]{:S(2)}) collective-permute-start(bf16[512,1152]{1,0:T(8,128)(2,1)} %raw_ref.1), channel_id=1, source_target_pairs={{0,64},{1,65},{2,66},{3,67},{4,68},{5,69},{6,70},{7,71},{8,72},{9,... | collective-permute-start | bytes 3538952 | tf_op jit(solution)/shard_map/ppermute | solution.py:64
  2.4 2.2 %collective-permute-start = (bf16[64,1152]{1,0:T(8,128)(2,1)}, bf16[64,1152]{1,0:T(8,128)(2,1)S(1)}, u32[]{:S(2)}, u32[]{:S(2)}) collective-permute-start(bf16[64,1152]{1,0:T(8,128)(2,1)} %refs_0_.3), channel_id=1, source_target_pairs={{0,65},{1,64},{2,67},{3,66},{4,69},{5,68},{6,71},{7,70},{8,73},{9,... | collective-permute-start | bytes 442376 | tf_op jit(solution)/shard_map/ppermute | solution.py:64
  5.6 3.5 %collective-permute-done.refs_1_ = bf16[64,1152]{1,0:T(8,128)(2,1)S(1)} collective-permute-done((bf16[64,1152]{1,0:T(8,128)(2,1)}, bf16[64,1152]{1,0:T(8,128)(2,1)S(1)}, u32[]{:S(2)}, u32[]{:S(2)}) %collective-permute-start) | collective-permute-done | bytes 147488 | tf_op jit(solution)/shard_map/ppermute | solution.py:64
  9.2 3.1 %collective-permute-start.3 = (bf16[128,1152]{1,0:T(8,128)(2,1)S(1)}, bf16[128,1152]{1,0:T(8,128)(2,1)S(1)}, u32[]{:S(2)}, u32[]{:S(2)}) collective-permute-start(bf16[128,1152]{1,0:T(8,128)(2,1)S(1)} %shard_map.69.refs_0_), channel_id=1, source_target_pairs={{0,32},{1,33},{2,34},{3,35},{4,36},{5,37},{6,38},{7,39},{8,12},{9,... | collective-permute-start | bytes 884744 | tf_op jit(solution)/shard_map/ppermute | solution.py:64
  14.4 1.4 %fusion.4 = (s32[]{:T(128)}, s32[64]{0:T(128)S(1)}) fusion(s32[8192]{0:T(1024)} %param.7, s32[]{:T(128)S(6)} %select_n.7), kind=kLoop, calls=%fused_computation.15 | loop fusion | flops 63 | bytes 520 | tf_op jit(solution)/shard_map/reduce_sum | solution.py:352
  18.3 2.6 %collective-permute-done.2.refs_2_ = bf16[128,1152]{1,0:T(8,128)(2,1)S(1)} collective-permute-done((bf16[128,1152]{1,0:T(8,128)(2,1)S(1)}, bf16[128,1152]{1,0:T(8,128)(2,1)S(1)}, u32[]{:S(2)}, u32[]{:S(2)}) %collective-permute-start.2) | collective-permute-done | bytes 294944 | tf_op jit(solution)/shard_map/ppermute | solution.py:64
  21.5 7.0 %collective-permute-done.4.refs_2_ = bf16[512,1152]{1,0:T(8,128)(2,1)S(1)} collective-permute-done((bf16[512,1152]{1,0:T(8,128)(2,1)}, bf16[512,1152]{1,0:T(8,128)(2,1)S(1)}, u32[]{:S(2)}, u32[]{:S(2)}) %collective-permute-start.4) | collective-permute-done | bytes 1179680 | tf_op jit(solution)/shard_map/ppermute | solution.py:64
  29.9 4.3 %collective-permute-start.8 = (bf16[256,1152]{1,0:T(8,128)(2,1)S(1)}, bf16[256,1152]{1,0:T(8,128)(2,1)}, u32[]{:S(2)}, u32[]{:S(2)}) collective-permute-start(bf16[256,1152]{1,0:T(8,128)(2,1)S(1)} %get-tuple-element.34.refs_3_), channel_id=1, source_target_pairs={{0,6},{1,7},{2,0},{3,1},{4,2},{5,3},{6,4},{7,5},{8,56},{9,57},{10,... | collective-permute-start | bytes 1769480 | tf_op jit(solution)/shard_map/ppermute | solution.py:64
  34.2 3.2 %collective-permute-start.10 = (bf16[256,1152]{1,0:T(8,128)(2,1)S(1)}, bf16[256,1152]{1,0:T(8,128)(2,1)}, u32[]{:S(2)}, u32[]{:S(2)}) collective-permute-start(bf16[256,1152]{1,0:T(8,128)(2,1)S(1)} %get-tuple-element.33.refs_3_.refs_2_), channel_id=1, source_target_pairs={{0,6},{1,7},{2,0},{3,1},{4,2},{5,3},{6,4},{7,5},{8,56},{9,57},{10,... | collective-permute-start | bytes 1769480 | tf_op jit(solution)/shard_map/ppermute | solution.py:64
  38.9 2.7 %collective-permute-done.8.refs_3_ = bf16[256,1152]{1,0:T(8,128)(2,1)} collective-permute-done((bf16[256,1152]{1,0:T(8,128)(2,1)S(1)}, bf16[256,1152]{1,0:T(8,128)(2,1)}, u32[]{:S(2)}, u32[]{:S(2)}) %collective-permute-start.8) | collective-permute-done | bytes 589856 | tf_op jit(solution)/shard_map/ppermute | solution.py:64
  41.6 3.8 %collective-permute-start.9 = (bf16[256,1152]{1,0:T(8,128)(2,1)}, bf16[256,1152]{1,0:T(8,128)(2,1)}, u32[]{:S(2)}, u32[]{:S(2)}) collective-permute-start(bf16[256,1152]{1,0:T(8,128)(2,1)} %collective-permute-done.8.refs_3_), channel_id=1, source_target_pairs={{0,6},{1,7},{2,0},{3,1},{4,2},{5,3},{6,4},{7,5},{8,56},{9,57},{10,... | collective-permute-start | bytes 1769480 | tf_op jit(solution)/shard_map/ppermute | solution.py:64
  46.6 2.4 %block_local.1 = (bf16[512,1152]{1,0:T(8,128)(2,1)S(1)}, bf16[512,1152]{1,0:T(8,128)(2,1)S(1)}) custom-call(f32[2]{0:T(128)S(1)} %pad_maximum_fusion.refs_0_, s32[64,2]{1,0:T(8,128)S(1)} %copy.14.refs_1_, bf16[256,1152]{1,0:T(8,128)(2,1)S(1)} %get-tuple-element.33.refs_3_.refs_2_, bf16[256,1152]{1,0:T(8,128)(2,1)S(1)} %copy-done.5, ...), custom_call_target="tpu_custom_call" | custom-call | flops 1358954496 | bytes 8388608 | tf_op jit(solution)/shard_map/block_local/pallas_call | solution.py:169
  49.1 4.9 %block_remote.3 = (bf16[512,1152]{1,0:T(8,128)(2,1)S(1)}, bf16[512,1152]{1,0:T(8,128)(2,1)S(1)}, f32[256,1152]{1,0:T(8,128)S(1)}, bf16[256,1152]{1,0:T(8,128)(2,1)S(1)}) custom-call(f32[2]{0:T(128)S(1)} %pad_maximum_fusion.refs_0_, s32[64,2]{1,0:T(8,128)S(1)} %copy.14.refs_1_, bf16[256,1152]{1,0:T(8,128)(2,1)} %collective-permute-done.10.refs_2_, ...), custom_call_target="tpu_custom_call" | custom-call | flops 2717908992 | bytes 8388608 | tf_op jit(solution)/shard_map/block_remote/pallas_call | solution.py:169
  54.3 2.5 %collective-permute-done.7.refs_2_ = bf16[256,1152]{1,0:T(8,128)(2,1)} collective-permute-done((bf16[256,1152]{1,0:T(8,128)(2,1)}, bf16[256,1152]{1,0:T(8,128)(2,1)}, u32[]{:S(2)}, u32[]{:S(2)}) %collective-permute-start.7) | collective-permute-done | bytes 589856 | tf_op jit(solution)/shard_map/ppermute | solution.py:64
  56.8 4.9 %block_remote.4 = (bf16[512,1152]{1,0:T(8,128)(2,1)S(1)}, bf16[512,1152]{1,0:T(8,128)(2,1)S(1)}, bf16[256,1152]{1,0:T(8,128)(2,1)S(1)}, bf16[256,1152]{1,0:T(8,128)(2,1)S(1)}) custom-call(f32[2]{0:T(128)S(1)} %pad_maximum_fusion.refs_0_, s32[64,2]{1,0:T(8,128)S(1)} %copy.14.refs_1_, bf16[256,1152]{1,0:T(8,128)(2,1)} %collective-permute-done.7.refs_2_, ...), custom_call_target="tpu_custom_call" | custom-call | flops 2717908992 | bytes 8388608 | tf_op jit(solution)/shard_map/block_remote/pallas_call | solution.py:169
  61.7 1.3 %collective-permute-start.13 = (bf16[256,1152]{1,0:T(8,128)(2,1)S(1)}, bf16[256,1152]{1,0:T(8,128)(2,1)S(1)}, u32[]{:S(2)}, u32[]{:S(2)}) collective-permute-start(bf16[256,1152]{1,0:T(8,128)(2,1)S(1)} %get-tuple-element.49), channel_id=1, source_target_pairs={{0,6},{1,7},{2,0},{3,1},{4,2},{5,3},{6,4},{7,5},{8,56},{9,57},{10,... | collective-permute-start | bytes 1769480 | tf_op jit(solution)/shard_map/ppermute | solution.py:64
  63.8 4.8 %block_remote.5 = (bf16[512,1152]{1,0:T(8,128)(2,1)S(1)}, bf16[512,1152]{1,0:T(8,128)(2,1)S(1)}, bf16[256,1152]{1,0:T(8,128)(2,1)S(1)}, f32[256,1152]{1,0:T(8,128)S(1)}) custom-call(f32[2]{0:T(128)S(1)} %pad_maximum_fusion.refs_0_, s32[64,2]{1,0:T(8,128)S(1)} %copy.14.refs_1_, bf16[256,1152]{1,0:T(8,128)(2,1)} %collective-permute-done.6.refs_2_, ...), custom_call_target="tpu_custom_call" | custom-call | flops 2717908992 | bytes 8388608 | tf_op jit(solution)/shard_map/block_remote/pallas_call | solution.py:169
  68.6 3.6 %shard_map.74 = (bf16[576,1152]{1,0:T(8,128)(2,1)S(1)}, f32[64,1152]{1,0:T(8,128)S(1)}) custom-call(bf16[512,1152]{1,0:T(8,128)(2,1)S(1)} %get-tuple-element.36.refs_5_.refs_0_, bf16[512,1152]{1,0:T(8,128)(2,1)S(1)} %get-tuple-element.38.refs_1_, bf16[512,1152]{1,0:T(8,128)(2,1)S(1)} %get-tuple-element.39.refs_2_, ...), custom_call_target="tpu_custom_call" | custom-call | flops 2717908992 | bytes 1048576 | tf_op jit(solution)/shard_map/pallas_call | solution.py:92
  72.3 1.8 %collective-permute-done.12.refs_2_ = bf16[256,1152]{1,0:T(8,128)(2,1)S(1)} collective-permute-done((bf16[256,1152]{1,0:T(8,128)(2,1)S(1)}, bf16[256,1152]{1,0:T(8,128)(2,1)S(1)}, u32[]{:S(2)}, u32[]{:S(2)}) %collective-permute-start.12) | collective-permute-done | bytes 589856 | tf_op jit(solution)/shard_map/ppermute | solution.py:64
  74.5 3.2 %collective-permute-start.16 = (bf16[512,1152]{1,0:T(8,128)(2,1)S(1)}, bf16[512,1152]{1,0:T(8,128)(2,1)S(1)}, u32[]{:S(2)}, u32[]{:S(2)}) collective-permute-start(bf16[512,1152]{1,0:T(8,128)(2,1)S(1)} %get-tuple-element.51.refs_8_), channel_id=1, source_target_pairs={{0,6},{1,7},{2,0},{3,1},{4,2},{5,3},{6,4},{7,5},{8,56},{9,57},{10,... | collective-permute-start | bytes 3538952 | tf_op jit(solution)/shard_map/ppermute | solution.py:64
  77.8 2.9 %shard_map.76.refs_0_ = f32[512,1152]{1,0:T(8,128)S(1)} custom-call(bf16[512,1152]{1,0:T(8,128)(2,1)S(1)} %get-tuple-element.36.refs_5_.refs_0_, bf16[512,1152]{1,0:T(8,128)(2,1)S(1)} %get-tuple-element.38.refs_1_, bf16[512,1152]{1,0:T(8,128)(2,1)S(1)} %get-tuple-element.39.refs_2_, bf16[512,1152]{1,0:T(8,128)(2,1)S(1)} %get-tuple-element.41.refs_3_, ...), custom_call_target="tpu_custom_call" | custom-call | flops 2717908992 | bytes 1048576 | tf_op jit(solution)/shard_map/pallas_call | solution.py:92
  81.1 1.8 %shard_map.78 = (f32[256,1152]{1,0:T(8,128)S(1)}, f32[256,1152]{1,0:T(8,128)S(1)}) custom-call(bf16[512,1152]{1,0:T(8,128)(2,1)S(1)} %get-tuple-element.36.refs_5_.refs_0_, bf16[1152,1152]{1,0:T(8,128)(2,1)S(1)} %shard_map.73.refs_4_.refs_1_, bf16[320,1152]{1,0:T(8,128)(2,1)S(1)} %get-tuple-element.53.refs_2_), custom_call_target="tpu_custom_call" | custom-call | flops 1358954496 | bytes 1048576 | tf_op jit(solution)/shard_map/pallas_call | solution.py:92
  82.9 9.0 %collective-permute-done.15 = bf16[512,1152]{1,0:T(8,128)(2,1)S(1)} collective-permute-done((bf16[512,1152]{1,0:T(8,128)(2,1)S(1)}, bf16[512,1152]{1,0:T(8,128)(2,1)S(1)}, u32[]{:S(2)}, u32[]{:S(2)}) %collective-permute-start.15) | collective-permute-done | bytes 1179680 | tf_op jit(solution)/shard_map/ppermute | solution.py:64
  92.7 2.8 %collective-permute-start.18 = (bf16[128,1152]{1,0:T(8,128)(2,1)S(1)}, bf16[128,1152]{1,0:T(8,128)(2,1)S(1)}, u32[]{:S(2)}, u32[]{:S(2)}) collective-permute-start(bf16[128,1152]{1,0:T(8,128)(2,1)S(1)} %slice.84), channel_id=1, source_target_pairs={{0,48},{1,49},{2,50},{3,51},{4,52},{5,53},{6,54},{7,55},{8,14},{9,... | collective-permute-start | bytes 884744 | tf_op jit(solution)/shard_map/ppermute | solution.py:64
  95.6 2.3 %collective-permute-start.17 = (bf16[128,1152]{1,0:T(8,128)(2,1)S(1)}, bf16[128,1152]{1,0:T(8,128)(2,1)S(1)}, u32[]{:S(2)}, u32[]{:S(2)}) collective-permute-start(bf16[128,1152]{1,0:T(8,128)(2,1)S(1)} %get-tuple-element.69), channel_id=1, source_target_pairs={{0,32},{1,33},{2,34},{3,35},{4,36},{5,37},{6,38},{7,39},{8,12},{9,... | collective-permute-start | bytes 884744 | tf_op jit(solution)/shard_map/ppermute | solution.py:64
  97.8 1.6 %collective-permute-start.21 = (bf16[320,1152]{1,0:T(8,128)(2,1)S(1)}, bf16[320,1152]{1,0:T(8,128)(2,1)S(1)}, u32[]{:S(2)}, u32[]{:S(2)}) collective-permute-start(bf16[320,1152]{1,0:T(8,128)(2,1)S(1)} %get-tuple-element.53.refs_2_), channel_id=1, source_target_pairs={{0,64},{1,65},{2,66},{3,67},{4,68},{5,69},{6,70},{7,71},{8,72},{9,... | collective-permute-start | bytes 2211848 | tf_op jit(solution)/shard_map/ppermute | solution.py:64
  99.9 6.8 %collective-permute-done.19.refs_4_ = bf16[128,1152]{1,0:T(8,128)(2,1)S(1)} collective-permute-done((bf16[128,1152]{1,0:T(8,128)(2,1)S(1)}, bf16[128,1152]{1,0:T(8,128)(2,1)S(1)}, u32[]{:S(2)}, u32[]{:S(2)}) %collective-permute-start.19) | collective-permute-done | bytes 294944 | tf_op jit(solution)/shard_map/ppermute | solution.py:64
  106.7 3.1 %collective-permute-start.20 = (bf16[64,1152]{1,0:T(8,128)(2,1)S(1)}, bf16[64,1152]{1,0:T(8,128)(2,1)S(1)}, u32[]{:S(2)}, u32[]{:S(2)}) collective-permute-start(bf16[64,1152]{1,0:T(8,128)(2,1)S(1)} %get-tuple-element.66), channel_id=1, source_target_pairs={{0,65},{1,64},{2,67},{3,66},{4,69},{5,68},{6,71},{7,70},{8,73},{9,... | collective-permute-start | bytes 442376 | tf_op jit(solution)/shard_map/ppermute | solution.py:64
  109.8 7.4 %collective-permute-done.21.back_ref = bf16[320,1152]{1,0:T(8,128)(2,1)S(1)} collective-permute-done((bf16[320,1152]{1,0:T(8,128)(2,1)S(1)}, bf16[320,1152]{1,0:T(8,128)(2,1)S(1)}, u32[]{:S(2)}, u32[]{:S(2)}) %collective-permute-start.21) | collective-permute-done | bytes 737312 | tf_op jit(solution)/shard_map/ppermute | solution.py:64
  117.2 3.1 %caption_grad.1 = (f32[512,1152]{1,0:T(8,128)}, bf16[208,1152]{1,0:T(8,128)(2,1)S(1)}, f32[208,1152]{1,0:T(8,128)S(1)}) custom-call(s32[1]{0:T(128)} %bitcast.2.refs_0_.total_ref, bf16[512,1152]{1,0:T(8,128)(2,1)S(1)} %copy-done.1, f32[512,1152]{1,0:T(8,128)S(1)} %get-tuple-element.57.own_ref, bf16[320,1152]{1,0:T(8,128)(2,1)S(1)} %collective-permute-done.21.back_ref), custom_call_target="tpu_custom_call" | custom-call | flops 603979776 | bytes 8388608 | tf_op jit(solution)/shard_map/caption_grad/pallas_call | solution.py:299
  120.3 1.9 %collective-permute-done.22.back_ref = bf16[192,1152]{1,0:T(8,128)(2,1)S(1)} collective-permute-done((bf16[192,1152]{1,0:T(8,128)(2,1)S(1)}, bf16[192,1152]{1,0:T(8,128)(2,1)S(1)}, u32[]{:S(2)}, u32[]{:S(2)}) %collective-permute-start.22) | collective-permute-done | bytes 442400 | tf_op jit(solution)/shard_map/ppermute | solution.py:64
  122.2 2.2 %caption_grad_last.1 = f32[512,1152]{1,0:T(8,128)} custom-call(s32[1]{0:T(128)} %bitcast.2.refs_0_.total_ref, bf16[208,1152]{1,0:T(8,128)(2,1)S(1)} %get-tuple-element.58.raw_ref, f32[208,1152]{1,0:T(8,128)S(1)} %get-tuple-element.59.sums_ref, bf16[192,1152]{1,0:T(8,128)(2,1)S(1)} %collective-permute-done.22.back_ref, ...), custom_call_target="tpu_custom_call", output_to_operand_aliasing={{}: (4, {})} | custom-call | flops 1000000 | bytes 1048576 | tf_op jit(solution)/shard_map/caption_grad_last/pallas_call | solution.py:323
  (56 shorter events, 13.2 us)
Async XLA Ops:
  0.6 27.9 %collective-permute-start.4 = (bf16[512,1152]{1,0:T(8,128)(2,1)}, bf16[512,1152]{1,0:T(8,128)(2,1)S(1)}, u32[]{:S(2)}, u32[]{:S(2)}) collective-permute-start(bf16[512,1152]{1,0:T(8,128)(2,1)} %raw_ref.1), channel_id=1, source_target_pairs={{0,64},{1,65},{2,66},{3,67},{4,68},{5,69},{6,70},{7,71},{8,72},{9,... | collective-permute-start | bytes 3538952 | tf_op jit(solution)/shard_map/ppermute | solution.py:64
  2.4 6.7 %collective-permute-start = (bf16[64,1152]{1,0:T(8,128)(2,1)}, bf16[64,1152]{1,0:T(8,128)(2,1)S(1)}, u32[]{:S(2)}, u32[]{:S(2)}) collective-permute-start(bf16[64,1152]{1,0:T(8,128)(2,1)} %refs_0_.3), channel_id=1, source_target_pairs={{0,65},{1,64},{2,67},{3,66},{4,69},{5,68},{6,71},{7,70},{8,73},{9,... | collective-permute-start | bytes 442376 | tf_op jit(solution)/shard_map/ppermute | solution.py:64
  4.6 0.9 copy-start.2
  9.2 9.0 %collective-permute-start.3 = (bf16[128,1152]{1,0:T(8,128)(2,1)S(1)}, bf16[128,1152]{1,0:T(8,128)(2,1)S(1)}, u32[]{:S(2)}, u32[]{:S(2)}) collective-permute-start(bf16[128,1152]{1,0:T(8,128)(2,1)S(1)} %shard_map.69.refs_0_), channel_id=1, source_target_pairs={{0,32},{1,33},{2,34},{3,35},{4,36},{5,37},{6,38},{7,39},{8,12},{9,... | collective-permute-start | bytes 884744 | tf_op jit(solution)/shard_map/ppermute | solution.py:64
  12.4 8.5 %collective-permute-start.2 = (bf16[128,1152]{1,0:T(8,128)(2,1)S(1)}, bf16[128,1152]{1,0:T(8,128)(2,1)S(1)}, u32[]{:S(2)}, u32[]{:S(2)}) collective-permute-start(bf16[128,1152]{1,0:T(8,128)(2,1)S(1)} %shard_map.69.refs_0_), channel_id=1, source_target_pairs={{0,48},{1,49},{2,50},{3,51},{4,52},{5,53},{6,54},{7,55},{8,14},{9,... | collective-permute-start | bytes 884744 | tf_op jit(solution)/shard_map/ppermute | solution.py:64
  13.5 7.9 %collective-permute-start.1 = (bf16[128,1152]{1,0:T(8,128)(2,1)S(1)}, bf16[128,1152]{1,0:T(8,128)(2,1)S(1)}, u32[]{:S(2)}, u32[]{:S(2)}) collective-permute-start(bf16[128,1152]{1,0:T(8,128)(2,1)S(1)} %shard_map.69.refs_0_), channel_id=1, source_target_pairs={{0,16},{1,17},{2,18},{3,19},{4,20},{5,21},{6,22},{7,23},{8,10},{9,... | collective-permute-start | bytes 884744 | tf_op jit(solution)/shard_map/ppermute | solution.py:64
  15.8 1.3 %copy-start = (bf16[512,1152]{1,0:T(8,128)(2,1)S(1)}, bf16[512,1152]{1,0:T(8,128)(2,1)}, u32[]{:S(2)}) copy-start(bf16[512,1152]{1,0:T(8,128)(2,1)} %raw_ref.1) | copy-start | bytes 3538948
  21.5 23.8 %copy-start.4 = (bf16[256,1152]{1,0:T(8,128)(2,1)}, bf16[256,1152]{1,0:T(8,128)(2,1)S(1)}, u32[]{:S(2)}) copy-start(bf16[256,1152]{1,0:T(8,128)(2,1)S(1)} %get-tuple-element.34.refs_3_) | copy-start | bytes 1769476
  29.8 16.0 %collective-permute-start.5 = (bf16[576,1152]{1,0:T(8,128)(2,1)S(1)}, bf16[576,1152]{1,0:T(8,128)(2,1)S(1)}, u32[]{:S(2)}, u32[]{:S(2)}) collective-permute-start(bf16[576,1152]{1,0:T(8,128)(2,1)S(1)} %shard_map.72.refs_0_), channel_id=1, source_target_pairs={{0,8},{1,9},{2,10},{3,11},{4,12},{5,13},{6,14},{7,15},{8,0},{9,1},... | collective-permute-start | bytes 3981320 | tf_op jit(solution)/shard_map/ppermute | solution.py:64
  29.9 11.7 %collective-permute-start.8 = (bf16[256,1152]{1,0:T(8,128)(2,1)S(1)}, bf16[256,1152]{1,0:T(8,128)(2,1)}, u32[]{:S(2)}, u32[]{:S(2)}) collective-permute-start(bf16[256,1152]{1,0:T(8,128)(2,1)S(1)} %get-tuple-element.34.refs_3_), channel_id=1, source_target_pairs={{0,6},{1,7},{2,0},{3,1},{4,2},{5,3},{6,4},{7,5},{8,56},{9,57},{10,... | collective-permute-start | bytes 1769480 | tf_op jit(solution)/shard_map/ppermute | solution.py:64
  34.2 11.2 %collective-permute-start.6 = (bf16[256,1152]{1,0:T(8,128)(2,1)S(1)}, bf16[256,1152]{1,0:T(8,128)(2,1)}, u32[]{:S(2)}, u32[]{:S(2)}) collective-permute-start(bf16[256,1152]{1,0:T(8,128)(2,1)S(1)} %get-tuple-element.33.refs_3_.refs_2_), channel_id=1, source_target_pairs={{0,2},{1,3},{2,4},{3,5},{4,6},{5,7},{6,0},{7,1},{8,24},{9,25},{10,... | collective-permute-start | bytes 1769480 | tf_op jit(solution)/shard_map/ppermute | solution.py:64
  34.2 14.9 %collective-permute-start.10 = (bf16[256,1152]{1,0:T(8,128)(2,1)S(1)}, bf16[256,1152]{1,0:T(8,128)(2,1)}, u32[]{:S(2)}, u32[]{:S(2)}) collective-permute-start(bf16[256,1152]{1,0:T(8,128)(2,1)S(1)} %get-tuple-element.33.refs_3_.refs_2_), channel_id=1, source_target_pairs={{0,6},{1,7},{2,0},{3,1},{4,2},{5,3},{6,4},{7,5},{8,56},{9,57},{10,... | collective-permute-start | bytes 1769480 | tf_op jit(solution)/shard_map/ppermute | solution.py:64
  41.6 12.7 %collective-permute-start.9 = (bf16[256,1152]{1,0:T(8,128)(2,1)}, bf16[256,1152]{1,0:T(8,128)(2,1)}, u32[]{:S(2)}, u32[]{:S(2)}) collective-permute-start(bf16[256,1152]{1,0:T(8,128)(2,1)} %collective-permute-done.8.refs_3_), channel_id=1, source_target_pairs={{0,6},{1,7},{2,0},{3,1},{4,2},{5,3},{6,4},{7,5},{8,56},{9,57},{10,... | collective-permute-start | bytes 1769480 | tf_op jit(solution)/shard_map/ppermute | solution.py:64
  45.4 11.4 %collective-permute-start.7 = (bf16[256,1152]{1,0:T(8,128)(2,1)}, bf16[256,1152]{1,0:T(8,128)(2,1)}, u32[]{:S(2)}, u32[]{:S(2)}) collective-permute-start(bf16[256,1152]{1,0:T(8,128)(2,1)} %collective-permute-done.6.refs_2_), channel_id=1, source_target_pairs={{0,2},{1,3},{2,4},{3,5},{4,6},{5,7},{6,0},{7,1},{8,24},{9,25},{10,... | collective-permute-start | bytes 1769480 | tf_op jit(solution)/shard_map/ppermute | solution.py:64
  45.5 1.1 copy-start.5
  45.6 18.3 %collective-permute-start.11 = (bf16[256,1152]{1,0:T(8,128)(2,1)}, bf16[256,1152]{1,0:T(8,128)(2,1)S(1)}, u32[]{:S(2)}, u32[]{:S(2)}) collective-permute-start(bf16[256,1152]{1,0:T(8,128)(2,1)} %copy-done.4), channel_id=1, source_target_pairs={{0,2},{1,3},{2,4},{3,5},{4,6},{5,7},{6,0},{7,1},{8,24},{9,25},{10,... | collective-permute-start | bytes 1769480 | tf_op jit(solution)/shard_map/ppermute | solution.py:64
  61.7 10.6 %collective-permute-start.13 = (bf16[256,1152]{1,0:T(8,128)(2,1)S(1)}, bf16[256,1152]{1,0:T(8,128)(2,1)S(1)}, u32[]{:S(2)}, u32[]{:S(2)}) collective-permute-start(bf16[256,1152]{1,0:T(8,128)(2,1)S(1)} %get-tuple-element.49), channel_id=1, source_target_pairs={{0,6},{1,7},{2,0},{3,1},{4,2},{5,3},{6,4},{7,5},{8,56},{9,57},{10,... | collective-permute-start | bytes 1769480 | tf_op jit(solution)/shard_map/ppermute | solution.py:64
  63.0 11.1 %collective-permute-start.12 = (bf16[256,1152]{1,0:T(8,128)(2,1)S(1)}, bf16[256,1152]{1,0:T(8,128)(2,1)S(1)}, u32[]{:S(2)}, u32[]{:S(2)}) collective-permute-start(bf16[256,1152]{1,0:T(8,128)(2,1)S(1)} %get-tuple-element.40.refs_5_), channel_id=1, source_target_pairs={{0,2},{1,3},{2,4},{3,5},{4,6},{5,7},{6,0},{7,1},{8,24},{9,25},{10,... | collective-permute-start | bytes 1769480 | tf_op jit(solution)/shard_map/ppermute | solution.py:64
  72.2 8.5 %collective-permute-start.14 = (bf16[576,1152]{1,0:T(8,128)(2,1)S(1)}, bf16[576,1152]{1,0:T(8,128)(2,1)S(1)}, u32[]{:S(2)}, u32[]{:S(2)}) collective-permute-start(bf16[576,1152]{1,0:T(8,128)(2,1)S(1)} %get-tuple-element.50.refs_6_), channel_id=1, source_target_pairs={{0,8},{1,9},{2,10},{3,11},{4,12},{5,13},{6,14},{7,15},{8,0},{9,1},... | collective-permute-start | bytes 3981320 | tf_op jit(solution)/shard_map/ppermute | solution.py:64
  74.5 17.5 %collective-permute-start.15 = (bf16[512,1152]{1,0:T(8,128)(2,1)S(1)}, bf16[512,1152]{1,0:T(8,128)(2,1)S(1)}, u32[]{:S(2)}, u32[]{:S(2)}) collective-permute-start(bf16[512,1152]{1,0:T(8,128)(2,1)S(1)} %get-tuple-element.55), channel_id=1, source_target_pairs={{0,2},{1,3},{2,4},{3,5},{4,6},{5,7},{6,0},{7,1},{8,24},{9,25},{10,... | collective-permute-start | bytes 3538952 | tf_op jit(solution)/shard_map/ppermute | solution.py:64
  74.5 17.6 %collective-permute-start.16 = (bf16[512,1152]{1,0:T(8,128)(2,1)S(1)}, bf16[512,1152]{1,0:T(8,128)(2,1)S(1)}, u32[]{:S(2)}, u32[]{:S(2)}) collective-permute-start(bf16[512,1152]{1,0:T(8,128)(2,1)S(1)} %get-tuple-element.51.refs_8_), channel_id=1, source_target_pairs={{0,6},{1,7},{2,0},{3,1},{4,2},{5,3},{6,4},{7,5},{8,56},{9,57},{10,... | collective-permute-start | bytes 3538952 | tf_op jit(solution)/shard_map/ppermute | solution.py:64
  92.7 24.5 %copy-start.1 = (bf16[512,1152]{1,0:T(8,128)(2,1)S(1)}, bf16[512,1152]{1,0:T(8,128)(2,1)}, u32[]{:S(2)}) copy-start(bf16[512,1152]{1,0:T(8,128)(2,1)} %raw_ref.1) | copy-start | bytes 3538948
  92.7 7.2 %collective-permute-start.18 = (bf16[128,1152]{1,0:T(8,128)(2,1)S(1)}, bf16[128,1152]{1,0:T(8,128)(2,1)S(1)}, u32[]{:S(2)}, u32[]{:S(2)}) collective-permute-start(bf16[128,1152]{1,0:T(8,128)(2,1)S(1)} %slice.84), channel_id=1, source_target_pairs={{0,48},{1,49},{2,50},{3,51},{4,52},{5,53},{6,54},{7,55},{8,14},{9,... | collective-permute-start | bytes 884744 | tf_op jit(solution)/shard_map/ppermute | solution.py:64
  95.6 11.1 %collective-permute-start.19 = (bf16[128,1152]{1,0:T(8,128)(2,1)S(1)}, bf16[128,1152]{1,0:T(8,128)(2,1)S(1)}, u32[]{:S(2)}, u32[]{:S(2)}) collective-permute-start(bf16[128,1152]{1,0:T(8,128)(2,1)S(1)} %get-tuple-element.68), channel_id=1, source_target_pairs={{0,16},{1,17},{2,18},{3,19},{4,20},{5,21},{6,22},{7,23},{8,10},{9,... | collective-permute-start | bytes 884744 | tf_op jit(solution)/shard_map/ppermute | solution.py:64
  95.6 11.1 %collective-permute-start.17 = (bf16[128,1152]{1,0:T(8,128)(2,1)S(1)}, bf16[128,1152]{1,0:T(8,128)(2,1)S(1)}, u32[]{:S(2)}, u32[]{:S(2)}) collective-permute-start(bf16[128,1152]{1,0:T(8,128)(2,1)S(1)} %get-tuple-element.69), channel_id=1, source_target_pairs={{0,32},{1,33},{2,34},{3,35},{4,36},{5,37},{6,38},{7,39},{8,12},{9,... | collective-permute-start | bytes 884744 | tf_op jit(solution)/shard_map/ppermute | solution.py:64
  97.8 19.4 %collective-permute-start.21 = (bf16[320,1152]{1,0:T(8,128)(2,1)S(1)}, bf16[320,1152]{1,0:T(8,128)(2,1)S(1)}, u32[]{:S(2)}, u32[]{:S(2)}) collective-permute-start(bf16[320,1152]{1,0:T(8,128)(2,1)S(1)} %get-tuple-element.53.refs_2_), channel_id=1, source_target_pairs={{0,64},{1,65},{2,66},{3,67},{4,68},{5,69},{6,70},{7,71},{8,72},{9,... | collective-permute-start | bytes 2211848 | tf_op jit(solution)/shard_map/ppermute | solution.py:64
  99.4 22.8 %collective-permute-start.22 = (bf16[192,1152]{1,0:T(8,128)(2,1)S(1)}, bf16[192,1152]{1,0:T(8,128)(2,1)S(1)}, u32[]{:S(2)}, u32[]{:S(2)}) collective-permute-start(bf16[192,1152]{1,0:T(8,128)(2,1)S(1)} %get-tuple-element.60), channel_id=1, source_target_pairs={{0,64},{1,65},{2,66},{3,67},{4,68},{5,69},{6,70},{7,71},{8,72},{9,... | collective-permute-start | bytes 1327112 | tf_op jit(solution)/shard_map/ppermute | solution.py:64
  106.7 17.7 %collective-permute-start.20 = (bf16[64,1152]{1,0:T(8,128)(2,1)S(1)}, bf16[64,1152]{1,0:T(8,128)(2,1)S(1)}, u32[]{:S(2)}, u32[]{:S(2)}) collective-permute-start(bf16[64,1152]{1,0:T(8,128)(2,1)S(1)} %get-tuple-element.66), channel_id=1, source_target_pairs={{0,65},{1,64},{2,67},{3,66},{4,69},{5,68},{6,71},{7,70},{8,73},{9,... | collective-permute-start | bytes 442376 | tf_op jit(solution)/shard_map/ppermute | solution.py:64
  122.2 2.2 %copy-start.3 = (bf16[64,1152]{1,0:T(8,128)(2,1)S(1)}, bf16[64,1152]{1,0:T(8,128)(2,1)}, u32[]{:S(2)}) copy-start(bf16[64,1152]{1,0:T(8,128)(2,1)} %refs_0_.3) | copy-start | bytes 442372

commit v5 on v4

--- a/solution.py
+++ b/solution.py
@@ -80,12 +80,12 @@
     near_ref[count:] = unit_rows(far_ref[...])[0].astype(BF16)
 
 
-def join_kernel(*refs):
-    rows = refs[0].shape[0]
-    refs[-2][:rows] = refs[0][...]
-    refs[-2][rows:] = refs[1][...]
-    refs[-1][:rows] = refs[2][...]
-    refs[-1][rows:] = refs[3][...]
+def join_kernel(a_ref, b_ref, c_ref, d_ref, head_ref, tail_ref, whole_ref):
+    rows = a_ref.shape[0]
+    for number, ref in enumerate((a_ref, b_ref, c_ref, d_ref)):
+        half_ref = head_ref if number < 2 else tail_ref
+        half_ref[number % 2 * rows : (number % 2 + 1) * rows] = ref[...]
+        whole_ref[number * rows : (number + 1) * rows] = ref[...]
 
 
 def plain(kernel, out_shape, args, flops=10**6, smem=0, limit=16, after=()):
@@ -185,6 +185,10 @@
         ),
         name="block_local" if local else "block_remote",
     )(scalars, spans, head, tail, captions, *after)
+
+
+def local_kernel(scalar_ref, spans_ref, images_ref, captions_ref, weight_ref):
+    weigh(True, scalar_ref, spans_ref, images_ref[...], captions_ref[...], weight_ref)
 
 
 def local_sums_kernel(weight_ref, captions_ref, head_out, tail_out):
@@ -368,8 +372,11 @@
         (total, caption_vectors),
         smem=1,
     )
-    head, tail = plain(
-        join_kernel, (half, half), (near, first[1], first[3], first[2]), after=(own_pad,)
+    head, tail, i_local = plain(
+        join_kernel,
+        (half, half, jax.ShapeDtypeStruct((8 * count, width), BF16)),
+        (near, first[1], first[3], first[2]),
+        after=(own_pad,),
     )
     up_head = send(head, ring_route(1, 1))
     down_tail = send(tail, ring_route(1, 3))
@@ -393,7 +400,14 @@
     def terms(head, tail, types, local=False, after=()):
         return weight_terms(local, types, scalars, spans, head, tail, captions, after)
 
-    w_local, i_local = terms(head, tail, (), True)
+    w_local = plain(
+        local_kernel,
+        jax.ShapeDtypeStruct((8 * count, 2 * pair_rows), BF16),
+        (scalars, spans, i_local, captions),
+        32 * count * pair_rows * width,
+        1,
+        20,
+    )
     w_down, i_down, down_a, down_b = terms(down_head, down_tail, (F32, BF16), after=(w_local,))
     w_two, i_two, two_a, two_b = terms(two_head, two_tail, (BF16, BF16), after=(down_b,))
     over_head = send(two_a, ring_route(1, 1))

time: 126 us -> 127 us (level)
  the two profiles are of different devices: /device:TPU:0 before, /device:TPU:47 now
where the time goes in v5:
time: 127 us
  waiting for transfers between devices  53.4 us (42%)
  Pallas kernels  38 us (30%)
  starting transfers between devices  28.5 us (22%)
  local copies, waits for them, and re-layouts  2.41 us (2%)
  other arithmetic  2.37 us (2%)
  between operations  2.22 us (2%)
    ppermute x23, waiting for transfers between devices, send(): return lax.ppermute(value, AXES, pairs)  53.4 us
    ppermute x23, starting transfers between devices, send(): return lax.ppermute(value, AXES, pairs)  28.5 us
    pallas_call x13, Pallas kernels, plain(): pl.pallas_call(lambda *refs: kernel(*refs[:len(args)], *refs[len(args) +...  18.1 us
    pallas_call x3, Pallas kernels, weight_terms(): pl.pallas_call(lambda *refs: weight_kernel(local, bool(types), *refs[:ari...  14.7 us
    pallas_call x1, Pallas kernels, caption_grads(): pl.pallas_call(functools.partial(home_kernel, last), out_shape=(jax.Shape...  3.1 us
  transfers between devices with their start and end apart: 23, of which 12 were waited for; matrix products, arithmetic and copies ran while one was open for 2% of the time, Pallas kernels for 27%

profile of v5, /device:TPU:47, one launch (start us, length us, event | category | flops | bytes accessed | tf_op | source)
XLA Modules:
  0.0 126.9 jit_solution(6409316412744154801)
XLA Ops:
  0.9 2.1 %collective-permute-start = (bf16[64,1152]{1,0:T(8,128)(2,1)}, bf16[64,1152]{1,0:T(8,128)(2,1)S(1)}, u32[]{:S(2)}, u32[]{:S(2)}) collective-permute-start(bf16[64,1152]{1,0:T(8,128)(2,1)} %refs_0_.3), channel_id=1, source_target_pairs={{0,65},{1,64},{2,67},{3,66},{4,69},{5,68},{6,71},{7,70},{8,73},{9,... | collective-permute-start | bytes 442376 | tf_op jit(solution)/shard_map/ppermute | solution.py:64
  4.1 2.5 %collective-permute-done.refs_1_ = bf16[64,1152]{1,0:T(8,128)(2,1)S(1)} collective-permute-done((bf16[64,1152]{1,0:T(8,128)(2,1)}, bf16[64,1152]{1,0:T(8,128)(2,1)S(1)}, u32[]{:S(2)}, u32[]{:S(2)}) %collective-permute-start) | collective-permute-done | bytes 147488 | tf_op jit(solution)/shard_map/ppermute | solution.py:64
  6.7 2.8 %collective-permute-start.3 = (bf16[128,1152]{1,0:T(8,128)(2,1)S(1)}, bf16[128,1152]{1,0:T(8,128)(2,1)S(1)}, u32[]{:S(2)}, u32[]{:S(2)}) collective-permute-start(bf16[128,1152]{1,0:T(8,128)(2,1)S(1)} %shard_map.69.refs_0_), channel_id=1, source_target_pairs={{0,32},{1,33},{2,34},{3,35},{4,36},{5,37},{6,38},{7,39},{8,12},{9,... | collective-permute-start | bytes 884744 | tf_op jit(solution)/shard_map/ppermute | solution.py:64
  11.0 1.4 %fusion.4 = (s32[]{:T(128)}, s32[64]{0:T(128)S(1)}) fusion(s32[8192]{0:T(1024)} %param.7, s32[]{:T(128)S(6)} %select_n.7), kind=kLoop, calls=%fused_computation.15 | loop fusion | flops 63 | bytes 520 | tf_op jit(solution)/shard_map/reduce_sum | solution.py:356
  12.4 1.3 copy-done
  14.9 2.6 %collective-permute-done.2.refs_2_ = bf16[128,1152]{1,0:T(8,128)(2,1)S(1)} collective-permute-done((bf16[128,1152]{1,0:T(8,128)(2,1)S(1)}, bf16[128,1152]{1,0:T(8,128)(2,1)S(1)}, u32[]{:S(2)}, u32[]{:S(2)}) %collective-permute-start.2) | collective-permute-done | bytes 294944 | tf_op jit(solution)/shard_map/ppermute | solution.py:64
  18.1 9.8 %collective-permute-done.4.refs_2_ = bf16[512,1152]{1,0:T(8,128)(2,1)} collective-permute-done((bf16[512,1152]{1,0:T(8,128)(2,1)}, bf16[512,1152]{1,0:T(8,128)(2,1)}, u32[]{:S(2)}, u32[]{:S(2)}) %collective-permute-start.4) | collective-permute-done | bytes 1179680 | tf_op jit(solution)/shard_map/ppermute | solution.py:64
  27.9 2.5 %shard_map.72.refs_0_ = bf16[576,1152]{1,0:T(8,128)(2,1)S(1)} custom-call(bf16[576,1152]{1,0:T(8,128)(2,1)S(1)} %get-tuple-element.31.refs_4_.refs_0_, bf16[576,512]{1,0:T(8,128)(2,1)S(1)} %get-tuple-element.33.refs_1_, bf16[512,1152]{1,0:T(8,128)(2,1)} %collective-permute-done.4.refs_2_, bf16[256,1152]{1,0:T(8,128)(2,1)S(1)} %get-tuple-element.34.refs_3_), custom_call_target="tpu_custom_call" | custom-call | flops 679477248 | bytes 1048576 | tf_op jit(solution)/shard_map/pallas_call | solution.py:92
  30.4 1.6 %collective-permute-start.5 = (bf16[576,1152]{1,0:T(8,128)(2,1)S(1)}, bf16[576,1152]{1,0:T(8,128)(2,1)}, u32[]{:S(2)}, u32[]{:S(2)}) collective-permute-start(bf16[576,1152]{1,0:T(8,128)(2,1)S(1)} %shard_map.72.refs_0_), channel_id=1, source_target_pairs={{0,8},{1,9},{2,10},{3,11},{4,12},{5,13},{6,14},{7,15},{8,0},{9,1},... | collective-permute-start | bytes 3981320 | tf_op jit(solution)/shard_map/ppermute | solution.py:64
  32.6 2.1 %collective-permute-start.6 = (bf16[256,1152]{1,0:T(8,128)(2,1)S(1)}, bf16[256,1152]{1,0:T(8,128)(2,1)}, u32[]{:S(2)}, u32[]{:S(2)}) collective-permute-start(bf16[256,1152]{1,0:T(8,128)(2,1)S(1)} %get-tuple-element.34.refs_3_), channel_id=1, source_target_pairs={{0,2},{1,3},{2,4},{3,5},{4,6},{5,7},{6,0},{7,1},{8,24},{9,25},{10,... | collective-permute-start | bytes 1769480 | tf_op jit(solution)/shard_map/ppermute | solution.py:64
  36.2 5.9 %collective-permute-done.8.refs_3_ = bf16[256,1152]{1,0:T(8,128)(2,1)} collective-permute-done((bf16[256,1152]{1,0:T(8,128)(2,1)S(1)}, bf16[256,1152]{1,0:T(8,128)(2,1)}, u32[]{:S(2)}, u32[]{:S(2)}) %collective-permute-start.8) | collective-permute-done | bytes 589856 | tf_op jit(solution)/shard_map/ppermute | solution.py:64
  42.1 2.7 %collective-permute-start.7 = (bf16[256,1152]{1,0:T(8,128)(2,1)}, bf16[256,1152]{1,0:T(8,128)(2,1)}, u32[]{:S(2)}, u32[]{:S(2)}) collective-permute-start(bf16[256,1152]{1,0:T(8,128)(2,1)} %collective-permute-done.6.refs_2_), channel_id=1, source_target_pairs={{0,2},{1,3},{2,4},{3,5},{4,6},{5,7},{6,0},{7,1},{8,24},{9,25},{10,... | collective-permute-start | bytes 1769480 | tf_op jit(solution)/shard_map/ppermute | solution.py:64
  45.1 1.5 %shard_map.73.refs_3_.refs_4_.refs_1_ = bf16[1152,1152]{1,0:T(8,128)(2,1)S(1)} custom-call(bf16[576,1152]{1,0:T(8,128)(2,1)S(1)} %shard_map.72.refs_0_, bf16[576,1152]{1,0:T(8,128)(2,1)} %collective-permute-done.5.refs_1_), custom_call_target="tpu_custom_call" | custom-call | flops 1000000 | bytes 1048576 | tf_op jit(solution)/shard_map/pallas_call | solution.py:92
  46.7 2.4 %shard_map.74.refs_5_.refs_0_ = bf16[512,1152]{1,0:T(8,128)(2,1)S(1)} custom-call(f32[2]{0:T(128)S(1)} %pad_maximum_fusion.refs_0_, s32[64,2]{1,0:T(8,128)S(1)} %copy.14.refs_1_, bf16[512,1152]{1,0:T(8,128)(2,1)S(1)} %get-tuple-element.32.refs_2_.refs_4_, bf16[1152,1152]{1,0:T(8,128)(2,1)S(1)} %shard_map.73.refs_3_.refs_4_.refs_1_), custom_call_target="tpu_custom_call" | custom-call | flops 1358954496 | bytes 1048576 | tf_op jit(solution)/shard_map/pallas_call | solution.py:92
  49.1 4.9 %block_remote.3 = (bf16[512,1152]{1,0:T(8,128)(2,1)S(1)}, bf16[512,1152]{1,0:T(8,128)(2,1)S(1)}, f32[256,1152]{1,0:T(8,128)S(1)}, bf16[256,1152]{1,0:T(8,128)(2,1)S(1)}) custom-call(f32[2]{0:T(128)S(1)} %pad_maximum_fusion.refs_0_, s32[64,2]{1,0:T(8,128)S(1)} %copy.14.refs_1_, bf16[256,1152]{1,0:T(8,128)(2,1)} %collective-permute-done.10.refs_2_, ...), custom_call_target="tpu_custom_call" | custom-call | flops 2717908992 | bytes 8388608 | tf_op jit(solution)/shard_map/block_remote/pallas_call | solution.py:169
  54.7 4.9 %block_remote.4 = (bf16[512,1152]{1,0:T(8,128)(2,1)S(1)}, bf16[512,1152]{1,0:T(8,128)(2,1)S(1)}, bf16[256,1152]{1,0:T(8,128)(2,1)S(1)}, bf16[256,1152]{1,0:T(8,128)(2,1)S(1)}) custom-call(f32[2]{0:T(128)S(1)} %pad_maximum_fusion.refs_0_, s32[64,2]{1,0:T(8,128)S(1)} %copy.14.refs_1_, bf16[256,1152]{1,0:T(8,128)(2,1)} %collective-permute-done.7.refs_2_, ...), custom_call_target="tpu_custom_call" | custom-call | flops 2717908992 | bytes 8388608 | tf_op jit(solution)/shard_map/block_remote/pallas_call | solution.py:169
  60.5 1.9 %collective-permute-start.12 = (bf16[256,1152]{1,0:T(8,128)(2,1)S(1)}, bf16[256,1152]{1,0:T(8,128)(2,1)S(1)}, u32[]{:S(2)}, u32[]{:S(2)}) collective-permute-start(bf16[256,1152]{1,0:T(8,128)(2,1)S(1)} %get-tuple-element.39.refs_5_), channel_id=1, source_target_pairs={{0,2},{1,3},{2,4},{3,5},{4,6},{5,7},{6,0},{7,1},{8,24},{9,25},{10,... | collective-permute-start | bytes 1769480 | tf_op jit(solution)/shard_map/ppermute | solution.py:64
  62.4 4.8 %block_remote.5 = (bf16[512,1152]{1,0:T(8,128)(2,1)S(1)}, bf16[512,1152]{1,0:T(8,128)(2,1)S(1)}, bf16[256,1152]{1,0:T(8,128)(2,1)S(1)}, f32[256,1152]{1,0:T(8,128)S(1)}) custom-call(f32[2]{0:T(128)S(1)} %pad_maximum_fusion.refs_0_, s32[64,2]{1,0:T(8,128)S(1)} %copy.14.refs_1_, bf16[256,1152]{1,0:T(8,128)(2,1)} %collective-permute-done.6.refs_2_, ...), custom_call_target="tpu_custom_call" | custom-call | flops 2717908992 | bytes 8388608 | tf_op jit(solution)/shard_map/block_remote/pallas_call | solution.py:169
  67.2 3.6 %shard_map.75 = (bf16[576,1152]{1,0:T(8,128)(2,1)S(1)}, f32[64,1152]{1,0:T(8,128)S(1)}) custom-call(bf16[512,1152]{1,0:T(8,128)(2,1)S(1)} %shard_map.74.refs_5_.refs_0_, bf16[512,1152]{1,0:T(8,128)(2,1)S(1)} %get-tuple-element.37.refs_1_, bf16[512,1152]{1,0:T(8,128)(2,1)S(1)} %get-tuple-element.38.refs_2_, bf16[512,1152]{1,0:T(8,128)(2,1)S(1)} %get-tuple-element.40.refs_3_, ...), custom_call_target="tpu_custom_call" | custom-call | flops 2717908992 | bytes 1048576 | tf_op jit(solution)/shard_map/pallas_call | solution.py:92
  70.8 2.4 %collective-permute-start.14 = (bf16[576,1152]{1,0:T(8,128)(2,1)S(1)}, bf16[576,1152]{1,0:T(8,128)(2,1)S(1)}, u32[]{:S(2)}, u32[]{:S(2)}) collective-permute-start(bf16[576,1152]{1,0:T(8,128)(2,1)S(1)} %get-tuple-element.48.refs_6_), channel_id=1, source_target_pairs={{0,8},{1,9},{2,10},{3,11},{4,12},{5,13},{6,14},{7,15},{8,0},{9,1},... | collective-permute-start | bytes 3981320 | tf_op jit(solution)/shard_map/ppermute | solution.py:64
  75.1 2.9 %shard_map.77.refs_0_ = f32[512,1152]{1,0:T(8,128)S(1)} custom-call(bf16[512,1152]{1,0:T(8,128)(2,1)S(1)} %shard_map.74.refs_5_.refs_0_, bf16[512,1152]{1,0:T(8,128)(2,1)S(1)} %get-tuple-element.37.refs_1_, bf16[512,1152]{1,0:T(8,128)(2,1)S(1)} %get-tuple-element.38.refs_2_, bf16[512,1152]{1,0:T(8,128)(2,1)S(1)} %get-tuple-element.40.refs_3_, ...), custom_call_target="tpu_custom_call" | custom-call | flops 2717908992 | bytes 1048576 | tf_op jit(solution)/shard_map/pallas_call | solution.py:92
  78.4 1.8 %shard_map.79 = (f32[256,1152]{1,0:T(8,128)S(1)}, f32[256,1152]{1,0:T(8,128)S(1)}) custom-call(bf16[512,1152]{1,0:T(8,128)(2,1)S(1)} %shard_map.74.refs_5_.refs_0_, bf16[1152,1152]{1,0:T(8,128)(2,1)S(1)} %shard_map.73.refs_3_.refs_4_.refs_1_, bf16[320,1152]{1,0:T(8,128)(2,1)S(1)} %get-tuple-element.51.refs_2_), custom_call_target="tpu_custom_call" | custom-call | flops 1358954496 | bytes 1048576 | tf_op jit(solution)/shard_map/pallas_call | solution.py:92
  80.2 8.8 %collective-permute-done.15 = bf16[512,1152]{1,0:T(8,128)(2,1)S(1)} collective-permute-done((bf16[512,1152]{1,0:T(8,128)(2,1)S(1)}, bf16[512,1152]{1,0:T(8,128)(2,1)S(1)}, u32[]{:S(2)}, u32[]{:S(2)}) %collective-permute-start.15) | collective-permute-done | bytes 1179680 | tf_op jit(solution)/shard_map/ppermute | solution.py:64
  90.7 1.3 collective-permute-start.18
  92.6 3.4 %collective-permute-start.17 = (bf16[128,1152]{1,0:T(8,128)(2,1)S(1)}, bf16[128,1152]{1,0:T(8,128)(2,1)S(1)}, u32[]{:S(2)}, u32[]{:S(2)}) collective-permute-start(bf16[128,1152]{1,0:T(8,128)(2,1)S(1)} %get-tuple-element.67), channel_id=1, source_target_pairs={{0,32},{1,33},{2,34},{3,35},{4,36},{5,37},{6,38},{7,39},{8,12},{9,... | collective-permute-start | bytes 884744 | tf_op jit(solution)/shard_map/ppermute | solution.py:64
  96.1 1.3 %collective-permute-start.22 = (bf16[192,1152]{1,0:T(8,128)(2,1)S(1)}, bf16[192,1152]{1,0:T(8,128)(2,1)S(1)}, u32[]{:S(2)}, u32[]{:S(2)}) collective-permute-start(bf16[192,1152]{1,0:T(8,128)(2,1)S(1)} %get-tuple-element.58), channel_id=1, source_target_pairs={{0,64},{1,65},{2,66},{3,67},{4,68},{5,69},{6,70},{7,71},{8,72},{9,... | collective-permute-start | bytes 1327112 | tf_op jit(solution)/shard_map/ppermute | solution.py:64
  98.6 2.4 %collective-permute-done.17.refs_2_ = bf16[128,1152]{1,0:T(8,128)(2,1)S(1)} collective-permute-done((bf16[128,1152]{1,0:T(8,128)(2,1)S(1)}, bf16[128,1152]{1,0:T(8,128)(2,1)S(1)}, u32[]{:S(2)}, u32[]{:S(2)}) %collective-permute-start.17) | collective-permute-done | bytes 294944 | tf_op jit(solution)/shard_map/ppermute | solution.py:64
  101.1 1.4 %collective-permute-start.20 = (bf16[64,1152]{1,0:T(8,128)(2,1)S(1)}, bf16[64,1152]{1,0:T(8,128)(2,1)S(1)}, u32[]{:S(2)}, u32[]{:S(2)}) collective-permute-start(bf16[64,1152]{1,0:T(8,128)(2,1)S(1)} %get-tuple-element.64), channel_id=1, source_target_pairs={{0,65},{1,64},{2,67},{3,66},{4,69},{5,68},{6,71},{7,70},{8,73},{9,... | collective-permute-start | bytes 442376 | tf_op jit(solution)/shard_map/ppermute | solution.py:64
  102.5 11.8 %collective-permute-done.21.back_ref = bf16[320,1152]{1,0:T(8,128)(2,1)S(1)} collective-permute-done((bf16[320,1152]{1,0:T(8,128)(2,1)S(1)}, bf16[320,1152]{1,0:T(8,128)(2,1)S(1)}, u32[]{:S(2)}, u32[]{:S(2)}) %collective-permute-start.21) | collective-permute-done | bytes 737312 | tf_op jit(solution)/shard_map/ppermute | solution.py:64
  114.2 3.1 %caption_grad.1 = (f32[512,1152]{1,0:T(8,128)}, bf16[208,1152]{1,0:T(8,128)(2,1)S(1)}, f32[208,1152]{1,0:T(8,128)S(1)}) custom-call(s32[1]{0:T(128)} %bitcast.2.refs_0_.total_ref, bf16[512,1152]{1,0:T(8,128)(2,1)S(1)} %copy-done.1, f32[512,1152]{1,0:T(8,128)S(1)} %get-tuple-element.55.own_ref, bf16[320,1152]{1,0:T(8,128)(2,1)S(1)} %collective-permute-done.21.back_ref), custom_call_target="tpu_custom_call" | custom-call | flops 603979776 | bytes 8388608 | tf_op jit(solution)/shard_map/caption_grad/pallas_call | solution.py:303
  117.3 6.4 %collective-permute-done.22.back_ref = bf16[192,1152]{1,0:T(8,128)(2,1)S(1)} collective-permute-done((bf16[192,1152]{1,0:T(8,128)(2,1)S(1)}, bf16[192,1152]{1,0:T(8,128)(2,1)S(1)}, u32[]{:S(2)}, u32[]{:S(2)}) %collective-permute-start.22) | collective-permute-done | bytes 442400 | tf_op jit(solution)/shard_map/ppermute | solution.py:64
  123.7 2.2 %caption_grad_last.1 = f32[512,1152]{1,0:T(8,128)} custom-call(s32[1]{0:T(128)} %bitcast.2.refs_0_.total_ref, bf16[208,1152]{1,0:T(8,128)(2,1)S(1)} %get-tuple-element.56.raw_ref, f32[208,1152]{1,0:T(8,128)S(1)} %get-tuple-element.57.sums_ref, bf16[192,1152]{1,0:T(8,128)(2,1)S(1)} %collective-permute-done.22.back_ref, ...), custom_call_target="tpu_custom_call", output_to_operand_aliasing={{}: (4, {})} | custom-call | flops 1000000 | bytes 1048576 | tf_op jit(solution)/shard_map/caption_grad_last/pallas_call | solution.py:327
  (54 shorter events, 14.2 us)
Async XLA Ops:
  0.6 27.2 %collective-permute-start.4 = (bf16[512,1152]{1,0:T(8,128)(2,1)}, bf16[512,1152]{1,0:T(8,128)(2,1)}, u32[]{:S(2)}, u32[]{:S(2)}) collective-permute-start(bf16[512,1152]{1,0:T(8,128)(2,1)} %raw_ref.1), channel_id=1, source_target_pairs={{0,64},{1,65},{2,66},{3,67},{4,68},{5,69},{6,70},{7,71},{8,72},{9,... | collective-permute-start | bytes 3538952 | tf_op jit(solution)/shard_map/ppermute | solution.py:64
  0.9 5.7 %collective-permute-start = (bf16[64,1152]{1,0:T(8,128)(2,1)}, bf16[64,1152]{1,0:T(8,128)(2,1)S(1)}, u32[]{:S(2)}, u32[]{:S(2)}) collective-permute-start(bf16[64,1152]{1,0:T(8,128)(2,1)} %refs_0_.3), channel_id=1, source_target_pairs={{0,65},{1,64},{2,67},{3,66},{4,69},{5,68},{6,71},{7,70},{8,73},{9,... | collective-permute-start | bytes 442376 | tf_op jit(solution)/shard_map/ppermute | solution.py:64
  3.0 0.9 copy-start.2
  6.7 8.1 %collective-permute-start.3 = (bf16[128,1152]{1,0:T(8,128)(2,1)S(1)}, bf16[128,1152]{1,0:T(8,128)(2,1)S(1)}, u32[]{:S(2)}, u32[]{:S(2)}) collective-permute-start(bf16[128,1152]{1,0:T(8,128)(2,1)S(1)} %shard_map.69.refs_0_), channel_id=1, source_target_pairs={{0,32},{1,33},{2,34},{3,35},{4,36},{5,37},{6,38},{7,39},{8,12},{9,... | collective-permute-start | bytes 884744 | tf_op jit(solution)/shard_map/ppermute | solution.py:64
  9.5 7.9 %collective-permute-start.2 = (bf16[128,1152]{1,0:T(8,128)(2,1)S(1)}, bf16[128,1152]{1,0:T(8,128)(2,1)S(1)}, u32[]{:S(2)}, u32[]{:S(2)}) collective-permute-start(bf16[128,1152]{1,0:T(8,128)(2,1)S(1)} %shard_map.69.refs_0_), channel_id=1, source_target_pairs={{0,48},{1,49},{2,50},{3,51},{4,52},{5,53},{6,54},{7,55},{8,14},{9,... | collective-permute-start | bytes 884744 | tf_op jit(solution)/shard_map/ppermute | solution.py:64
  10.2 7.7 %collective-permute-start.1 = (bf16[128,1152]{1,0:T(8,128)(2,1)S(1)}, bf16[128,1152]{1,0:T(8,128)(2,1)S(1)}, u32[]{:S(2)}, u32[]{:S(2)}) collective-permute-start(bf16[128,1152]{1,0:T(8,128)(2,1)S(1)} %shard_map.69.refs_0_), channel_id=1, source_target_pairs={{0,16},{1,17},{2,18},{3,19},{4,20},{5,21},{6,22},{7,23},{8,10},{9,... | collective-permute-start | bytes 884744 | tf_op jit(solution)/shard_map/ppermute | solution.py:64
  12.4 1.3 %copy-start = (bf16[512,1152]{1,0:T(8,128)(2,1)S(1)}, bf16[512,1152]{1,0:T(8,128)(2,1)}, u32[]{:S(2)}) copy-start(bf16[512,1152]{1,0:T(8,128)(2,1)} %raw_ref.1) | copy-start | bytes 3538948
  18.1 26.6 %copy-start.4 = (bf16[256,1152]{1,0:T(8,128)(2,1)}, bf16[256,1152]{1,0:T(8,128)(2,1)S(1)}, u32[]{:S(2)}) copy-start(bf16[256,1152]{1,0:T(8,128)(2,1)S(1)} %get-tuple-element.35) | copy-start | bytes 1769476
  30.4 14.7 %collective-permute-start.5 = (bf16[576,1152]{1,0:T(8,128)(2,1)S(1)}, bf16[576,1152]{1,0:T(8,128)(2,1)}, u32[]{:S(2)}, u32[]{:S(2)}) collective-permute-start(bf16[576,1152]{1,0:T(8,128)(2,1)S(1)} %shard_map.72.refs_0_), channel_id=1, source_target_pairs={{0,8},{1,9},{2,10},{3,11},{4,12},{5,13},{6,14},{7,15},{8,0},{9,1},... | collective-permute-start | bytes 3981320 | tf_op jit(solution)/shard_map/ppermute | solution.py:64
  32.0 10.0 %collective-permute-start.8 = (bf16[256,1152]{1,0:T(8,128)(2,1)S(1)}, bf16[256,1152]{1,0:T(8,128)(2,1)}, u32[]{:S(2)}, u32[]{:S(2)}) collective-permute-start(bf16[256,1152]{1,0:T(8,128)(2,1)S(1)} %get-tuple-element.35), channel_id=1, source_target_pairs={{0,6},{1,7},{2,0},{3,1},{4,2},{5,3},{6,4},{7,5},{8,56},{9,57},{10,... | collective-permute-start | bytes 1769480 | tf_op jit(solution)/shard_map/ppermute | solution.py:64
  32.6 9.5 %collective-permute-start.6 = (bf16[256,1152]{1,0:T(8,128)(2,1)S(1)}, bf16[256,1152]{1,0:T(8,128)(2,1)}, u32[]{:S(2)}, u32[]{:S(2)}) collective-permute-start(bf16[256,1152]{1,0:T(8,128)(2,1)S(1)} %get-tuple-element.34.refs_3_), channel_id=1, source_target_pairs={{0,2},{1,3},{2,4},{3,5},{4,6},{5,7},{6,0},{7,1},{8,24},{9,25},{10,... | collective-permute-start | bytes 1769480 | tf_op jit(solution)/shard_map/ppermute | solution.py:64
  34.7 14.4 %collective-permute-start.10 = (bf16[256,1152]{1,0:T(8,128)(2,1)S(1)}, bf16[256,1152]{1,0:T(8,128)(2,1)}, u32[]{:S(2)}, u32[]{:S(2)}) collective-permute-start(bf16[256,1152]{1,0:T(8,128)(2,1)S(1)} %get-tuple-element.34.refs_3_), channel_id=1, source_target_pairs={{0,6},{1,7},{2,0},{3,1},{4,2},{5,3},{6,4},{7,5},{8,56},{9,57},{10,... | collective-permute-start | bytes 1769480 | tf_op jit(solution)/shard_map/ppermute | solution.py:64
  42.1 12.6 %collective-permute-start.9 = (bf16[256,1152]{1,0:T(8,128)(2,1)}, bf16[256,1152]{1,0:T(8,128)(2,1)}, u32[]{:S(2)}, u32[]{:S(2)}) collective-permute-start(bf16[256,1152]{1,0:T(8,128)(2,1)} %collective-permute-done.8.refs_3_), channel_id=1, source_target_pairs={{0,6},{1,7},{2,0},{3,1},{4,2},{5,3},{6,4},{7,5},{8,56},{9,57},{10,... | collective-permute-start | bytes 1769480 | tf_op jit(solution)/shard_map/ppermute | solution.py:64
  42.1 12.6 %collective-permute-start.7 = (bf16[256,1152]{1,0:T(8,128)(2,1)}, bf16[256,1152]{1,0:T(8,128)(2,1)}, u32[]{:S(2)}, u32[]{:S(2)}) collective-permute-start(bf16[256,1152]{1,0:T(8,128)(2,1)} %collective-permute-done.6.refs_2_), channel_id=1, source_target_pairs={{0,2},{1,3},{2,4},{3,5},{4,6},{5,7},{6,0},{7,1},{8,24},{9,25},{10,... | collective-permute-start | bytes 1769480 | tf_op jit(solution)/shard_map/ppermute | solution.py:64
  44.9 17.5 %collective-permute-start.11 = (bf16[256,1152]{1,0:T(8,128)(2,1)}, bf16[256,1152]{1,0:T(8,128)(2,1)S(1)}, u32[]{:S(2)}, u32[]{:S(2)}) collective-permute-start(bf16[256,1152]{1,0:T(8,128)(2,1)} %copy-done.4), channel_id=1, source_target_pairs={{0,2},{1,3},{2,4},{3,5},{4,6},{5,7},{6,0},{7,1},{8,24},{9,25},{10,... | collective-permute-start | bytes 1769480 | tf_op jit(solution)/shard_map/ppermute | solution.py:64
  59.7 13.6 %collective-permute-start.13 = (bf16[256,1152]{1,0:T(8,128)(2,1)S(1)}, bf16[256,1152]{1,0:T(8,128)(2,1)S(1)}, u32[]{:S(2)}, u32[]{:S(2)}) collective-permute-start(bf16[256,1152]{1,0:T(8,128)(2,1)S(1)} %get-tuple-element.47), channel_id=1, source_target_pairs={{0,6},{1,7},{2,0},{3,1},{4,2},{5,3},{6,4},{7,5},{8,56},{9,57},{10,... | collective-permute-start | bytes 1769480 | tf_op jit(solution)/shard_map/ppermute | solution.py:64
  60.5 12.7 %collective-permute-start.12 = (bf16[256,1152]{1,0:T(8,128)(2,1)S(1)}, bf16[256,1152]{1,0:T(8,128)(2,1)S(1)}, u32[]{:S(2)}, u32[]{:S(2)}) collective-permute-start(bf16[256,1152]{1,0:T(8,128)(2,1)S(1)} %get-tuple-element.39.refs_5_), channel_id=1, source_target_pairs={{0,2},{1,3},{2,4},{3,5},{4,6},{5,7},{6,0},{7,1},{8,24},{9,25},{10,... | collective-permute-start | bytes 1769480 | tf_op jit(solution)/shard_map/ppermute | solution.py:64
  70.8 7.2 %collective-permute-start.14 = (bf16[576,1152]{1,0:T(8,128)(2,1)S(1)}, bf16[576,1152]{1,0:T(8,128)(2,1)S(1)}, u32[]{:S(2)}, u32[]{:S(2)}) collective-permute-start(bf16[576,1152]{1,0:T(8,128)(2,1)S(1)} %get-tuple-element.48.refs_6_), channel_id=1, source_target_pairs={{0,8},{1,9},{2,10},{3,11},{4,12},{5,13},{6,14},{7,15},{8,0},{9,1},... | collective-permute-start | bytes 3981320 | tf_op jit(solution)/shard_map/ppermute | solution.py:64
  73.5 15.4 %collective-permute-start.15 = (bf16[512,1152]{1,0:T(8,128)(2,1)S(1)}, bf16[512,1152]{1,0:T(8,128)(2,1)S(1)}, u32[]{:S(2)}, u32[]{:S(2)}) collective-permute-start(bf16[512,1152]{1,0:T(8,128)(2,1)S(1)} %get-tuple-element.53), channel_id=1, source_target_pairs={{0,2},{1,3},{2,4},{3,5},{4,6},{5,7},{6,0},{7,1},{8,24},{9,25},{10,... | collective-permute-start | bytes 3538952 | tf_op jit(solution)/shard_map/ppermute | solution.py:64
  73.8 16.3 %collective-permute-start.16 = (bf16[512,1152]{1,0:T(8,128)(2,1)S(1)}, bf16[512,1152]{1,0:T(8,128)(2,1)S(1)}, u32[]{:S(2)}, u32[]{:S(2)}) collective-permute-start(bf16[512,1152]{1,0:T(8,128)(2,1)S(1)} %get-tuple-element.49.refs_8_), channel_id=1, source_target_pairs={{0,6},{1,7},{2,0},{3,1},{4,2},{5,3},{6,4},{7,5},{8,56},{9,57},{10,... | collective-permute-start | bytes 3538952 | tf_op jit(solution)/shard_map/ppermute | solution.py:64
  90.7 23.6 %copy-start.1 = (bf16[512,1152]{1,0:T(8,128)(2,1)S(1)}, bf16[512,1152]{1,0:T(8,128)(2,1)}, u32[]{:S(2)}) copy-start(bf16[512,1152]{1,0:T(8,128)(2,1)} %raw_ref.1) | copy-start | bytes 3538948
  90.7 6.7 %collective-permute-start.18 = (bf16[128,1152]{1,0:T(8,128)(2,1)S(1)}, bf16[128,1152]{1,0:T(8,128)(2,1)S(1)}, u32[]{:S(2)}, u32[]{:S(2)}) collective-permute-start(bf16[128,1152]{1,0:T(8,128)(2,1)S(1)} %slice.84), channel_id=1, source_target_pairs={{0,48},{1,49},{2,50},{3,51},{4,52},{5,53},{6,54},{7,55},{8,14},{9,... | collective-permute-start | bytes 884744 | tf_op jit(solution)/shard_map/ppermute | solution.py:64
  92.0 6.6 %collective-permute-start.19 = (bf16[128,1152]{1,0:T(8,128)(2,1)S(1)}, bf16[128,1152]{1,0:T(8,128)(2,1)S(1)}, u32[]{:S(2)}, u32[]{:S(2)}) collective-permute-start(bf16[128,1152]{1,0:T(8,128)(2,1)S(1)} %get-tuple-element.66), channel_id=1, source_target_pairs={{0,16},{1,17},{2,18},{3,19},{4,20},{5,21},{6,22},{7,23},{8,10},{9,... | collective-permute-start | bytes 884744 | tf_op jit(solution)/shard_map/ppermute | solution.py:64
  92.6 8.4 %collective-permute-start.17 = (bf16[128,1152]{1,0:T(8,128)(2,1)S(1)}, bf16[128,1152]{1,0:T(8,128)(2,1)S(1)}, u32[]{:S(2)}, u32[]{:S(2)}) collective-permute-start(bf16[128,1152]{1,0:T(8,128)(2,1)S(1)} %get-tuple-element.67), channel_id=1, source_target_pairs={{0,32},{1,33},{2,34},{3,35},{4,36},{5,37},{6,38},{7,39},{8,12},{9,... | collective-permute-start | bytes 884744 | tf_op jit(solution)/shard_map/ppermute | solution.py:64
  96.0 18.3 %collective-permute-start.21 = (bf16[320,1152]{1,0:T(8,128)(2,1)S(1)}, bf16[320,1152]{1,0:T(8,128)(2,1)S(1)}, u32[]{:S(2)}, u32[]{:S(2)}) collective-permute-start(bf16[320,1152]{1,0:T(8,128)(2,1)S(1)} %get-tuple-element.51.refs_2_), channel_id=1, source_target_pairs={{0,64},{1,65},{2,66},{3,67},{4,68},{5,69},{6,70},{7,71},{8,72},{9,... | collective-permute-start | bytes 2211848 | tf_op jit(solution)/shard_map/ppermute | solution.py:64
  96.1 27.6 %collective-permute-start.22 = (bf16[192,1152]{1,0:T(8,128)(2,1)S(1)}, bf16[192,1152]{1,0:T(8,128)(2,1)S(1)}, u32[]{:S(2)}, u32[]{:S(2)}) collective-permute-start(bf16[192,1152]{1,0:T(8,128)(2,1)S(1)} %get-tuple-element.58), channel_id=1, source_target_pairs={{0,64},{1,65},{2,66},{3,67},{4,68},{5,69},{6,70},{7,71},{8,72},{9,... | collective-permute-start | bytes 1327112 | tf_op jit(solution)/shard_map/ppermute | solution.py:64
  101.1 24.8 %collective-permute-start.20 = (bf16[64,1152]{1,0:T(8,128)(2,1)S(1)}, bf16[64,1152]{1,0:T(8,128)(2,1)S(1)}, u32[]{:S(2)}, u32[]{:S(2)}) collective-permute-start(bf16[64,1152]{1,0:T(8,128)(2,1)S(1)} %get-tuple-element.64), channel_id=1, source_target_pairs={{0,65},{1,64},{2,67},{3,66},{4,69},{5,68},{6,71},{7,70},{8,73},{9,... | collective-permute-start | bytes 442376 | tf_op jit(solution)/shard_map/ppermute | solution.py:64
  123.7 2.2 %copy-start.3 = (bf16[64,1152]{1,0:T(8,128)(2,1)S(1)}, bf16[64,1152]{1,0:T(8,128)(2,1)}, u32[]{:S(2)}) copy-start(bf16[64,1152]{1,0:T(8,128)(2,1)} %refs_0_.3) | copy-start | bytes 442372
